TPU v7x, 256 devices: a whole 4x4x8 slice. The times are simulated.
256 devices in a mesh: fine: 32 (over z, x_lo, core), coarse: 8 (over y, x_hi).
Axes of the slice: x: 4 (x_hi: 2, x_lo: 2; x = x_hi * 2 + x_lo), y: 4, z: 8, core: 2. Of those that a mesh axis runs over, the one named last changes fastest.
Arguments:
- start_states: float32 [32, 1, 64, 64, 256], P('fine', None, 'coarse'), may hold values from -6 to 6
- weights: bfloat16 [128, 9, 256, 256], P('fine'), may hold values from -0.125 to 0.125
- biases: float32 [128, 256], P('fine'), may hold values from -3 to 3
- step_sizes: float32 [128], P('fine'), may hold values from 0.1 to 0.4
Outputs:
- corrected: float32 [32, 1, 64, 64, 256], P('fine', None, 'coarse')
- slab_ends: float32 [32, 1, 64, 64, 256], P('fine', None, 'coarse')
All inputs are finite; a program needn't handle non-finite values.
Results may differ from a plain program's by a relative error of at most 0.014.
Values may be sent and summed in bfloat16 or wider, within the bound.
No kernel may reach another device: no remote copies, remote signals or barrier semaphores. Data moves between devices by JAX's collectives and lax.ppermute only.
A program may use at most 64 MiB of HBM per device.

v0:
```python
import jax
import jax.numpy as jnp
from jax import lax
from jax.sharding import PartitionSpec as P


def extended_2(cells, sides, width):
    for axis, dim in sides:
        count = lax.axis_size(axis)
        ends = count - 1
        head = lax.slice_in_dim(cells, 0, width, axis=dim)
        tail = lax.slice_in_dim(cells, cells.shape[dim] - width, cells.shape[dim], axis=dim)
        cells = jnp.concatenate(
            [
                lax.ppermute(tail, axis, [(i, (i + 1) % count) for i in range(ends)]),
                cells,
                lax.ppermute(head, axis, [((i + 1) % count, i) for i in range(ends)]),
            ],
            axis=dim,
        )
    return cells


def from_behind(array, axis, by):
    count = lax.axis_size(axis)
    pairs = [(i, i + by) for i in range(count) if 0 <= i + by < count]
    return lax.ppermute(array, axis, pairs)


def conv_rows(padded, kernel):
    widened = jnp.pad(padded, ((0, 0), (0, 0), (1, 1), (0, 0)))
    row_count = padded.shape[1] - 2
    col_count = padded.shape[2]
    channels = padded.shape[3]
    tap_slices = [
        widened[:, row_shift : row_shift + row_count, col_shift : col_shift + col_count, :]
        for row_shift in range(3)
        for col_shift in range(3)
    ]
    stacked = jnp.concatenate(tap_slices, axis=-1).reshape(-1, 9 * channels)
    product = jnp.dot(
        stacked, kernel.reshape(9 * channels, channels), preferred_element_type=jnp.float32
    )
    return product.reshape(padded.shape[0], row_count, col_count, channels)


def relax(current_state, weights, biases, step_sizes):
    layer_count = weights.shape[0]
    row_count = current_state.shape[1]
    first_slope = jnp.zeros(current_state.shape, jnp.float32)
    extended = extended_2(current_state, (("coarse", 1),), layer_count)
    all_rows = row_count * lax.axis_size("coarse")
    row_start = lax.axis_index("coarse") * row_count
    for layer_index in range(layer_count):
        margin = layer_count - layer_index - 1
        slope_term = jnp.tanh(
            conv_rows(extended.astype(jnp.bfloat16), weights[layer_index]) + biases[layer_index]
        )
        extended = extended[:, 1:-1] + step_sizes[layer_index] * slope_term
        position = row_start - margin + jnp.arange(extended.shape[1], dtype=jnp.int32)
        inside = (position >= 0) & (position < all_rows)
        extended = jnp.where(inside[None, :, None, None], extended, 0.0)
        if layer_index == 0:
            first_slope = slope_term[:, margin : margin + row_count]
    return (extended, first_slope)


def local(start_states, weights, biases, step_sizes):
    initial = start_states[0]
    relaxed, first_slope = relax(initial, weights, biases, step_sizes)
    coarse_step = jnp.sum(step_sizes)
    defect = relaxed - (initial + coarse_step * first_slope)
    slab_index = lax.axis_index("fine")
    slab_count = lax.axis_size("fine")

    def turn(turn_index, carried):
        padded = extended_2(carried.astype(jnp.bfloat16), (("coarse", 1),), 1)
        slope_term = lax.cond(
            slab_index == turn_index,
            lambda: jnp.tanh(conv_rows(padded, weights[0]) + biases[0]),
            lambda: jnp.zeros(carried.shape, jnp.float32),
        )
        advanced = carried + coarse_step * slope_term + defect
        arrived = from_behind(advanced, "fine", 1)
        return jnp.where(slab_index == turn_index + 1, arrived, carried)

    corrected = lax.fori_loop(0, slab_count - 1, turn, initial)
    finished, unused = relax(corrected, weights, biases, step_sizes)
    return (corrected[None], finished[None])


def solution(mesh):
    in_specs = (
        P("fine", None, "coarse", None, None),
        P("fine", None, None, None),
        P("fine", None),
        P("fine"),
    )
    out_specs = (P("fine", None, "coarse", None, None), P("fine", None, "coarse", None, None))
    return jax.shard_map(local, mesh=mesh, in_specs=in_specs, out_specs=out_specs, check_vma=False)
```

profile of v0, /device:TPU:118, one launch (start us, length us, event | category | flops | bytes accessed | tf_op | source)
XLA Modules:
  0.0 833.8 jit_solution(9017527280331028861)
XLA Ops:
  32.2 775.1 %while.13 = (s32[]{:T(128)}, f32[1,8,64,256]{3,2,1,0:T(8,128)S(1)}, s32[]{:T(128)}, f32[]{:T(128)}, bf16[4,9,256,256]{3,2,1,0:T(8,128)(2,1)}, /*index=5*/f32[4,2...) while((s32[]{:T(128)}, f32[1,8,64,256]{3,2,1,0:T(8,128)S(1)}, s32[]{:T(128)}, f32[]{:T(128)}, ...), condition=%wide.region_4.5_spmd, body=%wide.region_1.4_spmd.sunk | while | flops 605093888 | bytes 19139848 | solution.py:87
  45.6 8.6 %collective-permute-done.2 = f32[1,8,64,256]{3,2,1,0:T(8,128)S(1)} collective-permute-done((f32[1,8,64,256]{3,2,1,0:T(8,128)S(1)}, f32[1,8,64,256]{3,2,1,0:T(8,128)S(1)}, u32[]{:S(2)}, u32[]{:S(2)}) %collective-permute-start.2) | collective-permute-done | bytes 524320 | tf_op jit(solution)/shard_map/while/body/eval_jaxpr/ppermute | solution.py:27
  69.8 8.4 %collective-permute-done.2 = f32[1,8,64,256]{3,2,1,0:T(8,128)S(1)} collective-permute-done((f32[1,8,64,256]{3,2,1,0:T(8,128)S(1)}, f32[1,8,64,256]{3,2,1,0:T(8,128)S(1)}, u32[]{:S(2)}, u32[]{:S(2)}) %collective-permute-start.2) | collective-permute-done | bytes 524320 | tf_op jit(solution)/shard_map/while/body/eval_jaxpr/ppermute | solution.py:27
  93.6 6.9 collective-permute-done.2
  113.6 6.3 collective-permute-start.2
  135.9 8.2 collective-permute-start.2
  149.4 5.4 collective-permute-start.1
  157.6 11.1 %collective-permute-start.2 = (f32[1,8,64,256]{3,2,1,0:T(8,128)S(1)}, f32[1,8,64,256]{3,2,1,0:T(8,128)S(1)}, u32[]{:S(2)}, u32[]{:S(2)}) collective-permute-start(f32[1,8,64,256]{3,2,1,0:T(8,128)S(1)} %add_add_fusion.2), channel_id=1, source_target_pairs={{0,8},{8,16},{16,24},{24,32},{32,40},{40,48},{48,56},{56,64},{64,7... | collective-permute-start | bytes 1572872 | tf_op jit(solution)/shard_map/while/body/eval_jaxpr/ppermute | solution.py:27
  170.4 8.5 %collective-permute-start = (bf16[1,1,64,256]{3,2,1,0:T(8,128)(2,1)S(1)}, bf16[1,1,64,256]{3,2,1,0:T(8,128)(2,1)S(1)}, u32[]{:S(2)}, u32[]{:S(2)}) collective-permute-start(bf16[1,1,64,256]{3,2,1,0:T(8,128)(2,1)S(1)} %get-tuple-element.233), channel_id=1, source_target_pairs={{1,0},{2,1},{3,2},{4,3},{5,4},{6,5},{7,6},{9,8},{10,9},{11,10},{12... | collective-permute-start | bytes 98312 | tf_op jit(solution)/shard_map/while/body/eval_jaxpr/ppermute | solution.py:17
  178.8 5.4 collective-permute-start.1
  187.0 9.9 %collective-permute-start.2 = (f32[1,8,64,256]{3,2,1,0:T(8,128)S(1)}, f32[1,8,64,256]{3,2,1,0:T(8,128)S(1)}, u32[]{:S(2)}, u32[]{:S(2)}) collective-permute-start(f32[1,8,64,256]{3,2,1,0:T(8,128)S(1)} %add_add_fusion.2), channel_id=1, source_target_pairs={{0,8},{8,16},{16,24},{24,32},{32,40},{40,48},{48,56},{56,64},{64,7... | collective-permute-start | bytes 1572872 | tf_op jit(solution)/shard_map/while/body/eval_jaxpr/ppermute | solution.py:27
  201.6 5.4 collective-permute-start.1
  209.8 11.5 %collective-permute-start.2 = (f32[1,8,64,256]{3,2,1,0:T(8,128)S(1)}, f32[1,8,64,256]{3,2,1,0:T(8,128)S(1)}, u32[]{:S(2)}, u32[]{:S(2)}) collective-permute-start(f32[1,8,64,256]{3,2,1,0:T(8,128)S(1)} %add_add_fusion.2), channel_id=1, source_target_pairs={{0,8},{8,16},{16,24},{24,32},{32,40},{40,48},{48,56},{56,64},{64,7... | collective-permute-start | bytes 1572872 | tf_op jit(solution)/shard_map/while/body/eval_jaxpr/ppermute | solution.py:27
  224.9 6.3 collective-permute-start.1
  233.7 10.3 %collective-permute-start.2 = (f32[1,8,64,256]{3,2,1,0:T(8,128)S(1)}, f32[1,8,64,256]{3,2,1,0:T(8,128)S(1)}, u32[]{:S(2)}, u32[]{:S(2)}) collective-permute-start(f32[1,8,64,256]{3,2,1,0:T(8,128)S(1)} %add_add_fusion.2), channel_id=1, source_target_pairs={{0,8},{8,16},{16,24},{24,32},{32,40},{40,48},{48,56},{56,64},{64,7... | collective-permute-start | bytes 1572872 | tf_op jit(solution)/shard_map/while/body/eval_jaxpr/ppermute | solution.py:27
  247.6 6.3 collective-permute-start.1
  256.4 10.3 %collective-permute-start.2 = (f32[1,8,64,256]{3,2,1,0:T(8,128)S(1)}, f32[1,8,64,256]{3,2,1,0:T(8,128)S(1)}, u32[]{:S(2)}, u32[]{:S(2)}) collective-permute-start(f32[1,8,64,256]{3,2,1,0:T(8,128)S(1)} %add_add_fusion.2), channel_id=1, source_target_pairs={{0,8},{8,16},{16,24},{24,32},{32,40},{40,48},{48,56},{56,64},{64,7... | collective-permute-start | bytes 1572872 | tf_op jit(solution)/shard_map/while/body/eval_jaxpr/ppermute | solution.py:27
  272.3 5.5 collective-permute-start.1
  277.8 7.0 collective-permute-done.1
  285.7 7.2 collective-permute-start.2
  298.7 7.3 collective-permute-start.1
  315.9 6.0 collective-permute-done.2
  324.0 6.3 collective-permute-start.1
  330.3 5.6 collective-permute-done.1
  341.9 5.6 collective-permute-done.2
  349.7 6.3 collective-permute-start.1
  364.9 5.6 collective-permute-done.2
  379.7 5.6 collective-permute-done.1
  390.7 8.9 %collective-permute-done.2 = f32[1,8,64,256]{3,2,1,0:T(8,128)S(1)} collective-permute-done((f32[1,8,64,256]{3,2,1,0:T(8,128)S(1)}, f32[1,8,64,256]{3,2,1,0:T(8,128)S(1)}, u32[]{:S(2)}, u32[]{:S(2)}) %collective-permute-start.2) | collective-permute-done | bytes 524320 | tf_op jit(solution)/shard_map/while/body/eval_jaxpr/ppermute | solution.py:27
  401.7 6.3 collective-permute-start.1
  417.7 6.4 collective-permute-done.2
  426.2 6.3 collective-permute-start.1
  437.1 8.9 %collective-permute-done.2 = f32[1,8,64,256]{3,2,1,0:T(8,128)S(1)} collective-permute-done((f32[1,8,64,256]{3,2,1,0:T(8,128)S(1)}, f32[1,8,64,256]{3,2,1,0:T(8,128)S(1)}, u32[]{:S(2)}, u32[]{:S(2)}) %collective-permute-start.2) | collective-permute-done | bytes 524320 | tf_op jit(solution)/shard_map/while/body/eval_jaxpr/ppermute | solution.py:27
  465.7 6.2 collective-permute-done.2
  480.4 5.4 collective-permute-done.1
  489.5 8.3 collective-permute-done.2
  500.7 5.6 collective-permute-start.1
  514.5 9.2 %collective-permute-done.2 = f32[1,8,64,256]{3,2,1,0:T(8,128)S(1)} collective-permute-done((f32[1,8,64,256]{3,2,1,0:T(8,128)S(1)}, f32[1,8,64,256]{3,2,1,0:T(8,128)S(1)}, u32[]{:S(2)}, u32[]{:S(2)}) %collective-permute-start.2) | collective-permute-done | bytes 524320 | tf_op jit(solution)/shard_map/while/body/eval_jaxpr/ppermute | solution.py:27
  525.8 6.3 collective-permute-start.1
  540.1 9.1 %collective-permute-done.2 = f32[1,8,64,256]{3,2,1,0:T(8,128)S(1)} collective-permute-done((f32[1,8,64,256]{3,2,1,0:T(8,128)S(1)}, f32[1,8,64,256]{3,2,1,0:T(8,128)S(1)}, u32[]{:S(2)}, u32[]{:S(2)}) %collective-permute-start.2) | collective-permute-done | bytes 524320 | tf_op jit(solution)/shard_map/while/body/eval_jaxpr/ppermute | solution.py:27
  551.3 6.3 collective-permute-start.1
  565.8 9.2 %collective-permute-done.2 = f32[1,8,64,256]{3,2,1,0:T(8,128)S(1)} collective-permute-done((f32[1,8,64,256]{3,2,1,0:T(8,128)S(1)}, f32[1,8,64,256]{3,2,1,0:T(8,128)S(1)}, u32[]{:S(2)}, u32[]{:S(2)}) %collective-permute-start.2) | collective-permute-done | bytes 524320 | tf_op jit(solution)/shard_map/while/body/eval_jaxpr/ppermute | solution.py:27
  577.2 6.3 collective-permute-start.1
  591.4 9.0 %collective-permute-done.2 = f32[1,8,64,256]{3,2,1,0:T(8,128)S(1)} collective-permute-done((f32[1,8,64,256]{3,2,1,0:T(8,128)S(1)}, f32[1,8,64,256]{3,2,1,0:T(8,128)S(1)}, u32[]{:S(2)}, u32[]{:S(2)}) %collective-permute-start.2) | collective-permute-done | bytes 524320 | tf_op jit(solution)/shard_map/while/body/eval_jaxpr/ppermute | solution.py:27
  602.4 6.3 collective-permute-start.1
  608.8 5.7 collective-permute-done
  617.2 8.9 %collective-permute-done.2 = f32[1,8,64,256]{3,2,1,0:T(8,128)S(1)} collective-permute-done((f32[1,8,64,256]{3,2,1,0:T(8,128)S(1)}, f32[1,8,64,256]{3,2,1,0:T(8,128)S(1)}, u32[]{:S(2)}, u32[]{:S(2)}) %collective-permute-start.2) | collective-permute-done | bytes 524320 | tf_op jit(solution)/shard_map/while/body/eval_jaxpr/ppermute | solution.py:27
  628.3 6.3 collective-permute-start.1
  642.3 8.9 %collective-permute-done.2 = f32[1,8,64,256]{3,2,1,0:T(8,128)S(1)} collective-permute-done((f32[1,8,64,256]{3,2,1,0:T(8,128)S(1)}, f32[1,8,64,256]{3,2,1,0:T(8,128)S(1)}, u32[]{:S(2)}, u32[]{:S(2)}) %collective-permute-start.2) | collective-permute-done | bytes 524320 | tf_op jit(solution)/shard_map/while/body/eval_jaxpr/ppermute | solution.py:27
  653.6 6.0 collective-permute-start.1
  659.7 5.6 collective-permute-done
  668.0 8.9 %collective-permute-done.2 = f32[1,8,64,256]{3,2,1,0:T(8,128)S(1)} collective-permute-done((f32[1,8,64,256]{3,2,1,0:T(8,128)S(1)}, f32[1,8,64,256]{3,2,1,0:T(8,128)S(1)}, u32[]{:S(2)}, u32[]{:S(2)}) %collective-permute-start.2) | collective-permute-done | bytes 524320 | tf_op jit(solution)/shard_map/while/body/eval_jaxpr/ppermute | solution.py:27
  679.0 6.3 collective-permute-start.1
  693.1 8.9 %collective-permute-done.2 = f32[1,8,64,256]{3,2,1,0:T(8,128)S(1)} collective-permute-done((f32[1,8,64,256]{3,2,1,0:T(8,128)S(1)}, f32[1,8,64,256]{3,2,1,0:T(8,128)S(1)}, u32[]{:S(2)}, u32[]{:S(2)}) %collective-permute-start.2) | collective-permute-done | bytes 524320 | tf_op jit(solution)/shard_map/while/body/eval_jaxpr/ppermute | solution.py:27
  704.1 6.3 collective-permute-start.1
  710.5 5.6 collective-permute-done
  718.8 8.9 %collective-permute-done.2 = f32[1,8,64,256]{3,2,1,0:T(8,128)S(1)} collective-permute-done((f32[1,8,64,256]{3,2,1,0:T(8,128)S(1)}, f32[1,8,64,256]{3,2,1,0:T(8,128)S(1)}, u32[]{:S(2)}, u32[]{:S(2)}) %collective-permute-start.2) | collective-permute-done | bytes 524320 | tf_op jit(solution)/shard_map/while/body/eval_jaxpr/ppermute | solution.py:27
  729.9 6.3 collective-permute-start.1
  743.9 8.9 %collective-permute-done.2 = f32[1,8,64,256]{3,2,1,0:T(8,128)S(1)} collective-permute-done((f32[1,8,64,256]{3,2,1,0:T(8,128)S(1)}, f32[1,8,64,256]{3,2,1,0:T(8,128)S(1)}, u32[]{:S(2)}, u32[]{:S(2)}) %collective-permute-start.2) | collective-permute-done | bytes 524320 | tf_op jit(solution)/shard_map/while/body/eval_jaxpr/ppermute | solution.py:27
  755.0 6.3 collective-permute-start.1
  761.3 5.6 collective-permute-done
  769.6 8.9 %collective-permute-done.2 = f32[1,8,64,256]{3,2,1,0:T(8,128)S(1)} collective-permute-done((f32[1,8,64,256]{3,2,1,0:T(8,128)S(1)}, f32[1,8,64,256]{3,2,1,0:T(8,128)S(1)}, u32[]{:S(2)}, u32[]{:S(2)}) %collective-permute-start.2) | collective-permute-done | bytes 524320 | tf_op jit(solution)/shard_map/while/body/eval_jaxpr/ppermute | solution.py:27
  780.7 6.3 collective-permute-start.1
  794.7 12.4 %collective-permute-done.2 = f32[1,8,64,256]{3,2,1,0:T(8,128)S(1)} collective-permute-done((f32[1,8,64,256]{3,2,1,0:T(8,128)S(1)}, f32[1,8,64,256]{3,2,1,0:T(8,128)S(1)}, u32[]{:S(2)}, u32[]{:S(2)}) %collective-permute-start.2) | collective-permute-done | bytes 524320 | tf_op jit(solution)/shard_map/while/body/eval_jaxpr/ppermute | solution.py:27
  (494 shorter events, 370.9 us)
Async XLA Ops:
  2.5 13.8 %collective-permute-start.3 = (f32[1,4,64,256]{3,2,1,0:T(8,128)}, f32[1,4,64,256]{3,2,1,0:T(8,128)S(1)}, u32[]{:S(2)}, u32[]{:S(2)}) collective-permute-start(f32[1,4,64,256]{3,2,1,0:T(8,128)} %get-tuple-element.167), channel_id=1, source_target_pairs={{0,1},{1,2},{2,3},{3,4},{4,5},{5,6},{6,7},{8,9},{9,10},{10,11},{11... | collective-permute-start | bytes 786440 | tf_op jit(solution)/shard_map/ppermute | solution.py:15
  6.5 14.0 %collective-permute-start.4 = (f32[1,4,64,256]{3,2,1,0:T(8,128)}, f32[1,4,64,256]{3,2,1,0:T(8,128)S(1)}, u32[]{:S(2)}, u32[]{:S(2)}) collective-permute-start(f32[1,4,64,256]{3,2,1,0:T(8,128)} %get-tuple-element.168), channel_id=1, source_target_pairs={{1,0},{2,1},{3,2},{4,3},{5,4},{6,5},{7,6},{9,8},{10,9},{11,10},{12... | collective-permute-start | bytes 786440 | tf_op jit(solution)/shard_map/ppermute | solution.py:17
  43.7 10.5 %collective-permute-start.2 = (f32[1,8,64,256]{3,2,1,0:T(8,128)S(1)}, f32[1,8,64,256]{3,2,1,0:T(8,128)S(1)}, u32[]{:S(2)}, u32[]{:S(2)}) collective-permute-start(f32[1,8,64,256]{3,2,1,0:T(8,128)S(1)} %add_add_fusion.2), channel_id=1, source_target_pairs={{0,8},{8,16},{16,24},{24,32},{32,40},{40,48},{48,56},{56,64},{64,7... | collective-permute-start | bytes 1572872 | tf_op jit(solution)/shard_map/while/body/eval_jaxpr/ppermute | solution.py:27
  67.7 10.5 %collective-permute-start.2 = (f32[1,8,64,256]{3,2,1,0:T(8,128)S(1)}, f32[1,8,64,256]{3,2,1,0:T(8,128)S(1)}, u32[]{:S(2)}, u32[]{:S(2)}) collective-permute-start(f32[1,8,64,256]{3,2,1,0:T(8,128)S(1)} %add_add_fusion.2), channel_id=1, source_target_pairs={{0,8},{8,16},{16,24},{24,32},{32,40},{40,48},{48,56},{56,64},{64,7... | collective-permute-start | bytes 1572872 | tf_op jit(solution)/shard_map/while/body/eval_jaxpr/ppermute | solution.py:27
  90.0 10.5 %collective-permute-start.2 = (f32[1,8,64,256]{3,2,1,0:T(8,128)S(1)}, f32[1,8,64,256]{3,2,1,0:T(8,128)S(1)}, u32[]{:S(2)}, u32[]{:S(2)}) collective-permute-start(f32[1,8,64,256]{3,2,1,0:T(8,128)S(1)} %add_add_fusion.2), channel_id=1, source_target_pairs={{0,8},{8,16},{16,24},{24,32},{32,40},{40,48},{48,56},{56,64},{64,7... | collective-permute-start | bytes 1572872 | tf_op jit(solution)/shard_map/while/body/eval_jaxpr/ppermute | solution.py:27
  157.6 12.6 %collective-permute-start.2 = (f32[1,8,64,256]{3,2,1,0:T(8,128)S(1)}, f32[1,8,64,256]{3,2,1,0:T(8,128)S(1)}, u32[]{:S(2)}, u32[]{:S(2)}) collective-permute-start(f32[1,8,64,256]{3,2,1,0:T(8,128)S(1)} %add_add_fusion.2), channel_id=1, source_target_pairs={{0,8},{8,16},{16,24},{24,32},{32,40},{40,48},{48,56},{56,64},{64,7... | collective-permute-start | bytes 1572872 | tf_op jit(solution)/shard_map/while/body/eval_jaxpr/ppermute | solution.py:27
  170.4 13.9 %collective-permute-start = (bf16[1,1,64,256]{3,2,1,0:T(8,128)(2,1)S(1)}, bf16[1,1,64,256]{3,2,1,0:T(8,128)(2,1)S(1)}, u32[]{:S(2)}, u32[]{:S(2)}) collective-permute-start(bf16[1,1,64,256]{3,2,1,0:T(8,128)(2,1)S(1)} %get-tuple-element.233), channel_id=1, source_target_pairs={{1,0},{2,1},{3,2},{4,3},{5,4},{6,5},{7,6},{9,8},{10,9},{11,10},{12... | collective-permute-start | bytes 98312 | tf_op jit(solution)/shard_map/while/body/eval_jaxpr/ppermute | solution.py:17
  187.0 11.4 %collective-permute-start.2 = (f32[1,8,64,256]{3,2,1,0:T(8,128)S(1)}, f32[1,8,64,256]{3,2,1,0:T(8,128)S(1)}, u32[]{:S(2)}, u32[]{:S(2)}) collective-permute-start(f32[1,8,64,256]{3,2,1,0:T(8,128)S(1)} %add_add_fusion.2), channel_id=1, source_target_pairs={{0,8},{8,16},{16,24},{24,32},{32,40},{40,48},{48,56},{56,64},{64,7... | collective-permute-start | bytes 1572872 | tf_op jit(solution)/shard_map/while/body/eval_jaxpr/ppermute | solution.py:27
  209.8 13.0 %collective-permute-start.2 = (f32[1,8,64,256]{3,2,1,0:T(8,128)S(1)}, f32[1,8,64,256]{3,2,1,0:T(8,128)S(1)}, u32[]{:S(2)}, u32[]{:S(2)}) collective-permute-start(f32[1,8,64,256]{3,2,1,0:T(8,128)S(1)} %add_add_fusion.2), channel_id=1, source_target_pairs={{0,8},{8,16},{16,24},{24,32},{32,40},{40,48},{48,56},{56,64},{64,7... | collective-permute-start | bytes 1572872 | tf_op jit(solution)/shard_map/while/body/eval_jaxpr/ppermute | solution.py:27
  233.7 11.8 %collective-permute-start.2 = (f32[1,8,64,256]{3,2,1,0:T(8,128)S(1)}, f32[1,8,64,256]{3,2,1,0:T(8,128)S(1)}, u32[]{:S(2)}, u32[]{:S(2)}) collective-permute-start(f32[1,8,64,256]{3,2,1,0:T(8,128)S(1)} %add_add_fusion.2), channel_id=1, source_target_pairs={{0,8},{8,16},{16,24},{24,32},{32,40},{40,48},{48,56},{56,64},{64,7... | collective-permute-start | bytes 1572872 | tf_op jit(solution)/shard_map/while/body/eval_jaxpr/ppermute | solution.py:27
  256.4 11.8 %collective-permute-start.2 = (f32[1,8,64,256]{3,2,1,0:T(8,128)S(1)}, f32[1,8,64,256]{3,2,1,0:T(8,128)S(1)}, u32[]{:S(2)}, u32[]{:S(2)}) collective-permute-start(f32[1,8,64,256]{3,2,1,0:T(8,128)S(1)} %add_add_fusion.2), channel_id=1, source_target_pairs={{0,8},{8,16},{16,24},{24,32},{32,40},{40,48},{48,56},{56,64},{64,7... | collective-permute-start | bytes 1572872 | tf_op jit(solution)/shard_map/while/body/eval_jaxpr/ppermute | solution.py:27
  272.3 12.6 %collective-permute-start.1 = (bf16[1,1,64,256]{3,2,1,0:T(8,128)(2,1)S(1)}, bf16[1,1,64,256]{3,2,1,0:T(8,128)(2,1)S(1)}, u32[]{:S(2)}, u32[]{:S(2)}) collective-permute-start(bf16[1,1,64,256]{3,2,1,0:T(8,128)(2,1)S(1)} %get-tuple-element.234), channel_id=1, source_target_pairs={{0,1},{1,2},{2,3},{3,4},{4,5},{5,6},{6,7},{8,9},{9,10},{10,11},{11... | collective-permute-start | bytes 98312 | tf_op jit(solution)/shard_map/while/body/eval_jaxpr/ppermute | solution.py:15
  285.7 10.9 %collective-permute-start.2 = (f32[1,8,64,256]{3,2,1,0:T(8,128)S(1)}, f32[1,8,64,256]{3,2,1,0:T(8,128)S(1)}, u32[]{:S(2)}, u32[]{:S(2)}) collective-permute-start(f32[1,8,64,256]{3,2,1,0:T(8,128)S(1)} %add_add_fusion.2), channel_id=1, source_target_pairs={{0,8},{8,16},{16,24},{24,32},{32,40},{40,48},{48,56},{56,64},{64,7... | collective-permute-start | bytes 1572872 | tf_op jit(solution)/shard_map/while/body/eval_jaxpr/ppermute | solution.py:27
  298.7 11.4 %collective-permute-start.1 = (bf16[1,1,64,256]{3,2,1,0:T(8,128)(2,1)S(1)}, bf16[1,1,64,256]{3,2,1,0:T(8,128)(2,1)S(1)}, u32[]{:S(2)}, u32[]{:S(2)}) collective-permute-start(bf16[1,1,64,256]{3,2,1,0:T(8,128)(2,1)S(1)} %get-tuple-element.234), channel_id=1, source_target_pairs={{0,1},{1,2},{2,3},{3,4},{4,5},{5,6},{6,7},{8,9},{9,10},{10,11},{11... | collective-permute-start | bytes 98312 | tf_op jit(solution)/shard_map/while/body/eval_jaxpr/ppermute | solution.py:15
  311.0 10.9 %collective-permute-start.2 = (f32[1,8,64,256]{3,2,1,0:T(8,128)S(1)}, f32[1,8,64,256]{3,2,1,0:T(8,128)S(1)}, u32[]{:S(2)}, u32[]{:S(2)}) collective-permute-start(f32[1,8,64,256]{3,2,1,0:T(8,128)S(1)} %add_add_fusion.2), channel_id=1, source_target_pairs={{0,8},{8,16},{16,24},{24,32},{32,40},{40,48},{48,56},{56,64},{64,7... | collective-permute-start | bytes 1572872 | tf_op jit(solution)/shard_map/while/body/eval_jaxpr/ppermute | solution.py:27
  324.0 11.9 %collective-permute-start.1 = (bf16[1,1,64,256]{3,2,1,0:T(8,128)(2,1)S(1)}, bf16[1,1,64,256]{3,2,1,0:T(8,128)(2,1)S(1)}, u32[]{:S(2)}, u32[]{:S(2)}) collective-permute-start(bf16[1,1,64,256]{3,2,1,0:T(8,128)(2,1)S(1)} %get-tuple-element.234), channel_id=1, source_target_pairs={{0,1},{1,2},{2,3},{3,4},{4,5},{5,6},{6,7},{8,9},{9,10},{10,11},{11... | collective-permute-start | bytes 98312 | tf_op jit(solution)/shard_map/while/body/eval_jaxpr/ppermute | solution.py:15
  336.7 10.9 %collective-permute-start.2 = (f32[1,8,64,256]{3,2,1,0:T(8,128)S(1)}, f32[1,8,64,256]{3,2,1,0:T(8,128)S(1)}, u32[]{:S(2)}, u32[]{:S(2)}) collective-permute-start(f32[1,8,64,256]{3,2,1,0:T(8,128)S(1)} %add_add_fusion.2), channel_id=1, source_target_pairs={{0,8},{8,16},{16,24},{24,32},{32,40},{40,48},{48,56},{56,64},{64,7... | collective-permute-start | bytes 1572872 | tf_op jit(solution)/shard_map/while/body/eval_jaxpr/ppermute | solution.py:27
  359.7 10.9 %collective-permute-start.2 = (f32[1,8,64,256]{3,2,1,0:T(8,128)S(1)}, f32[1,8,64,256]{3,2,1,0:T(8,128)S(1)}, u32[]{:S(2)}, u32[]{:S(2)}) collective-permute-start(f32[1,8,64,256]{3,2,1,0:T(8,128)S(1)} %add_add_fusion.2), channel_id=1, source_target_pairs={{0,8},{8,16},{16,24},{24,32},{32,40},{40,48},{48,56},{56,64},{64,7... | collective-permute-start | bytes 1572872 | tf_op jit(solution)/shard_map/while/body/eval_jaxpr/ppermute | solution.py:27
  374.6 10.7 %collective-permute-start.1 = (bf16[1,1,64,256]{3,2,1,0:T(8,128)(2,1)S(1)}, bf16[1,1,64,256]{3,2,1,0:T(8,128)(2,1)S(1)}, u32[]{:S(2)}, u32[]{:S(2)}) collective-permute-start(bf16[1,1,64,256]{3,2,1,0:T(8,128)(2,1)S(1)} %get-tuple-element.234), channel_id=1, source_target_pairs={{0,1},{1,2},{2,3},{3,4},{4,5},{5,6},{6,7},{8,9},{9,10},{10,11},{11... | collective-permute-start | bytes 98312 | tf_op jit(solution)/shard_map/while/body/eval_jaxpr/ppermute | solution.py:15
  388.7 10.9 %collective-permute-start.2 = (f32[1,8,64,256]{3,2,1,0:T(8,128)S(1)}, f32[1,8,64,256]{3,2,1,0:T(8,128)S(1)}, u32[]{:S(2)}, u32[]{:S(2)}) collective-permute-start(f32[1,8,64,256]{3,2,1,0:T(8,128)S(1)} %add_add_fusion.2), channel_id=1, source_target_pairs={{0,8},{8,16},{16,24},{24,32},{32,40},{40,48},{48,56},{56,64},{64,7... | collective-permute-start | bytes 1572872 | tf_op jit(solution)/shard_map/while/body/eval_jaxpr/ppermute | solution.py:27
  399.8 12.7 %collective-permute-start = (bf16[1,1,64,256]{3,2,1,0:T(8,128)(2,1)S(1)}, bf16[1,1,64,256]{3,2,1,0:T(8,128)(2,1)S(1)}, u32[]{:S(2)}, u32[]{:S(2)}) collective-permute-start(bf16[1,1,64,256]{3,2,1,0:T(8,128)(2,1)S(1)} %get-tuple-element.233), channel_id=1, source_target_pairs={{1,0},{2,1},{3,2},{4,3},{5,4},{6,5},{7,6},{9,8},{10,9},{11,10},{12... | collective-permute-start | bytes 98312 | tf_op jit(solution)/shard_map/while/body/eval_jaxpr/ppermute | solution.py:17
  401.7 10.7 %collective-permute-start.1 = (bf16[1,1,64,256]{3,2,1,0:T(8,128)(2,1)S(1)}, bf16[1,1,64,256]{3,2,1,0:T(8,128)(2,1)S(1)}, u32[]{:S(2)}, u32[]{:S(2)}) collective-permute-start(bf16[1,1,64,256]{3,2,1,0:T(8,128)(2,1)S(1)} %get-tuple-element.234), channel_id=1, source_target_pairs={{0,1},{1,2},{2,3},{3,4},{4,5},{5,6},{6,7},{8,9},{9,10},{10,11},{11... | collective-permute-start | bytes 98312 | tf_op jit(solution)/shard_map/while/body/eval_jaxpr/ppermute | solution.py:15
  413.3 10.9 %collective-permute-start.2 = (f32[1,8,64,256]{3,2,1,0:T(8,128)S(1)}, f32[1,8,64,256]{3,2,1,0:T(8,128)S(1)}, u32[]{:S(2)}, u32[]{:S(2)}) collective-permute-start(f32[1,8,64,256]{3,2,1,0:T(8,128)S(1)} %add_add_fusion.2), channel_id=1, source_target_pairs={{0,8},{8,16},{16,24},{24,32},{32,40},{40,48},{48,56},{56,64},{64,7... | collective-permute-start | bytes 1572872 | tf_op jit(solution)/shard_map/while/body/eval_jaxpr/ppermute | solution.py:27
  435.2 10.9 %collective-permute-start.2 = (f32[1,8,64,256]{3,2,1,0:T(8,128)S(1)}, f32[1,8,64,256]{3,2,1,0:T(8,128)S(1)}, u32[]{:S(2)}, u32[]{:S(2)}) collective-permute-start(f32[1,8,64,256]{3,2,1,0:T(8,128)S(1)} %add_add_fusion.2), channel_id=1, source_target_pairs={{0,8},{8,16},{16,24},{24,32},{32,40},{40,48},{48,56},{56,64},{64,7... | collective-permute-start | bytes 1572872 | tf_op jit(solution)/shard_map/while/body/eval_jaxpr/ppermute | solution.py:27
  446.2 11.0 %collective-permute-start = (bf16[1,1,64,256]{3,2,1,0:T(8,128)(2,1)S(1)}, bf16[1,1,64,256]{3,2,1,0:T(8,128)(2,1)S(1)}, u32[]{:S(2)}, u32[]{:S(2)}) collective-permute-start(bf16[1,1,64,256]{3,2,1,0:T(8,128)(2,1)S(1)} %get-tuple-element.233), channel_id=1, source_target_pairs={{1,0},{2,1},{3,2},{4,3},{5,4},{6,5},{7,6},{9,8},{10,9},{11,10},{12... | collective-permute-start | bytes 98312 | tf_op jit(solution)/shard_map/while/body/eval_jaxpr/ppermute | solution.py:17
  460.7 11.2 %collective-permute-start.2 = (f32[1,8,64,256]{3,2,1,0:T(8,128)S(1)}, f32[1,8,64,256]{3,2,1,0:T(8,128)S(1)}, u32[]{:S(2)}, u32[]{:S(2)}) collective-permute-start(f32[1,8,64,256]{3,2,1,0:T(8,128)S(1)} %add_add_fusion.2), channel_id=1, source_target_pairs={{0,8},{8,16},{16,24},{24,32},{32,40},{40,48},{48,56},{56,64},{64,7... | collective-permute-start | bytes 1572872 | tf_op jit(solution)/shard_map/while/body/eval_jaxpr/ppermute | solution.py:27
  486.6 11.2 %collective-permute-start.2 = (f32[1,8,64,256]{3,2,1,0:T(8,128)S(1)}, f32[1,8,64,256]{3,2,1,0:T(8,128)S(1)}, u32[]{:S(2)}, u32[]{:S(2)}) collective-permute-start(f32[1,8,64,256]{3,2,1,0:T(8,128)S(1)} %add_add_fusion.2), channel_id=1, source_target_pairs={{0,8},{8,16},{16,24},{24,32},{32,40},{40,48},{48,56},{56,64},{64,7... | collective-permute-start | bytes 1572872 | tf_op jit(solution)/shard_map/while/body/eval_jaxpr/ppermute | solution.py:27
  498.0 13.6 %collective-permute-start = (bf16[1,1,64,256]{3,2,1,0:T(8,128)(2,1)S(1)}, bf16[1,1,64,256]{3,2,1,0:T(8,128)(2,1)S(1)}, u32[]{:S(2)}, u32[]{:S(2)}) collective-permute-start(bf16[1,1,64,256]{3,2,1,0:T(8,128)(2,1)S(1)} %get-tuple-element.233), channel_id=1, source_target_pairs={{1,0},{2,1},{3,2},{4,3},{5,4},{6,5},{7,6},{9,8},{10,9},{11,10},{12... | collective-permute-start | bytes 98312 | tf_op jit(solution)/shard_map/while/body/eval_jaxpr/ppermute | solution.py:17
  500.7 10.9 %collective-permute-start.1 = (bf16[1,1,64,256]{3,2,1,0:T(8,128)(2,1)S(1)}, bf16[1,1,64,256]{3,2,1,0:T(8,128)(2,1)S(1)}, u32[]{:S(2)}, u32[]{:S(2)}) collective-permute-start(bf16[1,1,64,256]{3,2,1,0:T(8,128)(2,1)S(1)} %get-tuple-element.234), channel_id=1, source_target_pairs={{0,1},{1,2},{2,3},{3,4},{4,5},{5,6},{6,7},{8,9},{9,10},{10,11},{11... | collective-permute-start | bytes 98312 | tf_op jit(solution)/shard_map/while/body/eval_jaxpr/ppermute | solution.py:15
  512.4 11.2 %collective-permute-start.2 = (f32[1,8,64,256]{3,2,1,0:T(8,128)S(1)}, f32[1,8,64,256]{3,2,1,0:T(8,128)S(1)}, u32[]{:S(2)}, u32[]{:S(2)}) collective-permute-start(f32[1,8,64,256]{3,2,1,0:T(8,128)S(1)} %add_add_fusion.2), channel_id=1, source_target_pairs={{0,8},{8,16},{16,24},{24,32},{32,40},{40,48},{48,56},{56,64},{64,7... | collective-permute-start | bytes 1572872 | tf_op jit(solution)/shard_map/while/body/eval_jaxpr/ppermute | solution.py:27
  523.8 13.5 %collective-permute-start = (bf16[1,1,64,256]{3,2,1,0:T(8,128)(2,1)S(1)}, bf16[1,1,64,256]{3,2,1,0:T(8,128)(2,1)S(1)}, u32[]{:S(2)}, u32[]{:S(2)}) collective-permute-start(bf16[1,1,64,256]{3,2,1,0:T(8,128)(2,1)S(1)} %get-tuple-element.233), channel_id=1, source_target_pairs={{1,0},{2,1},{3,2},{4,3},{5,4},{6,5},{7,6},{9,8},{10,9},{11,10},{12... | collective-permute-start | bytes 98312 | tf_op jit(solution)/shard_map/while/body/eval_jaxpr/ppermute | solution.py:17
  525.8 11.5 %collective-permute-start.1 = (bf16[1,1,64,256]{3,2,1,0:T(8,128)(2,1)S(1)}, bf16[1,1,64,256]{3,2,1,0:T(8,128)(2,1)S(1)}, u32[]{:S(2)}, u32[]{:S(2)}) collective-permute-start(bf16[1,1,64,256]{3,2,1,0:T(8,128)(2,1)S(1)} %get-tuple-element.234), channel_id=1, source_target_pairs={{0,1},{1,2},{2,3},{3,4},{4,5},{5,6},{6,7},{8,9},{9,10},{10,11},{11... | collective-permute-start | bytes 98312 | tf_op jit(solution)/shard_map/while/body/eval_jaxpr/ppermute | solution.py:15
  538.2 11.0 %collective-permute-start.2 = (f32[1,8,64,256]{3,2,1,0:T(8,128)S(1)}, f32[1,8,64,256]{3,2,1,0:T(8,128)S(1)}, u32[]{:S(2)}, u32[]{:S(2)}) collective-permute-start(f32[1,8,64,256]{3,2,1,0:T(8,128)S(1)} %add_add_fusion.2), channel_id=1, source_target_pairs={{0,8},{8,16},{16,24},{24,32},{32,40},{40,48},{48,56},{56,64},{64,7... | collective-permute-start | bytes 1572872 | tf_op jit(solution)/shard_map/while/body/eval_jaxpr/ppermute | solution.py:27
  549.4 13.6 %collective-permute-start = (bf16[1,1,64,256]{3,2,1,0:T(8,128)(2,1)S(1)}, bf16[1,1,64,256]{3,2,1,0:T(8,128)(2,1)S(1)}, u32[]{:S(2)}, u32[]{:S(2)}) collective-permute-start(bf16[1,1,64,256]{3,2,1,0:T(8,128)(2,1)S(1)} %get-tuple-element.233), channel_id=1, source_target_pairs={{1,0},{2,1},{3,2},{4,3},{5,4},{6,5},{7,6},{9,8},{10,9},{11,10},{12... | collective-permute-start | bytes 98312 | tf_op jit(solution)/shard_map/while/body/eval_jaxpr/ppermute | solution.py:17
  551.3 11.7 %collective-permute-start.1 = (bf16[1,1,64,256]{3,2,1,0:T(8,128)(2,1)S(1)}, bf16[1,1,64,256]{3,2,1,0:T(8,128)(2,1)S(1)}, u32[]{:S(2)}, u32[]{:S(2)}) collective-permute-start(bf16[1,1,64,256]{3,2,1,0:T(8,128)(2,1)S(1)} %get-tuple-element.234), channel_id=1, source_target_pairs={{0,1},{1,2},{2,3},{3,4},{4,5},{5,6},{6,7},{8,9},{9,10},{10,11},{11... | collective-permute-start | bytes 98312 | tf_op jit(solution)/shard_map/while/body/eval_jaxpr/ppermute | solution.py:15
  563.9 11.2 %collective-permute-start.2 = (f32[1,8,64,256]{3,2,1,0:T(8,128)S(1)}, f32[1,8,64,256]{3,2,1,0:T(8,128)S(1)}, u32[]{:S(2)}, u32[]{:S(2)}) collective-permute-start(f32[1,8,64,256]{3,2,1,0:T(8,128)S(1)} %add_add_fusion.2), channel_id=1, source_target_pairs={{0,8},{8,16},{16,24},{24,32},{32,40},{40,48},{48,56},{56,64},{64,7... | collective-permute-start | bytes 1572872 | tf_op jit(solution)/shard_map/while/body/eval_jaxpr/ppermute | solution.py:27
  575.2 13.3 %collective-permute-start = (bf16[1,1,64,256]{3,2,1,0:T(8,128)(2,1)S(1)}, bf16[1,1,64,256]{3,2,1,0:T(8,128)(2,1)S(1)}, u32[]{:S(2)}, u32[]{:S(2)}) collective-permute-start(bf16[1,1,64,256]{3,2,1,0:T(8,128)(2,1)S(1)} %get-tuple-element.233), channel_id=1, source_target_pairs={{1,0},{2,1},{3,2},{4,3},{5,4},{6,5},{7,6},{9,8},{10,9},{11,10},{12... | collective-permute-start | bytes 98312 | tf_op jit(solution)/shard_map/while/body/eval_jaxpr/ppermute | solution.py:17
  577.2 11.4 %collective-permute-start.1 = (bf16[1,1,64,256]{3,2,1,0:T(8,128)(2,1)S(1)}, bf16[1,1,64,256]{3,2,1,0:T(8,128)(2,1)S(1)}, u32[]{:S(2)}, u32[]{:S(2)}) collective-permute-start(bf16[1,1,64,256]{3,2,1,0:T(8,128)(2,1)S(1)} %get-tuple-element.234), channel_id=1, source_target_pairs={{0,1},{1,2},{2,3},{3,4},{4,5},{5,6},{6,7},{8,9},{9,10},{10,11},{11... | collective-permute-start | bytes 98312 | tf_op jit(solution)/shard_map/while/body/eval_jaxpr/ppermute | solution.py:15
  589.4 10.9 %collective-permute-start.2 = (f32[1,8,64,256]{3,2,1,0:T(8,128)S(1)}, f32[1,8,64,256]{3,2,1,0:T(8,128)S(1)}, u32[]{:S(2)}, u32[]{:S(2)}) collective-permute-start(f32[1,8,64,256]{3,2,1,0:T(8,128)S(1)} %add_add_fusion.2), channel_id=1, source_target_pairs={{0,8},{8,16},{16,24},{24,32},{32,40},{40,48},{48,56},{56,64},{64,7... | collective-permute-start | bytes 1572872 | tf_op jit(solution)/shard_map/while/body/eval_jaxpr/ppermute | solution.py:27
  600.5 13.9 %collective-permute-start = (bf16[1,1,64,256]{3,2,1,0:T(8,128)(2,1)S(1)}, bf16[1,1,64,256]{3,2,1,0:T(8,128)(2,1)S(1)}, u32[]{:S(2)}, u32[]{:S(2)}) collective-permute-start(bf16[1,1,64,256]{3,2,1,0:T(8,128)(2,1)S(1)} %get-tuple-element.233), channel_id=1, source_target_pairs={{1,0},{2,1},{3,2},{4,3},{5,4},{6,5},{7,6},{9,8},{10,9},{11,10},{12... | collective-permute-start | bytes 98312 | tf_op jit(solution)/shard_map/while/body/eval_jaxpr/ppermute | solution.py:17
  602.4 12.0 %collective-permute-start.1 = (bf16[1,1,64,256]{3,2,1,0:T(8,128)(2,1)S(1)}, bf16[1,1,64,256]{3,2,1,0:T(8,128)(2,1)S(1)}, u32[]{:S(2)}, u32[]{:S(2)}) collective-permute-start(bf16[1,1,64,256]{3,2,1,0:T(8,128)(2,1)S(1)} %get-tuple-element.234), channel_id=1, source_target_pairs={{0,1},{1,2},{2,3},{3,4},{4,5},{5,6},{6,7},{8,9},{9,10},{10,11},{11... | collective-permute-start | bytes 98312 | tf_op jit(solution)/shard_map/while/body/eval_jaxpr/ppermute | solution.py:15
  615.3 10.9 %collective-permute-start.2 = (f32[1,8,64,256]{3,2,1,0:T(8,128)S(1)}, f32[1,8,64,256]{3,2,1,0:T(8,128)S(1)}, u32[]{:S(2)}, u32[]{:S(2)}) collective-permute-start(f32[1,8,64,256]{3,2,1,0:T(8,128)S(1)} %add_add_fusion.2), channel_id=1, source_target_pairs={{0,8},{8,16},{16,24},{24,32},{32,40},{40,48},{48,56},{56,64},{64,7... | collective-permute-start | bytes 1572872 | tf_op jit(solution)/shard_map/while/body/eval_jaxpr/ppermute | solution.py:27
  626.4 13.1 %collective-permute-start = (bf16[1,1,64,256]{3,2,1,0:T(8,128)(2,1)S(1)}, bf16[1,1,64,256]{3,2,1,0:T(8,128)(2,1)S(1)}, u32[]{:S(2)}, u32[]{:S(2)}) collective-permute-start(bf16[1,1,64,256]{3,2,1,0:T(8,128)(2,1)S(1)} %get-tuple-element.233), channel_id=1, source_target_pairs={{1,0},{2,1},{3,2},{4,3},{5,4},{6,5},{7,6},{9,8},{10,9},{11,10},{12... | collective-permute-start | bytes 98312 | tf_op jit(solution)/shard_map/while/body/eval_jaxpr/ppermute | solution.py:17
  628.3 11.2 %collective-permute-start.1 = (bf16[1,1,64,256]{3,2,1,0:T(8,128)(2,1)S(1)}, bf16[1,1,64,256]{3,2,1,0:T(8,128)(2,1)S(1)}, u32[]{:S(2)}, u32[]{:S(2)}) collective-permute-start(bf16[1,1,64,256]{3,2,1,0:T(8,128)(2,1)S(1)} %get-tuple-element.234), channel_id=1, source_target_pairs={{0,1},{1,2},{2,3},{3,4},{4,5},{5,6},{6,7},{8,9},{9,10},{10,11},{11... | collective-permute-start | bytes 98312 | tf_op jit(solution)/shard_map/while/body/eval_jaxpr/ppermute | solution.py:15
  640.3 10.9 %collective-permute-start.2 = (f32[1,8,64,256]{3,2,1,0:T(8,128)S(1)}, f32[1,8,64,256]{3,2,1,0:T(8,128)S(1)}, u32[]{:S(2)}, u32[]{:S(2)}) collective-permute-start(f32[1,8,64,256]{3,2,1,0:T(8,128)S(1)} %add_add_fusion.2), channel_id=1, source_target_pairs={{0,8},{8,16},{16,24},{24,32},{32,40},{40,48},{48,56},{56,64},{64,7... | collective-permute-start | bytes 1572872 | tf_op jit(solution)/shard_map/while/body/eval_jaxpr/ppermute | solution.py:27
  651.4 13.8 %collective-permute-start = (bf16[1,1,64,256]{3,2,1,0:T(8,128)(2,1)S(1)}, bf16[1,1,64,256]{3,2,1,0:T(8,128)(2,1)S(1)}, u32[]{:S(2)}, u32[]{:S(2)}) collective-permute-start(bf16[1,1,64,256]{3,2,1,0:T(8,128)(2,1)S(1)} %get-tuple-element.233), channel_id=1, source_target_pairs={{1,0},{2,1},{3,2},{4,3},{5,4},{6,5},{7,6},{9,8},{10,9},{11,10},{12... | collective-permute-start | bytes 98312 | tf_op jit(solution)/shard_map/while/body/eval_jaxpr/ppermute | solution.py:17
  653.6 11.6 %collective-permute-start.1 = (bf16[1,1,64,256]{3,2,1,0:T(8,128)(2,1)S(1)}, bf16[1,1,64,256]{3,2,1,0:T(8,128)(2,1)S(1)}, u32[]{:S(2)}, u32[]{:S(2)}) collective-permute-start(bf16[1,1,64,256]{3,2,1,0:T(8,128)(2,1)S(1)} %get-tuple-element.234), channel_id=1, source_target_pairs={{0,1},{1,2},{2,3},{3,4},{4,5},{5,6},{6,7},{8,9},{9,10},{10,11},{11... | collective-permute-start | bytes 98312 | tf_op jit(solution)/shard_map/while/body/eval_jaxpr/ppermute | solution.py:15
  666.1 10.9 %collective-permute-start.2 = (f32[1,8,64,256]{3,2,1,0:T(8,128)S(1)}, f32[1,8,64,256]{3,2,1,0:T(8,128)S(1)}, u32[]{:S(2)}, u32[]{:S(2)}) collective-permute-start(f32[1,8,64,256]{3,2,1,0:T(8,128)S(1)} %add_add_fusion.2), channel_id=1, source_target_pairs={{0,8},{8,16},{16,24},{24,32},{32,40},{40,48},{48,56},{56,64},{64,7... | collective-permute-start | bytes 1572872 | tf_op jit(solution)/shard_map/while/body/eval_jaxpr/ppermute | solution.py:27
  677.1 13.2 %collective-permute-start = (bf16[1,1,64,256]{3,2,1,0:T(8,128)(2,1)S(1)}, bf16[1,1,64,256]{3,2,1,0:T(8,128)(2,1)S(1)}, u32[]{:S(2)}, u32[]{:S(2)}) collective-permute-start(bf16[1,1,64,256]{3,2,1,0:T(8,128)(2,1)S(1)} %get-tuple-element.233), channel_id=1, source_target_pairs={{1,0},{2,1},{3,2},{4,3},{5,4},{6,5},{7,6},{9,8},{10,9},{11,10},{12... | collective-permute-start | bytes 98312 | tf_op jit(solution)/shard_map/while/body/eval_jaxpr/ppermute | solution.py:17
  679.0 11.3 %collective-permute-start.1 = (bf16[1,1,64,256]{3,2,1,0:T(8,128)(2,1)S(1)}, bf16[1,1,64,256]{3,2,1,0:T(8,128)(2,1)S(1)}, u32[]{:S(2)}, u32[]{:S(2)}) collective-permute-start(bf16[1,1,64,256]{3,2,1,0:T(8,128)(2,1)S(1)} %get-tuple-element.234), channel_id=1, source_target_pairs={{0,1},{1,2},{2,3},{3,4},{4,5},{5,6},{6,7},{8,9},{9,10},{10,11},{11... | collective-permute-start | bytes 98312 | tf_op jit(solution)/shard_map/while/body/eval_jaxpr/ppermute | solution.py:15
  691.2 10.9 %collective-permute-start.2 = (f32[1,8,64,256]{3,2,1,0:T(8,128)S(1)}, f32[1,8,64,256]{3,2,1,0:T(8,128)S(1)}, u32[]{:S(2)}, u32[]{:S(2)}) collective-permute-start(f32[1,8,64,256]{3,2,1,0:T(8,128)S(1)} %add_add_fusion.2), channel_id=1, source_target_pairs={{0,8},{8,16},{16,24},{24,32},{32,40},{40,48},{48,56},{56,64},{64,7... | collective-permute-start | bytes 1572872 | tf_op jit(solution)/shard_map/while/body/eval_jaxpr/ppermute | solution.py:27
  702.2 13.8 %collective-permute-start = (bf16[1,1,64,256]{3,2,1,0:T(8,128)(2,1)S(1)}, bf16[1,1,64,256]{3,2,1,0:T(8,128)(2,1)S(1)}, u32[]{:S(2)}, u32[]{:S(2)}) collective-permute-start(bf16[1,1,64,256]{3,2,1,0:T(8,128)(2,1)S(1)} %get-tuple-element.233), channel_id=1, source_target_pairs={{1,0},{2,1},{3,2},{4,3},{5,4},{6,5},{7,6},{9,8},{10,9},{11,10},{12... | collective-permute-start | bytes 98312 | tf_op jit(solution)/shard_map/while/body/eval_jaxpr/ppermute | solution.py:17
  704.1 11.9 %collective-permute-start.1 = (bf16[1,1,64,256]{3,2,1,0:T(8,128)(2,1)S(1)}, bf16[1,1,64,256]{3,2,1,0:T(8,128)(2,1)S(1)}, u32[]{:S(2)}, u32[]{:S(2)}) collective-permute-start(bf16[1,1,64,256]{3,2,1,0:T(8,128)(2,1)S(1)} %get-tuple-element.234), channel_id=1, source_target_pairs={{0,1},{1,2},{2,3},{3,4},{4,5},{5,6},{6,7},{8,9},{9,10},{10,11},{11... | collective-permute-start | bytes 98312 | tf_op jit(solution)/shard_map/while/body/eval_jaxpr/ppermute | solution.py:15
  716.9 10.9 %collective-permute-start.2 = (f32[1,8,64,256]{3,2,1,0:T(8,128)S(1)}, f32[1,8,64,256]{3,2,1,0:T(8,128)S(1)}, u32[]{:S(2)}, u32[]{:S(2)}) collective-permute-start(f32[1,8,64,256]{3,2,1,0:T(8,128)S(1)} %add_add_fusion.2), channel_id=1, source_target_pairs={{0,8},{8,16},{16,24},{24,32},{32,40},{40,48},{48,56},{56,64},{64,7... | collective-permute-start | bytes 1572872 | tf_op jit(solution)/shard_map/while/body/eval_jaxpr/ppermute | solution.py:27
  727.9 13.2 %collective-permute-start = (bf16[1,1,64,256]{3,2,1,0:T(8,128)(2,1)S(1)}, bf16[1,1,64,256]{3,2,1,0:T(8,128)(2,1)S(1)}, u32[]{:S(2)}, u32[]{:S(2)}) collective-permute-start(bf16[1,1,64,256]{3,2,1,0:T(8,128)(2,1)S(1)} %get-tuple-element.233), channel_id=1, source_target_pairs={{1,0},{2,1},{3,2},{4,3},{5,4},{6,5},{7,6},{9,8},{10,9},{11,10},{12... | collective-permute-start | bytes 98312 | tf_op jit(solution)/shard_map/while/body/eval_jaxpr/ppermute | solution.py:17
  729.9 11.3 %collective-permute-start.1 = (bf16[1,1,64,256]{3,2,1,0:T(8,128)(2,1)S(1)}, bf16[1,1,64,256]{3,2,1,0:T(8,128)(2,1)S(1)}, u32[]{:S(2)}, u32[]{:S(2)}) collective-permute-start(bf16[1,1,64,256]{3,2,1,0:T(8,128)(2,1)S(1)} %get-tuple-element.234), channel_id=1, source_target_pairs={{0,1},{1,2},{2,3},{3,4},{4,5},{5,6},{6,7},{8,9},{9,10},{10,11},{11... | collective-permute-start | bytes 98312 | tf_op jit(solution)/shard_map/while/body/eval_jaxpr/ppermute | solution.py:15
  742.0 10.9 %collective-permute-start.2 = (f32[1,8,64,256]{3,2,1,0:T(8,128)S(1)}, f32[1,8,64,256]{3,2,1,0:T(8,128)S(1)}, u32[]{:S(2)}, u32[]{:S(2)}) collective-permute-start(f32[1,8,64,256]{3,2,1,0:T(8,128)S(1)} %add_add_fusion.2), channel_id=1, source_target_pairs={{0,8},{8,16},{16,24},{24,32},{32,40},{40,48},{48,56},{56,64},{64,7... | collective-permute-start | bytes 1572872 | tf_op jit(solution)/shard_map/while/body/eval_jaxpr/ppermute | solution.py:27
  753.0 13.8 %collective-permute-start = (bf16[1,1,64,256]{3,2,1,0:T(8,128)(2,1)S(1)}, bf16[1,1,64,256]{3,2,1,0:T(8,128)(2,1)S(1)}, u32[]{:S(2)}, u32[]{:S(2)}) collective-permute-start(bf16[1,1,64,256]{3,2,1,0:T(8,128)(2,1)S(1)} %get-tuple-element.233), channel_id=1, source_target_pairs={{1,0},{2,1},{3,2},{4,3},{5,4},{6,5},{7,6},{9,8},{10,9},{11,10},{12... | collective-permute-start | bytes 98312 | tf_op jit(solution)/shard_map/while/body/eval_jaxpr/ppermute | solution.py:17
  755.0 11.9 %collective-permute-start.1 = (bf16[1,1,64,256]{3,2,1,0:T(8,128)(2,1)S(1)}, bf16[1,1,64,256]{3,2,1,0:T(8,128)(2,1)S(1)}, u32[]{:S(2)}, u32[]{:S(2)}) collective-permute-start(bf16[1,1,64,256]{3,2,1,0:T(8,128)(2,1)S(1)} %get-tuple-element.234), channel_id=1, source_target_pairs={{0,1},{1,2},{2,3},{3,4},{4,5},{5,6},{6,7},{8,9},{9,10},{10,11},{11... | collective-permute-start | bytes 98312 | tf_op jit(solution)/shard_map/while/body/eval_jaxpr/ppermute | solution.py:15
  767.7 10.9 %collective-permute-start.2 = (f32[1,8,64,256]{3,2,1,0:T(8,128)S(1)}, f32[1,8,64,256]{3,2,1,0:T(8,128)S(1)}, u32[]{:S(2)}, u32[]{:S(2)}) collective-permute-start(f32[1,8,64,256]{3,2,1,0:T(8,128)S(1)} %add_add_fusion.2), channel_id=1, source_target_pairs={{0,8},{8,16},{16,24},{24,32},{32,40},{40,48},{48,56},{56,64},{64,7... | collective-permute-start | bytes 1572872 | tf_op jit(solution)/shard_map/while/body/eval_jaxpr/ppermute | solution.py:27
  778.7 13.2 %collective-permute-start = (bf16[1,1,64,256]{3,2,1,0:T(8,128)(2,1)S(1)}, bf16[1,1,64,256]{3,2,1,0:T(8,128)(2,1)S(1)}, u32[]{:S(2)}, u32[]{:S(2)}) collective-permute-start(bf16[1,1,64,256]{3,2,1,0:T(8,128)(2,1)S(1)} %get-tuple-element.233), channel_id=1, source_target_pairs={{1,0},{2,1},{3,2},{4,3},{5,4},{6,5},{7,6},{9,8},{10,9},{11,10},{12... | collective-permute-start | bytes 98312 | tf_op jit(solution)/shard_map/while/body/eval_jaxpr/ppermute | solution.py:17
  780.7 11.3 %collective-permute-start.1 = (bf16[1,1,64,256]{3,2,1,0:T(8,128)(2,1)S(1)}, bf16[1,1,64,256]{3,2,1,0:T(8,128)(2,1)S(1)}, u32[]{:S(2)}, u32[]{:S(2)}) collective-permute-start(bf16[1,1,64,256]{3,2,1,0:T(8,128)(2,1)S(1)} %get-tuple-element.234), channel_id=1, source_target_pairs={{0,1},{1,2},{2,3},{3,4},{4,5},{5,6},{6,7},{8,9},{9,10},{10,11},{11... | collective-permute-start | bytes 98312 | tf_op jit(solution)/shard_map/while/body/eval_jaxpr/ppermute | solution.py:15
  792.8 14.4 %collective-permute-start.2 = (f32[1,8,64,256]{3,2,1,0:T(8,128)S(1)}, f32[1,8,64,256]{3,2,1,0:T(8,128)S(1)}, u32[]{:S(2)}, u32[]{:S(2)}) collective-permute-start(f32[1,8,64,256]{3,2,1,0:T(8,128)S(1)} %add_add_fusion.2), channel_id=1, source_target_pairs={{0,8},{8,16},{16,24},{24,32},{32,40},{40,48},{48,56},{56,64},{64,7... | collective-permute-start | bytes 1572872 | tf_op jit(solution)/shard_map/while/body/eval_jaxpr/ppermute | solution.py:27
  810.6 10.7 %collective-permute-start.6 = (f32[1,4,64,256]{3,2,1,0:T(8,128)S(1)}, f32[1,4,64,256]{3,2,1,0:T(8,128)S(1)}, u32[]{:S(2)}, u32[]{:S(2)}) collective-permute-start(f32[1,4,64,256]{3,2,1,0:T(8,128)S(1)} %get-tuple-element.165), channel_id=1, source_target_pairs={{1,0},{2,1},{3,2},{4,3},{5,4},{6,5},{7,6},{9,8},{10,9},{11,10},{12... | collective-permute-start | bytes 786440 | tf_op jit(solution)/shard_map/ppermute | solution.py:17
  (52 other events, 390.5 us)
where the time goes:
time: 842 us; the launch traced here: 834 us
  starting transfers between devices  416 us (49%)
  waiting for transfers between devices  348 us (41%)
  other arithmetic  29.5 us (4%)
  local copies, waits for them, and re-layouts  19.3 us (2%)
  matrix products  15.4 us (2%)
    ppermute x31, waiting for transfers between devices, from_behind(): return lax.ppermute(array, axis, pairs)  209 us
    ppermute x33, starting transfers between devices, extended_2(): lax.ppermute(tail, axis, [(i, (i + 1) % count) for i in range(ends)])  184 us
    ppermute x31, starting transfers between devices, from_behind(): return lax.ppermute(array, axis, pairs)  137 us
    ppermute x33, starting transfers between devices, extended_2(): lax.ppermute(head, axis, [((i + 1) % count, i) for i in range(ends)])  95.1 us
    ppermute x33, waiting for transfers between devices, extended_2(): lax.ppermute(head, axis, [((i + 1) % count, i) for i in range(ends)])  79.4 us
    ppermute x33, waiting for transfers between devices, extended_2(): lax.ppermute(tail, axis, [(i, (i + 1) % count) for i in range(ends)])  60 us
    add x31, other arithmetic, turn(): advanced = carried + coarse_step * slope_term + defect  22.4 us
  transfers between devices with their start and end apart: 97, of which 69 were waited for; matrix products, arithmetic and copies ran while one was open for 1% of the time, Pallas kernels for 0%

commit v1 on v0

v1 whole, which is shorter than its diff:
```python
import functools

import jax
import jax.numpy as jnp
from jax import lax
from jax.experimental import pallas as pl
from jax.experimental.pallas import tpu as pltpu
from jax.sharding import PartitionSpec as P

C = 256
COLS = 64
ROWS = 64
LAYERS = 4
OWN = 8
TILE = 4
GROUP = 4
PLANES = 8
TILES = ROWS // TILE
DEPTH = 7
WIDE = OWN + 2 * (DEPTH - LAYERS)
SENT = TILE + 2 * (GROUP - 1)
EXTRA = 16
BF16, F32 = jnp.bfloat16, jnp.float32
AXES = ("fine", "coarse")
VMEM = pl.BlockSpec(memory_space=pltpu.VMEM)
SMEM = pl.BlockSpec(memory_space=pltpu.SMEM)


def cells(row, rows):
    return pl.ds(row * COLS, rows * COLS)


def spread(wide, slot, row, values):
    col = lax.broadcasted_iota(jnp.int32, values.shape, 0)
    left = jnp.where(col == 0, 0.0, pltpu.roll(values, 1, 0))
    right = jnp.where(col == COLS - 1, 0.0, pltpu.roll(values, COLS - 1, 0))
    at = cells(row, 1)
    wide[slot, at, 0:C] = left.astype(BF16)
    wide[slot, at, C : 2 * C] = values.astype(BF16)
    wide[slot, at, 2 * C : 3 * C] = right.astype(BF16)


def convolve(wide, slot, kernel, row, rows):
    taps = [wide[slot, cells(row + a, rows), :] for a in range(3)]
    return jnp.dot(jnp.concatenate(taps, axis=1), kernel, preferred_element_type=F32)


def inside(row):
    return jnp.where((row >= 0) & (row < ROWS), 1.0, 0.0).astype(F32)


def chunks(rows, size):
    return [(row, min(size, rows - row)) for row in range(0, rows, size)]


def place():
    slab = lax.axis_index("fine")
    return slab // 4, (slab // 2) % 2, slab % 2, lax.axis_index("coarse")


def relax_rows(depth, first_row, read, weights, biases, steps, state, wide, visit):
    total = OWN + 2 * depth
    for row in range(total):
        values = read(row)
        state[cells(row, 1), :] = values
        spread(wide, 0, row, values)
    for layer in range(LAYERS):
        for start, rows in chunks(total - 2 * (layer + 1), 4):
            slope = jnp.tanh(
                convolve(wide, layer % 2, weights[layer], start, rows)
                + biases[layer : layer + 1, :]
            )
            for i in range(rows):
                row = start + i + layer + 1
                piece = slope[i * COLS : (i + 1) * COLS, :]
                values = state[cells(row, 1), :] + steps[layer] * piece
                if not depth <= row < depth + OWN:
                    values = values * inside(first_row + row - depth)
                state[cells(row, 1), :] = values
                if layer < LAYERS - 1:
                    spread(wide, (layer + 1) % 2, start + i, values)
                visit(layer, row, piece, values)


def split3(values):
    high = values.astype(BF16).astype(F32)
    rest = values - high
    middle = rest.astype(BF16).astype(F32)
    return [high, middle, rest - middle]


def prepare_kernel(initial, weights, to_below, to_above, kernel, sem):
    copy = pltpu.make_async_copy(weights.at[0], kernel, sem)
    copy.start()
    to_below[...] = initial[(OWN - DEPTH) * COLS :, :].astype(BF16)
    to_above[...] = initial[: DEPTH * COLS, :].astype(BF16)
    copy.wait()


def first_kernel(
    steps, up, own, down, weights, biases, same, other, relaxed, state, wide, gain
):
    plane, half, core, coarse = place()
    is_first = (plane == 0) & (half == 0) & (core == 0)
    total_step = steps[0] + steps[1] + steps[2] + steps[3]

    def read(row):
        if row < DEPTH:
            return up[cells(row, 1), :].astype(F32)
        if row < DEPTH + OWN:
            return own[cells(row - DEPTH, 1), :]
        return down[cells(row - DEPTH - OWN, 1), :].astype(F32)

    def visit(layer, row, slope, values):
        at = row - LAYERS
        if not 0 <= at < WIDE:
            return
        to = cells(at, 1)
        if layer == 0:
            gain[to, :] = (steps[0] - total_step) * slope
            return
        gained = gain[to, :] + steps[layer] * slope
        if layer == LAYERS - 1:
            gained = jnp.where(is_first, values, gained)
            if DEPTH <= row < DEPTH + OWN:
                relaxed[cells(row - DEPTH, 1), :] = values
        gain[to, :] = gained

    relax_rows(DEPTH, coarse * OWN, read, weights, biases, steps, state, wide, visit)
    pieces = split3(biases[0:1, :]) + split3(jnp.full((1, C), total_step, F32))
    pieces.append(jnp.zeros((EXTRA - len(pieces), C), F32))
    extra = jnp.concatenate(pieces, axis=0).astype(BF16)
    for ref, side in ((same, half), (other, 1 - half)):
        base = pl.multiple_of(side * (TILE * COLS), TILE * COLS)
        ref[0 : SENT * COLS, :] = gain[pl.ds(base, SENT * COLS), :].astype(BF16)
        ref[SENT * COLS :, :] = extra


def last_kernel(
    steps, initial, relaxed, mine, across, halo_a, halo_b, near, far, halo_c, halo_d,
    weights, biases, corrected, finished, state, wide,
):
    plane, half, core, coarse = place()
    is_first = (plane == 0) & (half == 0) & (core == 0)
    north, lower = core == 1, half == 1

    def read(row):
        at = cells(row % TILE, 1)
        a, b, c, d = (
            (halo_a, halo_b, halo_c, halo_d),
            (across, mine, far, near),
            (mine, across, near, far),
            (halo_b, halo_a, halo_d, halo_c),
        )[row // TILE]
        a, b, c, d = (ref[at, :].astype(F32) for ref in (a, b, c, d))
        values = jnp.where(north, jnp.where(lower, a, b), jnp.where(lower, c, d))
        if TILE <= row < TILE + OWN:
            to = cells(row - TILE, 1)
            corrected[to, :] = jnp.where(is_first, initial[to, :], values)
        return values

    def visit(layer, row, slope, values):
        if layer == LAYERS - 1:
            to = cells(row - LAYERS, 1)
            finished[to, :] = jnp.where(is_first, relaxed[to, :], values)

    relax_rows(LAYERS, coarse * OWN, read, weights, biases, steps, state, wide, visit)


def chain_kernel(turn, *refs):
    refs = list(refs)
    entering = None if turn == 0 else [refs.pop(0) for _ in range(3)]
    before = None if turn == 0 else [refs.pop(0) for _ in range(GROUP)]
    defects = [refs.pop(0) for _ in range(GROUP)]
    weights = refs.pop(0)
    following = None if turn == PLANES - 1 else refs.pop(0)
    passed = [refs.pop(0) for _ in range(GROUP)]
    state, wide, hold = refs
    plane, half, core, coarse = place()
    first_row = (coarse * 2 + half) * TILE - TILE
    active = (plane == turn) & (core == 1)

    def defect(step, at):
        a, b = defects[step][at, :].astype(F32), defects[step ^ 2][at, :].astype(F32)
        return jnp.where(half == 0, a, b)

    def keep(step, row, values):
        hold[step, cells(row - TILE, 1), :] = values.astype(BF16)

    @pl.when(jnp.logical_not(active))
    def _():
        for i in range(GROUP):
            passed[i][...] = jnp.zeros_like(passed[i]) if turn == 0 else before[i][...]
        if following is not None:
            following[...] = jnp.zeros_like(following)

    @pl.when(active)
    def _():
        if turn == 0:
            hold[0] = jnp.zeros(hold.shape[1:], BF16)
            for row in range(1, 1 + SENT):
                values = defect(0, cells(row - 1, 1))
                if TILE <= row < 2 * TILE:
                    keep(1, row, values)
                else:
                    values = values * inside(first_row + row)
                state[cells(row, 1), :] = values
                spread(wide, 1, row - 1, values)
        else:
            for row in range(3 * TILE):
                values = entering[row // TILE][cells(row % TILE, 1), :].astype(F32)
                state[cells(row, 1), :] = values
                spread(wide, 0, row, values)
                if TILE <= row < 2 * TILE:
                    keep(0, row, values)
        final = GROUP - 1 if turn == PLANES - 1 else GROUP
        for step in range(1 if turn == 0 else 0, final):
            extra = defect(step, pl.ds(SENT * COLS, EXTRA))
            bias = extra[0:1, :] + extra[1:2, :] + extra[2:3, :]
            scale = extra[3:4, :] + extra[4:5, :] + extra[5:6, :]
            kernel = weights[jnp.bitwise_xor(step, 2 * half)]
            for start, rows in chunks(3 * TILE - 2 * (step + 1), 2):
                slope = jnp.tanh(convolve(wide, step % 2, kernel, start, rows) + bias)
                for i in range(rows):
                    row = start + i + step + 1
                    piece = slope[i * COLS : (i + 1) * COLS, :]
                    values = state[cells(row, 1), :] + scale * piece
                    values = values + defect(step, cells(row - 1, 1))
                    if not TILE <= row < 2 * TILE:
                        values = values * inside(first_row + row)
                    elif step == GROUP - 1:
                        following[cells(row - TILE, 1), :] = values.astype(BF16)
                    else:
                        keep(step + 1, row, values)
                    if step < GROUP - 1:
                        state[cells(row, 1), :] = values
                        spread(wide, (step + 1) % 2, start + i, values)
        for i in range(GROUP):
            passed[i][...] = hold[jnp.bitwise_xor(i, 2 * half)]


def cost(row_products):
    flops = 2 * row_products * COLS * 9 * C * C
    return pl.CostEstimate(flops=flops, bytes_accessed=flops // 512, transcendentals=0)


def call(body, name, row_products, rows, outs, in_specs, more=()):
    return pl.pallas_call(
        body,
        name=name,
        out_shape=outs,
        in_specs=in_specs,
        out_specs=jax.tree.map(lambda _: VMEM, outs),
        scratch_shapes=[
            pltpu.VMEM((rows * COLS, C), F32),
            pltpu.VMEM((2, rows * COLS, 3 * C), BF16),
            *more,
        ],
        compiler_params=pltpu.CompilerParams(vmem_limit_bytes=16 * 2**20),
        cost_estimate=cost(row_products),
    )


def shape(rows, dtype=BF16):
    return jax.ShapeDtypeStruct((rows, C), dtype)


def device(plane, half, core, coarse):
    return ((plane * 2 + half) * 2 + core) * 8 + coarse


def tile_device(plane, tile):
    return device(plane, tile % 2, 1, tile // 2)


def beside(half, coarse, by):
    x = (2 * (coarse % 2) + half + by) % 4
    return x % 2, 2 * (coarse // 2) + x // 2


def within_plane(link):
    pairs = []
    for plane in range(PLANES):
        for half in range(2):
            for coarse in range(8):
                pairs.append(link(plane, half, coarse))
    return pairs


def local(start_states, weights, biases, step_sizes):
    initial = start_states.reshape(OWN * COLS, C)
    kernels = weights.reshape(LAYERS, 9 * C, C)
    downward = [(i, i + 1) for i in range(7)]
    upward = [(i + 1, i) for i in range(7)]

    to_below, to_above, kernel = pl.pallas_call(
        prepare_kernel,
        name="prepare",
        out_shape=(shape(DEPTH * COLS), shape(DEPTH * COLS), shape(9 * C)),
        in_specs=[VMEM, pl.BlockSpec(memory_space=pltpu.HBM)],
        out_specs=(VMEM, VMEM, VMEM),
        scratch_shapes=[pltpu.SemaphoreType.DMA(())],
        compiler_params=pltpu.CompilerParams(vmem_limit_bytes=8 * 2**20),
    )(initial, kernels)
    above = lax.ppermute(to_below, "coarse", downward)
    below = lax.ppermute(to_above, "coarse", upward)

    to_north = within_plane(lambda p, h, c: (device(p, h, 0, c), device(p, h, 1, c)))
    to_other_north = within_plane(
        lambda p, h, c: (device(p, h, 0, c), device(p, 1 - h, 1, c))
    )
    north_to_north = within_plane(
        lambda p, h, c: (device(p, h, 1, c), device(p, 1 - h, 1, c))
    )

    def from_right(p, h, c):
        half, coarse = beside(h, c, 1)
        return device(p, half, 0, coarse), device(p, h, 1, c)

    def from_left(p, h, c):
        half, coarse = beside(h, c, 1)
        return device(p, h, 1, c), device(p, half, 1, coarse)

    near_south = lax.ppermute(kernel, AXES, to_north)
    far_south = lax.ppermute(kernel, AXES, within_plane(from_right))
    far_north = lax.ppermute(kernel, AXES, within_plane(from_left))

    message = shape(SENT * COLS + EXTRA)
    same, other, relaxed = call(
        first_kernel,
        "first",
        68,
        OWN + 2 * DEPTH,
        (message, message, shape(OWN * COLS, F32)),
        [SMEM] + [VMEM] * 5,
        (pltpu.VMEM((WIDE * COLS, C), F32),),
    )(step_sizes, above, initial, below, kernels, biases)
    defects = [
        lax.ppermute(same, AXES, to_north),
        same,
        lax.ppermute(other, AXES, to_other_north),
        lax.ppermute(other, AXES, north_to_north),
    ]
    chain_kernels = jnp.stack([near_south, kernel, far_south, far_north])

    block = shape(TILE * COLS)
    entering, passed = [], []
    for turn in range(PLANES):
        last = turn == PLANES - 1
        outs = (block,) * (GROUP if last else GROUP + 1)
        operands = [*entering, *passed, *defects, chain_kernels]
        results = call(
            functools.partial(chain_kernel, turn),
            "chain",
            28,
            3 * TILE,
            outs,
            [VMEM] * len(operands),
            (pltpu.VMEM((GROUP, TILE * COLS, C), BF16),),
        )(*operands)
        passed = results[-GROUP:]
        if not last:
            own, up, down = (
                lax.ppermute(
                    results[0],
                    AXES,
                    [
                        (tile_device(turn, q), tile_device(turn + 1, q + by))
                        for q in range(TILES)
                        if 0 <= q + by < TILES
                    ],
                )
                for by in (0, 1, -1)
            )
            entering = [up, own, down]

    near_state, own_state, far_state, across_state = passed

    def halos(to_same, to_other_core):
        pairs = []
        for plane in range(PLANES):
            for coarse in range(8):
                if coarse > 0:
                    dest = device(plane, to_same, to_other_core, coarse)
                    pairs.append((device(plane, 1, 1, coarse - 1), dest))
                if coarse < 7:
                    dest = device(plane, 1 - to_same, to_other_core, coarse)
                    pairs.append((device(plane, 0, 1, coarse + 1), dest))
        return pairs

    across = lax.ppermute(across_state, AXES, north_to_north)
    halo_a = lax.ppermute(own_state, AXES, halos(1, 1))
    halo_b = lax.ppermute(across_state, AXES, halos(0, 1))
    near = lax.ppermute(near_state, AXES, [(b, a) for a, b in to_north])
    far = lax.ppermute(far_state, AXES, [(b, a) for a, b in to_other_north])
    halo_c = lax.ppermute(near_state, AXES, halos(1, 0))
    halo_d = lax.ppermute(far_state, AXES, halos(0, 0))
    result = shape(OWN * COLS, F32)
    corrected, finished = call(
        last_kernel,
        "last",
        44,
        OWN + 2 * LAYERS,
        (result, result),
        [SMEM] + [VMEM] * 12,
    )(
        step_sizes, initial, relaxed, own_state, across, halo_a, halo_b,
        near, far, halo_c, halo_d, kernels, biases,
    )
    return (
        corrected.reshape(start_states.shape),
        finished.reshape(start_states.shape),
    )


def solution(mesh):
    in_specs = (
        P("fine", None, "coarse", None, None),
        P("fine", None, None, None),
        P("fine", None),
        P("fine"),
    )
    out_specs = (P("fine", None, "coarse", None, None), P("fine", None, "coarse", None, None))
    return jax.shard_map(local, mesh=mesh, in_specs=in_specs, out_specs=out_specs, check_vma=False)
```

time: 842 us -> 153 us (0.18)
  the two profiles are of different devices: /device:TPU:118 before, /device:TPU:232 now
where the time goes in v1:
time: 153 us; the launch traced here: 152 us
  waiting for transfers between devices  86.2 us (56%)
  starting transfers between devices  48.4 us (32%)
  Pallas kernels  12.5 us (8%)
  local copies, waits for them, and re-layouts  3.39 us (2%)
    ppermute x1, waiting for transfers between devices, local(): near = lax.ppermute(near_state, AXES, [(b, a) for a, b in to_north])  67.6 us
    ppermute x21, starting transfers between devices, local(): lax.ppermute(results[0], AXES, [(tile_device(turn, q), tile_device(turn +...  14 us
    ppermute x1, starting transfers between devices, local(): lax.ppermute(same, AXES, to_north)  10.5 us
    pallas_call x1, Pallas kernels, local(): call(first_kernel, 'first', 68, OWN + 2 * DEPTH, (message, message, shape...  6.19 us
    ppermute x1, starting transfers between devices, local(): below = lax.ppermute(to_above, 'coarse', upward)  5.54 us
    ppermute x1, waiting for transfers between devices, local(): halo_d = lax.ppermute(far_state, AXES, halos(0, 0))  5.49 us
    pallas_call x1, Pallas kernels, local(): call(last_kernel, 'last', 44, OWN + 2 * LAYERS, (result, result), [SMEM]...  5.11 us
    ppermute x1, waiting for transfers between devices, local(): below = lax.ppermute(to_above, 'coarse', upward)  5.03 us
  transfers between devices with their start and end apart: 36, of which 7 were waited for; matrix products, arithmetic and copies ran while one was open for 0% of the time, Pallas kernels for 4%

profile of v1, /device:TPU:232, one launch (start us, length us, event | category | flops | bytes accessed | tf_op | source)
XLA Modules:
  0.0 152.5 jit_solution(13931941558314861059)
XLA Ops:
  0.7 2.3 %copy-done = bf16[4,9,256,256]{3,2,1,0:T(8,128)(2,1)S(1)} copy-done((bf16[4,9,256,256]{3,2,1,0:T(8,128)(2,1)S(1)}, bf16[4,9,256,256]{3,2,1,0:T(8,128)(2,1)}, u32[]{:S(2)}) %copy-start) | copy-done | bytes 4718616
  3.0 1.0 copy-done.2
  4.0 0.3 prepare.1
  4.3 2.1 %collective-permute-start.5 = (bf16[2304,256]{1,0:T(8,128)(2,1)S(1)}, bf16[2304,256]{1,0:T(8,128)(2,1)S(1)}, u32[]{:S(2)}, u32[]{:S(2)}) collective-permute-start(bf16[2304,256]{1,0:T(8,128)(2,1)S(1)} %get-tuple-element.54), channel_id=1, source_target_pairs={{0,8},{1,9},{2,10},{3,11},{4,12},{5,13},{6,14},{7,15},{16,24},{17,... | collective-permute-start | bytes 3538952 | tf_op jit(solution)/shard_map/ppermute | solution.py:324
  6.4 3.7 %collective-permute-start.6 = (bf16[2304,256]{1,0:T(8,128)(2,1)S(1)}, bf16[2304,256]{1,0:T(8,128)(2,1)S(1)}, u32[]{:S(2)}, u32[]{:S(2)}) collective-permute-start(bf16[2304,256]{1,0:T(8,128)(2,1)S(1)} %get-tuple-element.54), channel_id=1, source_target_pairs={{16,8},{17,9},{18,10},{19,11},{20,12},{21,13},{22,14},{23,15},{1,2... | collective-permute-start | bytes 3538952 | tf_op jit(solution)/shard_map/ppermute | solution.py:325
  10.1 0.7 collective-permute-start.7
  10.8 2.7 %collective-permute-start = (bf16[448,256]{1,0:T(8,128)(2,1)S(1)}, bf16[448,256]{1,0:T(8,128)(2,1)S(1)}, u32[]{:S(2)}, u32[]{:S(2)}) collective-permute-start(bf16[448,256]{1,0:T(8,128)(2,1)S(1)} %get-tuple-element.49), channel_id=1, source_target_pairs={{0,1},{1,2},{2,3},{3,4},{4,5},{5,6},{6,7},{8,9},{9,10},{10,11},{11... | collective-permute-start | bytes 688136 | tf_op jit(solution)/shard_map/ppermute | solution.py:305
  13.5 5.5 %collective-permute-start.1 = (bf16[448,256]{1,0:T(8,128)(2,1)S(1)}, bf16[448,256]{1,0:T(8,128)(2,1)S(1)}, u32[]{:S(2)}, u32[]{:S(2)}) collective-permute-start(bf16[448,256]{1,0:T(8,128)(2,1)S(1)} %get-tuple-element.50), channel_id=1, source_target_pairs={{1,0},{2,1},{3,2},{4,3},{5,4},{6,5},{7,6},{9,8},{10,9},{11,10},{12... | collective-permute-start | bytes 688136 | tf_op jit(solution)/shard_map/ppermute | solution.py:306
  19.1 4.5 %collective-permute-done.up = bf16[448,256]{1,0:T(8,128)(2,1)S(1)} collective-permute-done((bf16[448,256]{1,0:T(8,128)(2,1)S(1)}, bf16[448,256]{1,0:T(8,128)(2,1)S(1)}, u32[]{:S(2)}, u32[]{:S(2)}) %collective-permute-start) | collective-permute-done | bytes 229408 | tf_op jit(solution)/shard_map/ppermute | solution.py:305
  23.6 5.0 %collective-permute-done.1.down = bf16[448,256]{1,0:T(8,128)(2,1)S(1)} collective-permute-done((bf16[448,256]{1,0:T(8,128)(2,1)S(1)}, bf16[448,256]{1,0:T(8,128)(2,1)S(1)}, u32[]{:S(2)}, u32[]{:S(2)}) %collective-permute-start.1) | collective-permute-done | bytes 229408 | tf_op jit(solution)/shard_map/ppermute | solution.py:306
  28.6 6.2 %first.1 = (bf16[656,256]{1,0:T(8,128)(2,1)S(1)}, bf16[656,256]{1,0:T(8,128)(2,1)S(1)}, f32[512,256]{1,0:T(8,128)S(1)}) custom-call(f32[4]{0:T(128)S(1)} %copy-done.5, bf16[448,256]{1,0:T(8,128)(2,1)S(1)} %collective-permute-done.up, f32[512,256]{1,0:T(8,128)S(1)} %bitcast.13, bf16[448,256]{1,0:T(8,128)(2,1)S(1)} %collective-permute-done.1.down, ...), custom_call_target="tpu_custom_call" | custom-call | flops 5133828096 | bytes 10027008 | tf_op jit(solution)/shard_map/first/pallas_call | solution.py:329
  34.8 1.3 collective-permute-start.3
  36.2 0.7 collective-permute-start.4
  36.8 0.0 collective-permute-done.5
  36.9 10.5 %collective-permute-start.2 = (bf16[656,256]{1,0:T(8,128)(2,1)S(1)}, bf16[656,256]{1,0:T(8,128)(2,1)S(1)}, u32[]{:S(2)}, u32[]{:S(2)}) collective-permute-start(bf16[656,256]{1,0:T(8,128)(2,1)S(1)} %get-tuple-element.52.refs_1_.refs_8_), channel_id=1, source_target_pairs={{0,8},{1,9},{2,10},{3,11},{4,12},{5,13},{6,14},{7,15},{16,24},{17,... | collective-permute-start | bytes 1007624 | tf_op jit(solution)/shard_map/ppermute | solution.py:339
  47.4 0.0 collective-permute-done.6
  47.4 0.6 pad_maximum_fusion.refs_4_.refs_11_
  48.0 0.6 collective-permute-done.2.refs_0_.refs_7_
  48.6 0.0 collective-permute-done.3.refs_2_.refs_9_
  48.6 0.0 collective-permute-done.4.refs_3_.refs_10_
  48.7 0.7 collective-permute-start.10
  49.3 0.7 collective-permute-start.8
  50.0 0.7 collective-permute-start.9
  50.7 0.0 collective-permute-done.9.refs_1_
  50.7 0.1 chain.9
  50.8 0.7 collective-permute-start.11
  51.5 0.7 collective-permute-start.12
  52.2 0.7 collective-permute-start.13
  52.9 0.0 collective-permute-done.13.refs_2_
  52.9 0.3 chain.10
  53.1 0.7 collective-permute-start.14
  53.8 0.7 collective-permute-start.15
  54.5 0.7 collective-permute-start.16
  55.2 0.0 collective-permute-done.15.refs_1_
  55.2 0.0 collective-permute-done.16.refs_2_
  55.2 0.1 chain.11
  55.3 0.7 collective-permute-start.17
  55.9 0.7 collective-permute-start.18
  56.6 0.7 collective-permute-start.19
  57.3 0.1 chain.12
  57.4 0.7 collective-permute-start.20
  58.1 0.7 collective-permute-start.21
  58.8 0.7 collective-permute-start.22
  59.5 0.1 chain.13
  59.6 0.7 collective-permute-start.23
  60.2 0.7 collective-permute-start.24
  60.9 0.7 collective-permute-start.25
  61.6 0.3 chain.14
  61.9 0.7 collective-permute-start.26
  62.6 0.7 collective-permute-start.27
  63.3 0.7 collective-permute-start.28
  64.0 0.1 chain.15
  64.0 0.7 collective-permute-start.29
  64.7 0.7 collective-permute-start.30
  65.4 0.7 collective-permute-start.31
  66.1 1.3 collective-permute-start.32
  67.4 1.3 collective-permute-start.34
  68.7 1.3 collective-permute-start.33
  70.0 1.3 collective-permute-start.35
  71.3 67.6 %collective-permute-done.32.near = bf16[256,256]{1,0:T(8,128)(2,1)S(1)} collective-permute-done((bf16[256,256]{1,0:T(8,128)(2,1)S(1)}, bf16[256,256]{1,0:T(8,128)(2,1)S(1)}, u32[]{:S(2)}, u32[]{:S(2)}) %collective-permute-start.32) | collective-permute-done | bytes 131104 | tf_op jit(solution)/shard_map/ppermute | solution.py:394
  138.9 2.6 %collective-permute-done.33.far = bf16[256,256]{1,0:T(8,128)(2,1)S(1)} collective-permute-done((bf16[256,256]{1,0:T(8,128)(2,1)S(1)}, bf16[256,256]{1,0:T(8,128)(2,1)S(1)}, u32[]{:S(2)}, u32[]{:S(2)}) %collective-permute-start.33) | collective-permute-done | bytes 131104 | tf_op jit(solution)/shard_map/ppermute | solution.py:395
  141.5 0.3 collective-permute-done.34.halo_c
  141.8 5.5 %collective-permute-done.35.halo_d = bf16[256,256]{1,0:T(8,128)(2,1)S(1)} collective-permute-done((bf16[256,256]{1,0:T(8,128)(2,1)S(1)}, bf16[256,256]{1,0:T(8,128)(2,1)S(1)}, u32[]{:S(2)}, u32[]{:S(2)}) %collective-permute-start.35) | collective-permute-done | bytes 131104 | tf_op jit(solution)/shard_map/ppermute | solution.py:397
  147.3 5.1 %last.1 = (f32[512,256]{1,0:T(8,128)}, f32[512,256]{1,0:T(8,128)}) custom-call(f32[4]{0:T(128)S(1)} %copy-done.5, f32[512,256]{1,0:T(8,128)S(1)} %bitcast.14, f32[512,256]{1,0:T(8,128)S(1)} %get-tuple-element.51.relaxed, bf16[256,256]{1,0:T(8,128)(2,1)S(1)} %get-tuple-element.90.mine, bf16[256,256]{1,0:T(8,128)(2,1)S(1)} %collective-permute-done.29.across, ...), custom_call_target="tpu_custom_call" | custom-call | flops 3321888768 | bytes 6488064 | tf_op jit(solution)/shard_map/last/pallas_call | solution.py:399
  (32 shorter events, 0.1 us)
Async XLA Ops:
  0.6 28.0 %copy-start.5 = (f32[4]{0:T(128)S(1)}, f32[4]{0:T(128)}, u32[]{:S(2)}) copy-start(f32[4]{0:T(128)} %steps.3) | copy-start | bytes 52
  0.6 2.3 %copy-start = (bf16[4,9,256,256]{3,2,1,0:T(8,128)(2,1)S(1)}, bf16[4,9,256,256]{3,2,1,0:T(8,128)(2,1)}, u32[]{:S(2)}) copy-start(bf16[4,9,256,256]{3,2,1,0:T(8,128)(2,1)} %param.5) | copy-start | bytes 14155780
  3.0 1.0 copy-start.2
  4.0 24.6 %copy-start.1 = (bf16[4,9,256,256]{3,2,1,0:T(8,128)(2,1)S(1)}, bf16[4,9,256,256]{3,2,1,0:T(8,128)(2,1)}, u32[]{:S(2)}) copy-start(bf16[4,9,256,256]{3,2,1,0:T(8,128)(2,1)} %param.5) | copy-start | bytes 14155780
  4.0 24.6 %copy-start.3 = (f32[1,1,8,64,256]{4,3,2,1,0:T(8,128)S(1)}, f32[1,1,8,64,256]{4,3,2,1,0:T(8,128)}, u32[]{:S(2)}) copy-start(f32[1,1,8,64,256]{4,3,2,1,0:T(8,128)} %param.4) | copy-start | bytes 1572868
  4.0 24.6 %copy-start.4 = (f32[4,256]{1,0:T(4,128)S(1)}, f32[4,256]{1,0:T(4,128)}, u32[]{:S(2)}) copy-start(f32[4,256]{1,0:T(4,128)} %biases.3) | copy-start | bytes 12292
  4.3 32.5 %collective-permute-start.5 = (bf16[2304,256]{1,0:T(8,128)(2,1)S(1)}, bf16[2304,256]{1,0:T(8,128)(2,1)S(1)}, u32[]{:S(2)}, u32[]{:S(2)}) collective-permute-start(bf16[2304,256]{1,0:T(8,128)(2,1)S(1)} %get-tuple-element.54), channel_id=1, source_target_pairs={{0,8},{1,9},{2,10},{3,11},{4,12},{5,13},{6,14},{7,15},{16,24},{17,... | collective-permute-start | bytes 3538952 | tf_op jit(solution)/shard_map/ppermute | solution.py:324
  6.4 41.0 %collective-permute-start.6 = (bf16[2304,256]{1,0:T(8,128)(2,1)S(1)}, bf16[2304,256]{1,0:T(8,128)(2,1)S(1)}, u32[]{:S(2)}, u32[]{:S(2)}) collective-permute-start(bf16[2304,256]{1,0:T(8,128)(2,1)S(1)} %get-tuple-element.54), channel_id=1, source_target_pairs={{16,8},{17,9},{18,10},{19,11},{20,12},{21,13},{22,14},{23,15},{1,2... | collective-permute-start | bytes 3538952 | tf_op jit(solution)/shard_map/ppermute | solution.py:325
  10.1 37.3 %collective-permute-start.7 = (bf16[2304,256]{1,0:T(8,128)(2,1)S(1)}, bf16[2304,256]{1,0:T(8,128)(2,1)S(1)}, u32[]{:S(2)}, u32[]{:S(2)}) collective-permute-start(bf16[2304,256]{1,0:T(8,128)(2,1)S(1)} %get-tuple-element.54), channel_id=1, source_target_pairs={{8,24},{9,25},{10,26},{11,27},{12,28},{13,29},{14,30},{15,31},{24,... | collective-permute-start | bytes 3538952 | tf_op jit(solution)/shard_map/ppermute | solution.py:326
  10.8 12.8 %collective-permute-start = (bf16[448,256]{1,0:T(8,128)(2,1)S(1)}, bf16[448,256]{1,0:T(8,128)(2,1)S(1)}, u32[]{:S(2)}, u32[]{:S(2)}) collective-permute-start(bf16[448,256]{1,0:T(8,128)(2,1)S(1)} %get-tuple-element.49), channel_id=1, source_target_pairs={{0,1},{1,2},{2,3},{3,4},{4,5},{5,6},{6,7},{8,9},{9,10},{10,11},{11... | collective-permute-start | bytes 688136 | tf_op jit(solution)/shard_map/ppermute | solution.py:305
  13.5 15.1 %collective-permute-start.1 = (bf16[448,256]{1,0:T(8,128)(2,1)S(1)}, bf16[448,256]{1,0:T(8,128)(2,1)S(1)}, u32[]{:S(2)}, u32[]{:S(2)}) collective-permute-start(bf16[448,256]{1,0:T(8,128)(2,1)S(1)} %get-tuple-element.50), channel_id=1, source_target_pairs={{1,0},{2,1},{3,2},{4,3},{5,4},{6,5},{7,6},{9,8},{10,9},{11,10},{12... | collective-permute-start | bytes 688136 | tf_op jit(solution)/shard_map/ppermute | solution.py:306
  34.8 13.8 %collective-permute-start.3 = (bf16[656,256]{1,0:T(8,128)(2,1)S(1)}, bf16[656,256]{1,0:T(8,128)(2,1)S(1)}, u32[]{:S(2)}, u32[]{:S(2)}) collective-permute-start(bf16[656,256]{1,0:T(8,128)(2,1)S(1)} %get-tuple-element.53), channel_id=1, source_target_pairs={{0,24},{1,25},{2,26},{3,27},{4,28},{5,29},{6,30},{7,31},{16,8},{17... | collective-permute-start | bytes 1007624 | tf_op jit(solution)/shard_map/ppermute | solution.py:341
  36.2 12.5 %collective-permute-start.4 = (bf16[656,256]{1,0:T(8,128)(2,1)S(1)}, bf16[656,256]{1,0:T(8,128)(2,1)S(1)}, u32[]{:S(2)}, u32[]{:S(2)}) collective-permute-start(bf16[656,256]{1,0:T(8,128)(2,1)S(1)} %get-tuple-element.53), channel_id=1, source_target_pairs={{8,24},{9,25},{10,26},{11,27},{12,28},{13,29},{14,30},{15,31},{24,... | collective-permute-start | bytes 1007624 | tf_op jit(solution)/shard_map/ppermute | solution.py:342
  36.9 11.8 %collective-permute-start.2 = (bf16[656,256]{1,0:T(8,128)(2,1)S(1)}, bf16[656,256]{1,0:T(8,128)(2,1)S(1)}, u32[]{:S(2)}, u32[]{:S(2)}) collective-permute-start(bf16[656,256]{1,0:T(8,128)(2,1)S(1)} %get-tuple-element.52.refs_1_.refs_8_), channel_id=1, source_target_pairs={{0,8},{1,9},{2,10},{3,11},{4,12},{5,13},{6,14},{7,15},{16,24},{17,... | collective-permute-start | bytes 1007624 | tf_op jit(solution)/shard_map/ppermute | solution.py:339
  48.7 2.0 %collective-permute-start.10 = (bf16[256,256]{1,0:T(8,128)(2,1)S(1)}, bf16[256,256]{1,0:T(8,128)(2,1)S(1)}, u32[]{:S(2)}, u32[]{:S(2)}) collective-permute-start(bf16[256,256]{1,0:T(8,128)(2,1)S(1)} %get-tuple-element.55), channel_id=1, source_target_pairs={{24,40},{9,56},{25,41},{10,57},{26,42},{11,58},{27,43},{12,59},{28... | collective-permute-start | bytes 393224 | tf_op jit(solution)/shard_map/ppermute | solution.py:364
  49.3 1.4 collective-permute-start.8
  50.0 0.7 collective-permute-start.9
  50.8 2.0 %collective-permute-start.11 = (bf16[256,256]{1,0:T(8,128)(2,1)S(1)}, bf16[256,256]{1,0:T(8,128)(2,1)S(1)}, u32[]{:S(2)}, u32[]{:S(2)}) collective-permute-start(bf16[256,256]{1,0:T(8,128)(2,1)S(1)} %get-tuple-element.60), channel_id=1, source_target_pairs={{40,88},{56,73},{41,89},{57,74},{42,90},{58,75},{43,91},{59,76},{4... | collective-permute-start | bytes 393224 | tf_op jit(solution)/shard_map/ppermute | solution.py:364
  51.5 1.4 collective-permute-start.12
  52.2 0.7 collective-permute-start.13
  53.1 2.0 %collective-permute-start.14 = (bf16[256,256]{1,0:T(8,128)(2,1)S(1)}, bf16[256,256]{1,0:T(8,128)(2,1)S(1)}, u32[]{:S(2)}, u32[]{:S(2)}) collective-permute-start(bf16[256,256]{1,0:T(8,128)(2,1)S(1)} %get-tuple-element.65), channel_id=1, source_target_pairs={{72,120},{88,105},{73,121},{89,106},{74,122},{90,107},{75,123},{91... | collective-permute-start | bytes 393224 | tf_op jit(solution)/shard_map/ppermute | solution.py:364
  53.8 1.4 collective-permute-start.15
  54.5 0.7 collective-permute-start.16
  55.3 2.0 %collective-permute-start.17 = (bf16[256,256]{1,0:T(8,128)(2,1)S(1)}, bf16[256,256]{1,0:T(8,128)(2,1)S(1)}, u32[]{:S(2)}, u32[]{:S(2)}) collective-permute-start(bf16[256,256]{1,0:T(8,128)(2,1)S(1)} %get-tuple-element.70), channel_id=1, source_target_pairs={{104,152},{120,137},{105,153},{121,138},{106,154},{122,139},{107,1... | collective-permute-start | bytes 393224 | tf_op jit(solution)/shard_map/ppermute | solution.py:364
  55.9 1.4 collective-permute-start.18
  56.6 0.7 collective-permute-start.19
  57.4 2.0 %collective-permute-start.20 = (bf16[256,256]{1,0:T(8,128)(2,1)S(1)}, bf16[256,256]{1,0:T(8,128)(2,1)S(1)}, u32[]{:S(2)}, u32[]{:S(2)}) collective-permute-start(bf16[256,256]{1,0:T(8,128)(2,1)S(1)} %get-tuple-element.75), channel_id=1, source_target_pairs={{136,184},{152,169},{137,185},{153,170},{138,186},{154,171},{139,1... | collective-permute-start | bytes 393224 | tf_op jit(solution)/shard_map/ppermute | solution.py:364
  58.1 1.4 collective-permute-start.21
  58.8 0.7 collective-permute-start.22
  59.6 2.0 %collective-permute-start.23 = (bf16[256,256]{1,0:T(8,128)(2,1)S(1)}, bf16[256,256]{1,0:T(8,128)(2,1)S(1)}, u32[]{:S(2)}, u32[]{:S(2)}) collective-permute-start(bf16[256,256]{1,0:T(8,128)(2,1)S(1)} %get-tuple-element.80), channel_id=1, source_target_pairs={{168,216},{184,201},{169,217},{185,202},{170,218},{186,203},{171,2... | collective-permute-start | bytes 393224 | tf_op jit(solution)/shard_map/ppermute | solution.py:364
  60.2 1.4 collective-permute-start.24
  60.9 0.7 collective-permute-start.25
  61.9 2.0 %collective-permute-start.26 = (bf16[256,256]{1,0:T(8,128)(2,1)S(1)}, bf16[256,256]{1,0:T(8,128)(2,1)S(1)}, u32[]{:S(2)}, u32[]{:S(2)}) collective-permute-start(bf16[256,256]{1,0:T(8,128)(2,1)S(1)} %get-tuple-element.85), channel_id=1, source_target_pairs={{200,248},{216,233},{201,249},{217,234},{202,250},{218,235},{203,2... | collective-permute-start | bytes 393224 | tf_op jit(solution)/shard_map/ppermute | solution.py:364
  62.6 1.4 collective-permute-start.27
  63.3 0.7 collective-permute-start.28
  64.0 4.6 %collective-permute-start.29 = (bf16[256,256]{1,0:T(8,128)(2,1)S(1)}, bf16[256,256]{1,0:T(8,128)(2,1)S(1)}, u32[]{:S(2)}, u32[]{:S(2)}) collective-permute-start(bf16[256,256]{1,0:T(8,128)(2,1)S(1)} %get-tuple-element.91), channel_id=1, source_target_pairs={{8,24},{9,25},{10,26},{11,27},{12,28},{13,29},{14,30},{15,31},{24,... | collective-permute-start | bytes 393224 | tf_op jit(solution)/shard_map/ppermute | solution.py:391
  64.7 5.3 %collective-permute-start.30 = (bf16[256,256]{1,0:T(8,128)(2,1)S(1)}, bf16[256,256]{1,0:T(8,128)(2,1)S(1)}, u32[]{:S(2)}, u32[]{:S(2)}) collective-permute-start(bf16[256,256]{1,0:T(8,128)(2,1)S(1)} %get-tuple-element.90.mine), channel_id=1, source_target_pairs={{9,8},{24,25},{10,9},{25,26},{11,10},{26,27},{12,11},{27,28},{13,1... | collective-permute-start | bytes 393224 | tf_op jit(solution)/shard_map/ppermute | solution.py:392
  65.4 5.9 %collective-permute-start.31 = (bf16[256,256]{1,0:T(8,128)(2,1)S(1)}, bf16[256,256]{1,0:T(8,128)(2,1)S(1)}, u32[]{:S(2)}, u32[]{:S(2)}) collective-permute-start(bf16[256,256]{1,0:T(8,128)(2,1)S(1)} %get-tuple-element.91), channel_id=1, source_target_pairs={{9,24},{24,9},{10,25},{25,10},{11,26},{26,11},{12,27},{27,12},{13,... | collective-permute-start | bytes 393224 | tf_op jit(solution)/shard_map/ppermute | solution.py:393
  66.1 72.8 %collective-permute-start.32 = (bf16[256,256]{1,0:T(8,128)(2,1)S(1)}, bf16[256,256]{1,0:T(8,128)(2,1)S(1)}, u32[]{:S(2)}, u32[]{:S(2)}) collective-permute-start(bf16[256,256]{1,0:T(8,128)(2,1)S(1)} %get-tuple-element.92), channel_id=1, source_target_pairs={{8,0},{9,1},{10,2},{11,3},{12,4},{13,5},{14,6},{15,7},{24,16},{25,... | collective-permute-start | bytes 393224 | tf_op jit(solution)/shard_map/ppermute | solution.py:394
  67.4 74.5 %collective-permute-start.34 = (bf16[256,256]{1,0:T(8,128)(2,1)S(1)}, bf16[256,256]{1,0:T(8,128)(2,1)S(1)}, u32[]{:S(2)}, u32[]{:S(2)}) collective-permute-start(bf16[256,256]{1,0:T(8,128)(2,1)S(1)} %get-tuple-element.92), channel_id=1, source_target_pairs={{9,0},{24,17},{10,1},{25,18},{11,2},{26,19},{12,3},{27,20},{13,4},... | collective-permute-start | bytes 393224 | tf_op jit(solution)/shard_map/ppermute | solution.py:396
  68.7 72.8 %collective-permute-start.33 = (bf16[256,256]{1,0:T(8,128)(2,1)S(1)}, bf16[256,256]{1,0:T(8,128)(2,1)S(1)}, u32[]{:S(2)}, u32[]{:S(2)}) collective-permute-start(bf16[256,256]{1,0:T(8,128)(2,1)S(1)} %get-tuple-element.93), channel_id=1, source_target_pairs={{24,0},{25,1},{26,2},{27,3},{28,4},{29,5},{30,6},{31,7},{8,16},{9,... | collective-permute-start | bytes 393224 | tf_op jit(solution)/shard_map/ppermute | solution.py:395
  70.0 77.3 %collective-permute-start.35 = (bf16[256,256]{1,0:T(8,128)(2,1)S(1)}, bf16[256,256]{1,0:T(8,128)(2,1)S(1)}, u32[]{:S(2)}, u32[]{:S(2)}) collective-permute-start(bf16[256,256]{1,0:T(8,128)(2,1)S(1)} %get-tuple-element.93), channel_id=1, source_target_pairs={{9,16},{24,1},{10,17},{25,2},{11,18},{26,3},{12,19},{27,4},{13,20}... | collective-permute-start | bytes 393224 | tf_op jit(solution)/shard_map/ppermute | solution.py:397

commit v2 on v1

--- a/solution.py
+++ b/solution.py
@@ -6,6 +6,7 @@
 from jax.experimental import pallas as pl
 from jax.experimental.pallas import tpu as pltpu
 from jax.sharding import PartitionSpec as P
+
 
 C = 256
 COLS = 64
@@ -89,12 +90,13 @@
     return [high, middle, rest - middle]
 
 
-def prepare_kernel(initial, weights, to_below, to_above, kernel, sem):
-    copy = pltpu.make_async_copy(weights.at[0], kernel, sem)
-    copy.start()
+def prepare_kernel(initial, to_below, to_above):
     to_below[...] = initial[(OWN - DEPTH) * COLS :, :].astype(BF16)
     to_above[...] = initial[: DEPTH * COLS, :].astype(BF16)
-    copy.wait()
+
+
+def pick_kernel(weights, kernel):
+    kernel[...] = weights[0]
 
 
 def first_kernel(
@@ -244,10 +246,9 @@
     return pl.CostEstimate(flops=flops, bytes_accessed=flops // 512, transcendentals=0)
 
 
-def call(body, name, row_products, rows, outs, in_specs, more=()):
+def call(body, row_products, rows, outs, in_specs, more=()):
     return pl.pallas_call(
         body,
-        name=name,
         out_shape=outs,
         in_specs=in_specs,
         out_specs=jax.tree.map(lambda _: VMEM, outs),
@@ -293,17 +294,24 @@
     downward = [(i, i + 1) for i in range(7)]
     upward = [(i + 1, i) for i in range(7)]
 
-    to_below, to_above, kernel = pl.pallas_call(
+    to_below, to_above = pl.pallas_call(
         prepare_kernel,
         name="prepare",
-        out_shape=(shape(DEPTH * COLS), shape(DEPTH * COLS), shape(9 * C)),
-        in_specs=[VMEM, pl.BlockSpec(memory_space=pltpu.HBM)],
-        out_specs=(VMEM, VMEM, VMEM),
-        scratch_shapes=[pltpu.SemaphoreType.DMA(())],
+        out_shape=(shape(DEPTH * COLS), shape(DEPTH * COLS)),
+        in_specs=[VMEM],
+        out_specs=(VMEM, VMEM),
         compiler_params=pltpu.CompilerParams(vmem_limit_bytes=8 * 2**20),
-    )(initial, kernels)
+    )(initial)
     above = lax.ppermute(to_below, "coarse", downward)
     below = lax.ppermute(to_above, "coarse", upward)
+    kernel = pl.pallas_call(
+        pick_kernel,
+        name="pick",
+        out_shape=shape(9 * C),
+        in_specs=[VMEM],
+        out_specs=VMEM,
+        compiler_params=pltpu.CompilerParams(vmem_limit_bytes=8 * 2**20),
+    )(kernels)
 
     to_north = within_plane(lambda p, h, c: (device(p, h, 0, c), device(p, h, 1, c)))
     to_other_north = within_plane(
@@ -321,26 +329,23 @@
         half, coarse = beside(h, c, 1)
         return device(p, h, 1, c), device(p, half, 1, coarse)
 
-    near_south = lax.ppermute(kernel, AXES, to_north)
     far_south = lax.ppermute(kernel, AXES, within_plane(from_right))
     far_north = lax.ppermute(kernel, AXES, within_plane(from_left))
+    near_south = lax.ppermute(kernel, AXES, to_north)
 
     message = shape(SENT * COLS + EXTRA)
     same, other, relaxed = call(
         first_kernel,
-        "first",
         68,
         OWN + 2 * DEPTH,
         (message, message, shape(OWN * COLS, F32)),
         [SMEM] + [VMEM] * 5,
         (pltpu.VMEM((WIDE * COLS, C), F32),),
     )(step_sizes, above, initial, below, kernels, biases)
-    defects = [
-        lax.ppermute(same, AXES, to_north),
-        same,
-        lax.ppermute(other, AXES, to_other_north),
-        lax.ppermute(other, AXES, north_to_north),
-    ]
+    other_south = lax.ppermute(other, AXES, to_other_north)
+    other_north = lax.ppermute(other, AXES, north_to_north)
+    same_south = lax.ppermute(same, AXES, to_north)
+    defects = [same_south, same, other_south, other_north]
     chain_kernels = jnp.stack([near_south, kernel, far_south, far_north])
 
     block = shape(TILE * COLS)
@@ -351,7 +356,6 @@
         operands = [*entering, *passed, *defects, chain_kernels]
         results = call(
             functools.partial(chain_kernel, turn),
-            "chain",
             28,
             3 * TILE,
             outs,
@@ -360,19 +364,14 @@
         )(*operands)
         passed = results[-GROUP:]
         if not last:
-            own, up, down = (
-                lax.ppermute(
-                    results[0],
-                    AXES,
-                    [
-                        (tile_device(turn, q), tile_device(turn + 1, q + by))
-                        for q in range(TILES)
-                        if 0 <= q + by < TILES
-                    ],
-                )
-                for by in (0, 1, -1)
-            )
-            entering = [up, own, down]
+            entering = []
+            for by in (1, 0, -1):
+                pairs = [
+                    (tile_device(turn, q), tile_device(turn + 1, q + by))
+                    for q in range(TILES)
+                    if 0 <= q + by < TILES
+                ]
+                entering.append(lax.ppermute(results[0], AXES, pairs))
 
     near_state, own_state, far_state, across_state = passed
 
@@ -388,21 +387,16 @@
                     pairs.append((device(plane, 0, 1, coarse + 1), dest))
         return pairs
 
-    across = lax.ppermute(across_state, AXES, north_to_north)
-    halo_a = lax.ppermute(own_state, AXES, halos(1, 1))
-    halo_b = lax.ppermute(across_state, AXES, halos(0, 1))
     near = lax.ppermute(near_state, AXES, [(b, a) for a, b in to_north])
     far = lax.ppermute(far_state, AXES, [(b, a) for a, b in to_other_north])
     halo_c = lax.ppermute(near_state, AXES, halos(1, 0))
     halo_d = lax.ppermute(far_state, AXES, halos(0, 0))
+    across = lax.ppermute(across_state, AXES, north_to_north)
+    halo_a = lax.ppermute(own_state, AXES, halos(1, 1))
+    halo_b = lax.ppermute(across_state, AXES, halos(0, 1))
     result = shape(OWN * COLS, F32)
     corrected, finished = call(
-        last_kernel,
-        "last",
-        44,
-        OWN + 2 * LAYERS,
-        (result, result),
-        [SMEM] + [VMEM] * 12,
+        last_kernel, 44, OWN + 2 * LAYERS, (result, result), [SMEM] + [VMEM] * 12
     )(
         step_sizes, initial, relaxed, own_state, across, halo_a, halo_b,
         near, far, halo_c, halo_d, kernels, biases,

time: 153 us -> 153 us (level)
    unnamed x12 -> x10, local copies, waits for them, and re-layouts: 3.39 us -> 2.35 us
    pallas_call x10 -> x11, Pallas kernels: 12.2 us -> 12.8 us  [the longest x1 6.48 us: local(): call(first_kernel, 68, OWN + 2 * DEPTH, (message, message, shape(OWN * CO...]
where the time goes in v2:
time: 153 us
  waiting for transfers between devices  87.3 us (57%)
  starting transfers between devices  48.4 us (32%)
  Pallas kernels  12.8 us (8%)
  local copies, waits for them, and re-layouts  2.35 us (2%)
    ppermute x1, waiting for transfers between devices, local(): near = lax.ppermute(near_state, AXES, [(b, a) for a, b in to_north])  68.7 us
    ppermute x21, starting transfers between devices, local(): entering.append(lax.ppermute(results[0], AXES, pairs))  14 us
    ppermute x1, starting transfers between devices, local(): same_south = lax.ppermute(same, AXES, to_north)  10.5 us
    pallas_call x1, Pallas kernels, local(): call(first_kernel, 68, OWN + 2 * DEPTH, (message, message, shape(OWN * CO...  6.48 us
    ppermute x1, waiting for transfers between devices, local(): halo_d = lax.ppermute(far_state, AXES, halos(0, 0))  5.49 us
    ppermute x1, starting transfers between devices, local(): below = lax.ppermute(to_above, 'coarse', upward)  5.47 us
    pallas_call x1, Pallas kernels, local(): call(last_kernel, 44, OWN + 2 * LAYERS, (result, result), [SMEM] + [VMEM]...  5.26 us
    ppermute x1, waiting for transfers between devices, local(): below = lax.ppermute(to_above, 'coarse', upward)  5.03 us
  transfers between devices with their start and end apart: 36, of which 7 were waited for; matrix products, arithmetic and copies ran while one was open for 0% of the time, Pallas kernels for 4%

profile of v2, /device:TPU:232, one launch (start us, length us, event | category | flops | bytes accessed | tf_op | source)
XLA Modules:
  0.0 152.7 jit_solution(17047503679378346390)
XLA Ops:
  0.7 2.3 %copy-done = bf16[4,9,256,256]{3,2,1,0:T(8,128)(2,1)S(1)} copy-done((bf16[4,9,256,256]{3,2,1,0:T(8,128)(2,1)S(1)}, bf16[4,9,256,256]{3,2,1,0:T(8,128)(2,1)}, u32[]{:S(2)}) %copy-start) | copy-done | bytes 4718616
  3.0 0.1 pick.1
  3.1 2.2 %collective-permute-start.5 = (bf16[2304,256]{1,0:T(8,128)(2,1)S(1)}, bf16[2304,256]{1,0:T(8,128)(2,1)S(1)}, u32[]{:S(2)}, u32[]{:S(2)}) collective-permute-start(bf16[2304,256]{1,0:T(8,128)(2,1)S(1)} %pick.1), channel_id=1, source_target_pairs={{0,8},{1,9},{2,10},{3,11},{4,12},{5,13},{6,14},{7,15},{16,24},{17,... | collective-permute-start | bytes 3538952 | tf_op jit(solution)/shard_map/ppermute | solution.py:334
  5.3 3.5 %collective-permute-start.6 = (bf16[2304,256]{1,0:T(8,128)(2,1)S(1)}, bf16[2304,256]{1,0:T(8,128)(2,1)S(1)}, u32[]{:S(2)}, u32[]{:S(2)}) collective-permute-start(bf16[2304,256]{1,0:T(8,128)(2,1)S(1)} %pick.1), channel_id=1, source_target_pairs={{16,8},{17,9},{18,10},{19,11},{20,12},{21,13},{22,14},{23,15},{1,2... | collective-permute-start | bytes 3538952 | tf_op jit(solution)/shard_map/ppermute | solution.py:332
  8.8 0.7 collective-permute-start.7
  9.6 2.8 %collective-permute-start = (bf16[448,256]{1,0:T(8,128)(2,1)S(1)}, bf16[448,256]{1,0:T(8,128)(2,1)S(1)}, u32[]{:S(2)}, u32[]{:S(2)}) collective-permute-start(bf16[448,256]{1,0:T(8,128)(2,1)S(1)} %get-tuple-element.48), channel_id=1, source_target_pairs={{0,1},{1,2},{2,3},{3,4},{4,5},{5,6},{6,7},{8,9},{9,10},{10,11},{11... | collective-permute-start | bytes 688136 | tf_op jit(solution)/shard_map/ppermute | solution.py:305
  12.4 5.5 %collective-permute-start.1 = (bf16[448,256]{1,0:T(8,128)(2,1)S(1)}, bf16[448,256]{1,0:T(8,128)(2,1)S(1)}, u32[]{:S(2)}, u32[]{:S(2)}) collective-permute-start(bf16[448,256]{1,0:T(8,128)(2,1)S(1)} %get-tuple-element.49), channel_id=1, source_target_pairs={{1,0},{2,1},{3,2},{4,3},{5,4},{6,5},{7,6},{9,8},{10,9},{11,10},{12... | collective-permute-start | bytes 688136 | tf_op jit(solution)/shard_map/ppermute | solution.py:306
  17.9 4.5 %collective-permute-done.up = bf16[448,256]{1,0:T(8,128)(2,1)S(1)} collective-permute-done((bf16[448,256]{1,0:T(8,128)(2,1)S(1)}, bf16[448,256]{1,0:T(8,128)(2,1)S(1)}, u32[]{:S(2)}, u32[]{:S(2)}) %collective-permute-start) | collective-permute-done | bytes 229408 | tf_op jit(solution)/shard_map/ppermute | solution.py:305
  22.4 5.0 %collective-permute-done.1.down = bf16[448,256]{1,0:T(8,128)(2,1)S(1)} collective-permute-done((bf16[448,256]{1,0:T(8,128)(2,1)S(1)}, bf16[448,256]{1,0:T(8,128)(2,1)S(1)}, u32[]{:S(2)}, u32[]{:S(2)}) %collective-permute-start.1) | collective-permute-done | bytes 229408 | tf_op jit(solution)/shard_map/ppermute | solution.py:306
  27.4 6.5 %shard_map.59 = (bf16[656,256]{1,0:T(8,128)(2,1)S(1)}, bf16[656,256]{1,0:T(8,128)(2,1)S(1)}, f32[512,256]{1,0:T(8,128)S(1)}) custom-call(f32[4]{0:T(128)S(1)} %copy-done.4, bf16[448,256]{1,0:T(8,128)(2,1)S(1)} %collective-permute-done.up, f32[512,256]{1,0:T(8,128)S(1)} %bitcast.13, bf16[448,256]{1,0:T(8,128)(2,1)S(1)} %collective-permute-done.1.down, ...), custom_call_target="tpu_custom_call" | custom-call | flops 5133828096 | bytes 10027008 | tf_op jit(solution)/shard_map/pallas_call | solution.py:337
  33.9 1.3 collective-permute-start.3
  35.2 0.7 collective-permute-start.4
  35.9 0.0 collective-permute-done.5
  35.9 10.5 %collective-permute-start.2 = (bf16[656,256]{1,0:T(8,128)(2,1)S(1)}, bf16[656,256]{1,0:T(8,128)(2,1)S(1)}, u32[]{:S(2)}, u32[]{:S(2)}) collective-permute-start(bf16[656,256]{1,0:T(8,128)(2,1)S(1)} %get-tuple-element.51.refs_1_.refs_8_), channel_id=1, source_target_pairs={{0,8},{1,9},{2,10},{3,11},{4,12},{5,13},{6,14},{7,15},{16,24},{17,... | collective-permute-start | bytes 1007624 | tf_op jit(solution)/shard_map/ppermute | solution.py:347
  46.4 0.0 collective-permute-done.6
  46.4 0.6 pad_maximum_fusion.refs_4_.refs_11_
  47.1 0.6 collective-permute-done.2.refs_0_.refs_7_
  47.6 0.0 collective-permute-done.3.refs_2_.refs_9_
  47.6 0.0 collective-permute-done.4.refs_3_.refs_10_
  47.7 0.7 collective-permute-start.10
  48.4 0.7 collective-permute-start.8
  49.0 0.7 collective-permute-start.9
  49.7 0.0 collective-permute-done.8.refs_0_
  49.7 0.0 collective-permute-done.9.refs_1_
  49.8 0.1 shard_map.61
  49.8 0.7 collective-permute-start.11
  50.5 0.7 collective-permute-start.12
  51.2 0.7 collective-permute-start.13
  51.9 0.0 collective-permute-done.13.refs_2_
  51.9 0.3 shard_map.62
  52.2 0.7 collective-permute-start.14
  52.8 0.7 collective-permute-start.15
  53.5 0.7 collective-permute-start.16
  54.2 0.0 collective-permute-done.15.refs_1_
  54.2 0.0 collective-permute-done.16.refs_2_
  54.2 0.1 shard_map.63
  54.3 0.7 collective-permute-start.17
  55.0 0.7 collective-permute-start.18
  55.6 0.7 collective-permute-start.19
  56.4 0.1 shard_map.64
  56.4 0.7 collective-permute-start.20
  57.1 0.7 collective-permute-start.21
  57.8 0.7 collective-permute-start.22
  58.5 0.1 shard_map.65
  58.6 0.7 collective-permute-start.23
  59.3 0.7 collective-permute-start.24
  59.9 0.7 collective-permute-start.25
  60.6 0.3 shard_map.66
  60.9 0.7 collective-permute-start.26
  61.6 0.7 collective-permute-start.27
  62.3 0.7 collective-permute-start.28
  63.0 0.1 shard_map.67
  63.1 0.7 collective-permute-start.29
  63.8 0.7 collective-permute-start.30
  64.4 0.7 collective-permute-start.31
  65.1 1.3 collective-permute-start.32
  66.4 1.3 collective-permute-start.34
  67.7 1.3 collective-permute-start.33
  69.0 1.3 collective-permute-start.35
  70.3 68.7 %collective-permute-done.32.near = bf16[256,256]{1,0:T(8,128)(2,1)S(1)} collective-permute-done((bf16[256,256]{1,0:T(8,128)(2,1)S(1)}, bf16[256,256]{1,0:T(8,128)(2,1)S(1)}, u32[]{:S(2)}, u32[]{:S(2)}) %collective-permute-start.32) | collective-permute-done | bytes 131104 | tf_op jit(solution)/shard_map/ppermute | solution.py:390
  139.0 2.6 %collective-permute-done.33.far = bf16[256,256]{1,0:T(8,128)(2,1)S(1)} collective-permute-done((bf16[256,256]{1,0:T(8,128)(2,1)S(1)}, bf16[256,256]{1,0:T(8,128)(2,1)S(1)}, u32[]{:S(2)}, u32[]{:S(2)}) %collective-permute-start.33) | collective-permute-done | bytes 131104 | tf_op jit(solution)/shard_map/ppermute | solution.py:391
  141.7 0.3 collective-permute-done.34.halo_c
  142.0 5.5 %collective-permute-done.35.halo_d = bf16[256,256]{1,0:T(8,128)(2,1)S(1)} collective-permute-done((bf16[256,256]{1,0:T(8,128)(2,1)S(1)}, bf16[256,256]{1,0:T(8,128)(2,1)S(1)}, u32[]{:S(2)}, u32[]{:S(2)}) %collective-permute-start.35) | collective-permute-done | bytes 131104 | tf_op jit(solution)/shard_map/ppermute | solution.py:393
  147.5 5.3 %shard_map.68 = (f32[512,256]{1,0:T(8,128)}, f32[512,256]{1,0:T(8,128)}) custom-call(f32[4]{0:T(128)S(1)} %copy-done.4, f32[512,256]{1,0:T(8,128)S(1)} %bitcast.14, f32[512,256]{1,0:T(8,128)S(1)} %get-tuple-element.50.relaxed, bf16[256,256]{1,0:T(8,128)(2,1)S(1)} %get-tuple-element.88.mine, bf16[256,256]{1,0:T(8,128)(2,1)S(1)} %collective-permute-done.29.across, ...), custom_call_target="tpu_custom_call" | custom-call | flops 3321888768 | bytes 6488064 | tf_op jit(solution)/shard_map/pallas_call | solution.py:398
  (31 shorter events, 0.1 us)
Async XLA Ops:
  0.6 26.8 %copy-start.4 = (f32[4]{0:T(128)S(1)}, f32[4]{0:T(128)}, u32[]{:S(2)}) copy-start(f32[4]{0:T(128)} %steps.3) | copy-start | bytes 52
  0.6 2.3 %copy-start = (bf16[4,9,256,256]{3,2,1,0:T(8,128)(2,1)S(1)}, bf16[4,9,256,256]{3,2,1,0:T(8,128)(2,1)}, u32[]{:S(2)}) copy-start(bf16[4,9,256,256]{3,2,1,0:T(8,128)(2,1)} %param.5) | copy-start | bytes 14155780
  3.0 6.6 %copy-start.2 = (f32[1,1,8,64,256]{4,3,2,1,0:T(8,128)S(1)}, f32[1,1,8,64,256]{4,3,2,1,0:T(8,128)}, u32[]{:S(2)}) copy-start(f32[1,1,8,64,256]{4,3,2,1,0:T(8,128)} %param.4) | copy-start | bytes 1572868
  3.0 24.4 %copy-start.1 = (bf16[4,9,256,256]{3,2,1,0:T(8,128)(2,1)S(1)}, bf16[4,9,256,256]{3,2,1,0:T(8,128)(2,1)}, u32[]{:S(2)}) copy-start(bf16[4,9,256,256]{3,2,1,0:T(8,128)(2,1)} %param.5) | copy-start | bytes 14155780
  3.0 24.4 %copy-start.3 = (f32[4,256]{1,0:T(4,128)S(1)}, f32[4,256]{1,0:T(4,128)}, u32[]{:S(2)}) copy-start(f32[4,256]{1,0:T(4,128)} %biases.3) | copy-start | bytes 12292
  3.1 32.9 %collective-permute-start.5 = (bf16[2304,256]{1,0:T(8,128)(2,1)S(1)}, bf16[2304,256]{1,0:T(8,128)(2,1)S(1)}, u32[]{:S(2)}, u32[]{:S(2)}) collective-permute-start(bf16[2304,256]{1,0:T(8,128)(2,1)S(1)} %pick.1), channel_id=1, source_target_pairs={{0,8},{1,9},{2,10},{3,11},{4,12},{5,13},{6,14},{7,15},{16,24},{17,... | collective-permute-start | bytes 3538952 | tf_op jit(solution)/shard_map/ppermute | solution.py:334
  5.3 41.1 %collective-permute-start.6 = (bf16[2304,256]{1,0:T(8,128)(2,1)S(1)}, bf16[2304,256]{1,0:T(8,128)(2,1)S(1)}, u32[]{:S(2)}, u32[]{:S(2)}) collective-permute-start(bf16[2304,256]{1,0:T(8,128)(2,1)S(1)} %pick.1), channel_id=1, source_target_pairs={{16,8},{17,9},{18,10},{19,11},{20,12},{21,13},{22,14},{23,15},{1,2... | collective-permute-start | bytes 3538952 | tf_op jit(solution)/shard_map/ppermute | solution.py:332
  8.8 37.6 %collective-permute-start.7 = (bf16[2304,256]{1,0:T(8,128)(2,1)S(1)}, bf16[2304,256]{1,0:T(8,128)(2,1)S(1)}, u32[]{:S(2)}, u32[]{:S(2)}) collective-permute-start(bf16[2304,256]{1,0:T(8,128)(2,1)S(1)} %pick.1), channel_id=1, source_target_pairs={{8,24},{9,25},{10,26},{11,27},{12,28},{13,29},{14,30},{15,31},{24,... | collective-permute-start | bytes 3538952 | tf_op jit(solution)/shard_map/ppermute | solution.py:333
  9.6 12.8 %collective-permute-start = (bf16[448,256]{1,0:T(8,128)(2,1)S(1)}, bf16[448,256]{1,0:T(8,128)(2,1)S(1)}, u32[]{:S(2)}, u32[]{:S(2)}) collective-permute-start(bf16[448,256]{1,0:T(8,128)(2,1)S(1)} %get-tuple-element.48), channel_id=1, source_target_pairs={{0,1},{1,2},{2,3},{3,4},{4,5},{5,6},{6,7},{8,9},{9,10},{10,11},{11... | collective-permute-start | bytes 688136 | tf_op jit(solution)/shard_map/ppermute | solution.py:305
  12.4 15.0 %collective-permute-start.1 = (bf16[448,256]{1,0:T(8,128)(2,1)S(1)}, bf16[448,256]{1,0:T(8,128)(2,1)S(1)}, u32[]{:S(2)}, u32[]{:S(2)}) collective-permute-start(bf16[448,256]{1,0:T(8,128)(2,1)S(1)} %get-tuple-element.49), channel_id=1, source_target_pairs={{1,0},{2,1},{3,2},{4,3},{5,4},{6,5},{7,6},{9,8},{10,9},{11,10},{12... | collective-permute-start | bytes 688136 | tf_op jit(solution)/shard_map/ppermute | solution.py:306
  33.9 13.7 %collective-permute-start.3 = (bf16[656,256]{1,0:T(8,128)(2,1)S(1)}, bf16[656,256]{1,0:T(8,128)(2,1)S(1)}, u32[]{:S(2)}, u32[]{:S(2)}) collective-permute-start(bf16[656,256]{1,0:T(8,128)(2,1)S(1)} %get-tuple-element.52), channel_id=1, source_target_pairs={{0,24},{1,25},{2,26},{3,27},{4,28},{5,29},{6,30},{7,31},{16,8},{17... | collective-permute-start | bytes 1007624 | tf_op jit(solution)/shard_map/ppermute | solution.py:345
  35.2 12.4 %collective-permute-start.4 = (bf16[656,256]{1,0:T(8,128)(2,1)S(1)}, bf16[656,256]{1,0:T(8,128)(2,1)S(1)}, u32[]{:S(2)}, u32[]{:S(2)}) collective-permute-start(bf16[656,256]{1,0:T(8,128)(2,1)S(1)} %get-tuple-element.52), channel_id=1, source_target_pairs={{8,24},{9,25},{10,26},{11,27},{12,28},{13,29},{14,30},{15,31},{24,... | collective-permute-start | bytes 1007624 | tf_op jit(solution)/shard_map/ppermute | solution.py:346
  35.9 11.7 %collective-permute-start.2 = (bf16[656,256]{1,0:T(8,128)(2,1)S(1)}, bf16[656,256]{1,0:T(8,128)(2,1)S(1)}, u32[]{:S(2)}, u32[]{:S(2)}) collective-permute-start(bf16[656,256]{1,0:T(8,128)(2,1)S(1)} %get-tuple-element.51.refs_1_.refs_8_), channel_id=1, source_target_pairs={{0,8},{1,9},{2,10},{3,11},{4,12},{5,13},{6,14},{7,15},{16,24},{17,... | collective-permute-start | bytes 1007624 | tf_op jit(solution)/shard_map/ppermute | solution.py:347
  47.7 2.0 %collective-permute-start.10 = (bf16[256,256]{1,0:T(8,128)(2,1)S(1)}, bf16[256,256]{1,0:T(8,128)(2,1)S(1)}, u32[]{:S(2)}, u32[]{:S(2)}) collective-permute-start(bf16[256,256]{1,0:T(8,128)(2,1)S(1)} %get-tuple-element.53), channel_id=1, source_target_pairs={{24,40},{9,56},{25,41},{10,57},{26,42},{11,58},{27,43},{12,59},{28... | collective-permute-start | bytes 393224 | tf_op jit(solution)/shard_map/ppermute | solution.py:374
  48.4 1.4 collective-permute-start.8
  49.0 0.7 collective-permute-start.9
  49.8 2.0 %collective-permute-start.11 = (bf16[256,256]{1,0:T(8,128)(2,1)S(1)}, bf16[256,256]{1,0:T(8,128)(2,1)S(1)}, u32[]{:S(2)}, u32[]{:S(2)}) collective-permute-start(bf16[256,256]{1,0:T(8,128)(2,1)S(1)} %get-tuple-element.58), channel_id=1, source_target_pairs={{40,88},{56,73},{41,89},{57,74},{42,90},{58,75},{43,91},{59,76},{4... | collective-permute-start | bytes 393224 | tf_op jit(solution)/shard_map/ppermute | solution.py:374
  50.5 1.4 collective-permute-start.12
  51.2 0.7 collective-permute-start.13
  52.2 2.0 %collective-permute-start.14 = (bf16[256,256]{1,0:T(8,128)(2,1)S(1)}, bf16[256,256]{1,0:T(8,128)(2,1)S(1)}, u32[]{:S(2)}, u32[]{:S(2)}) collective-permute-start(bf16[256,256]{1,0:T(8,128)(2,1)S(1)} %get-tuple-element.63), channel_id=1, source_target_pairs={{72,120},{88,105},{73,121},{89,106},{74,122},{90,107},{75,123},{91... | collective-permute-start | bytes 393224 | tf_op jit(solution)/shard_map/ppermute | solution.py:374
  52.8 1.4 collective-permute-start.15
  53.5 0.7 collective-permute-start.16
  54.3 2.0 %collective-permute-start.17 = (bf16[256,256]{1,0:T(8,128)(2,1)S(1)}, bf16[256,256]{1,0:T(8,128)(2,1)S(1)}, u32[]{:S(2)}, u32[]{:S(2)}) collective-permute-start(bf16[256,256]{1,0:T(8,128)(2,1)S(1)} %get-tuple-element.68), channel_id=1, source_target_pairs={{104,152},{120,137},{105,153},{121,138},{106,154},{122,139},{107,1... | collective-permute-start | bytes 393224 | tf_op jit(solution)/shard_map/ppermute | solution.py:374
  55.0 1.4 collective-permute-start.18
  55.6 0.7 collective-permute-start.19
  56.4 2.0 %collective-permute-start.20 = (bf16[256,256]{1,0:T(8,128)(2,1)S(1)}, bf16[256,256]{1,0:T(8,128)(2,1)S(1)}, u32[]{:S(2)}, u32[]{:S(2)}) collective-permute-start(bf16[256,256]{1,0:T(8,128)(2,1)S(1)} %get-tuple-element.73), channel_id=1, source_target_pairs={{136,184},{152,169},{137,185},{153,170},{138,186},{154,171},{139,1... | collective-permute-start | bytes 393224 | tf_op jit(solution)/shard_map/ppermute | solution.py:374
  57.1 1.4 collective-permute-start.21
  57.8 0.7 collective-permute-start.22
  58.6 2.0 %collective-permute-start.23 = (bf16[256,256]{1,0:T(8,128)(2,1)S(1)}, bf16[256,256]{1,0:T(8,128)(2,1)S(1)}, u32[]{:S(2)}, u32[]{:S(2)}) collective-permute-start(bf16[256,256]{1,0:T(8,128)(2,1)S(1)} %get-tuple-element.78), channel_id=1, source_target_pairs={{168,216},{184,201},{169,217},{185,202},{170,218},{186,203},{171,2... | collective-permute-start | bytes 393224 | tf_op jit(solution)/shard_map/ppermute | solution.py:374
  59.3 1.4 collective-permute-start.24
  59.9 0.7 collective-permute-start.25
  60.9 2.0 %collective-permute-start.26 = (bf16[256,256]{1,0:T(8,128)(2,1)S(1)}, bf16[256,256]{1,0:T(8,128)(2,1)S(1)}, u32[]{:S(2)}, u32[]{:S(2)}) collective-permute-start(bf16[256,256]{1,0:T(8,128)(2,1)S(1)} %get-tuple-element.83), channel_id=1, source_target_pairs={{200,248},{216,233},{201,249},{217,234},{202,250},{218,235},{203,2... | collective-permute-start | bytes 393224 | tf_op jit(solution)/shard_map/ppermute | solution.py:374
  61.6 1.4 collective-permute-start.27
  62.3 0.7 collective-permute-start.28
  63.1 4.6 %collective-permute-start.29 = (bf16[256,256]{1,0:T(8,128)(2,1)S(1)}, bf16[256,256]{1,0:T(8,128)(2,1)S(1)}, u32[]{:S(2)}, u32[]{:S(2)}) collective-permute-start(bf16[256,256]{1,0:T(8,128)(2,1)S(1)} %get-tuple-element.89), channel_id=1, source_target_pairs={{8,24},{9,25},{10,26},{11,27},{12,28},{13,29},{14,30},{15,31},{24,... | collective-permute-start | bytes 393224 | tf_op jit(solution)/shard_map/ppermute | solution.py:394
  63.8 5.3 %collective-permute-start.30 = (bf16[256,256]{1,0:T(8,128)(2,1)S(1)}, bf16[256,256]{1,0:T(8,128)(2,1)S(1)}, u32[]{:S(2)}, u32[]{:S(2)}) collective-permute-start(bf16[256,256]{1,0:T(8,128)(2,1)S(1)} %get-tuple-element.88.mine), channel_id=1, source_target_pairs={{9,8},{24,25},{10,9},{25,26},{11,10},{26,27},{12,11},{27,28},{13,1... | collective-permute-start | bytes 393224 | tf_op jit(solution)/shard_map/ppermute | solution.py:395
  64.4 5.9 %collective-permute-start.31 = (bf16[256,256]{1,0:T(8,128)(2,1)S(1)}, bf16[256,256]{1,0:T(8,128)(2,1)S(1)}, u32[]{:S(2)}, u32[]{:S(2)}) collective-permute-start(bf16[256,256]{1,0:T(8,128)(2,1)S(1)} %get-tuple-element.89), channel_id=1, source_target_pairs={{9,24},{24,9},{10,25},{25,10},{11,26},{26,11},{12,27},{27,12},{13,... | collective-permute-start | bytes 393224 | tf_op jit(solution)/shard_map/ppermute | solution.py:396
  65.1 73.9 %collective-permute-start.32 = (bf16[256,256]{1,0:T(8,128)(2,1)S(1)}, bf16[256,256]{1,0:T(8,128)(2,1)S(1)}, u32[]{:S(2)}, u32[]{:S(2)}) collective-permute-start(bf16[256,256]{1,0:T(8,128)(2,1)S(1)} %get-tuple-element.90), channel_id=1, source_target_pairs={{8,0},{9,1},{10,2},{11,3},{12,4},{13,5},{14,6},{15,7},{24,16},{25,... | collective-permute-start | bytes 393224 | tf_op jit(solution)/shard_map/ppermute | solution.py:390
  66.4 75.6 %collective-permute-start.34 = (bf16[256,256]{1,0:T(8,128)(2,1)S(1)}, bf16[256,256]{1,0:T(8,128)(2,1)S(1)}, u32[]{:S(2)}, u32[]{:S(2)}) collective-permute-start(bf16[256,256]{1,0:T(8,128)(2,1)S(1)} %get-tuple-element.90), channel_id=1, source_target_pairs={{9,0},{24,17},{10,1},{25,18},{11,2},{26,19},{12,3},{27,20},{13,4},... | collective-permute-start | bytes 393224 | tf_op jit(solution)/shard_map/ppermute | solution.py:392
  67.7 73.9 %collective-permute-start.33 = (bf16[256,256]{1,0:T(8,128)(2,1)S(1)}, bf16[256,256]{1,0:T(8,128)(2,1)S(1)}, u32[]{:S(2)}, u32[]{:S(2)}) collective-permute-start(bf16[256,256]{1,0:T(8,128)(2,1)S(1)} %get-tuple-element.91), channel_id=1, source_target_pairs={{24,0},{25,1},{26,2},{27,3},{28,4},{29,5},{30,6},{31,7},{8,16},{9,... | collective-permute-start | bytes 393224 | tf_op jit(solution)/shard_map/ppermute | solution.py:391
  69.0 78.5 %collective-permute-start.35 = (bf16[256,256]{1,0:T(8,128)(2,1)S(1)}, bf16[256,256]{1,0:T(8,128)(2,1)S(1)}, u32[]{:S(2)}, u32[]{:S(2)}) collective-permute-start(bf16[256,256]{1,0:T(8,128)(2,1)S(1)} %get-tuple-element.91), channel_id=1, source_target_pairs={{9,16},{24,1},{10,17},{25,2},{11,18},{26,3},{12,19},{27,4},{13,20}... | collective-permute-start | bytes 393224 | tf_op jit(solution)/shard_map/ppermute | solution.py:393

commit v3 on v2

--- a/solution.py
+++ b/solution.py
@@ -100,7 +100,8 @@
 
 
 def first_kernel(
-    steps, up, own, down, weights, biases, same, other, relaxed, state, wide, gain
+    steps, up, own, down, weights, biases,
+    same, other0, other1, other2, other3, relaxed, state, wide, gain,
 ):
     plane, half, core, coarse = place()
     is_first = (plane == 0) & (half == 0) & (core == 0)
@@ -132,30 +133,45 @@
     pieces = split3(biases[0:1, :]) + split3(jnp.full((1, C), total_step, F32))
     pieces.append(jnp.zeros((EXTRA - len(pieces), C), F32))
     extra = jnp.concatenate(pieces, axis=0).astype(BF16)
-    for ref, side in ((same, half), (other, 1 - half)):
-        base = pl.multiple_of(side * (TILE * COLS), TILE * COLS)
-        ref[0 : SENT * COLS, :] = gain[pl.ds(base, SENT * COLS), :].astype(BF16)
-        ref[SENT * COLS :, :] = extra
+    sides = [(same, half, 0)]
+    sides += [(ref, 1 - half, k) for k, ref in enumerate((other0, other1, other2, other3))]
+    for ref, side, skip in sides:
+        rows = SENT - 2 * skip
+        base = pl.multiple_of(side * (TILE * COLS) + skip * COLS, COLS)
+        ref[0 : rows * COLS, :] = gain[pl.ds(base, rows * COLS), :].astype(BF16)
+        ref[rows * COLS :, :] = extra
+
+
+def pack_kernel(own, across, arrived, mine, theirs):
+    core = place()[2]
+
+    @pl.when(core == 1)
+    def _():
+        mine[...] = own[...]
+        theirs[...] = across[...]
+
+    @pl.when(core == 0)
+    def _():
+        mine[...] = arrived[: TILE * COLS, :]
+        theirs[...] = arrived[TILE * COLS :, :]
 
 
 def last_kernel(
-    steps, initial, relaxed, mine, across, halo_a, halo_b, near, far, halo_c, halo_d,
-    weights, biases, corrected, finished, state, wide,
+    steps, initial, relaxed, mine, across, halo_a, halo_b, weights, biases,
+    corrected, finished, state, wide,
 ):
     plane, half, core, coarse = place()
     is_first = (plane == 0) & (half == 0) & (core == 0)
-    north, lower = core == 1, half == 1
 
     def read(row):
         at = cells(row % TILE, 1)
-        a, b, c, d = (
-            (halo_a, halo_b, halo_c, halo_d),
-            (across, mine, far, near),
-            (mine, across, near, far),
-            (halo_b, halo_a, halo_d, halo_c),
+        lower, upper = (
+            (halo_a, halo_b),
+            (across, mine),
+            (mine, across),
+            (halo_b, halo_a),
         )[row // TILE]
-        a, b, c, d = (ref[at, :].astype(F32) for ref in (a, b, c, d))
-        values = jnp.where(north, jnp.where(lower, a, b), jnp.where(lower, c, d))
+        values = jnp.where(half == 1, lower[at, :].astype(F32), upper[at, :].astype(F32))
         if TILE <= row < TILE + OWN:
             to = cells(row - TILE, 1)
             corrected[to, :] = jnp.where(is_first, initial[to, :], values)
@@ -173,18 +189,30 @@
     refs = list(refs)
     entering = None if turn == 0 else [refs.pop(0) for _ in range(3)]
     before = None if turn == 0 else [refs.pop(0) for _ in range(GROUP)]
-    defects = [refs.pop(0) for _ in range(GROUP)]
+    near, own_defect, *others = [refs.pop(0) for _ in range(2 + GROUP)]
+    sources = [(near, others[0]), (own_defect, others[1]), (others[2], near), (others[3], own_defect)]
     weights = refs.pop(0)
     following = None if turn == PLANES - 1 else refs.pop(0)
-    passed = [refs.pop(0) for _ in range(GROUP)]
+    if turn == PLANES - 1:
+        to_south = refs.pop(0)
+        near_part, far_part = to_south.at[: TILE * COLS, :], to_south.at[TILE * COLS :, :]
+        own_part, across_part = refs.pop(0), refs.pop(0)
+        passed = [near_part, own_part, far_part, across_part]
+    else:
+        passed = [refs.pop(0) for _ in range(GROUP)]
     state, wide, hold = refs
     plane, half, core, coarse = place()
     first_row = (coarse * 2 + half) * TILE - TILE
     active = (plane == turn) & (core == 1)
 
-    def defect(step, at):
-        a, b = defects[step][at, :].astype(F32), defects[step ^ 2][at, :].astype(F32)
-        return jnp.where(half == 0, a, b)
+    def defect(step, row, rows, cut=1):
+        picked = []
+        for at_half in range(2):
+            ref = sources[step][at_half]
+            skip = step if any(ref is other for other in others) else 0
+            start = (row - skip) * COLS if cut else (SENT - 2 * skip) * COLS
+            picked.append(ref[pl.ds(start, rows), :].astype(F32))
+        return jnp.where(half == 0, picked[0], picked[1])
 
     def keep(step, row, values):
         hold[step, cells(row - TILE, 1), :] = values.astype(BF16)
@@ -201,7 +229,7 @@
         if turn == 0:
             hold[0] = jnp.zeros(hold.shape[1:], BF16)
             for row in range(1, 1 + SENT):
-                values = defect(0, cells(row - 1, 1))
+                values = defect(0, row - 1, COLS)
                 if TILE <= row < 2 * TILE:
                     keep(1, row, values)
                 else:
@@ -217,7 +245,7 @@
                     keep(0, row, values)
         final = GROUP - 1 if turn == PLANES - 1 else GROUP
         for step in range(1 if turn == 0 else 0, final):
-            extra = defect(step, pl.ds(SENT * COLS, EXTRA))
+            extra = defect(step, 0, EXTRA, cut=0)
             bias = extra[0:1, :] + extra[1:2, :] + extra[2:3, :]
             scale = extra[3:4, :] + extra[4:5, :] + extra[5:6, :]
             kernel = weights[jnp.bitwise_xor(step, 2 * half)]
@@ -227,7 +255,7 @@
                     row = start + i + step + 1
                     piece = slope[i * COLS : (i + 1) * COLS, :]
                     values = state[cells(row, 1), :] + scale * piece
-                    values = values + defect(step, cells(row - 1, 1))
+                    values = values + defect(step, row - 1, COLS)
                     if not TILE <= row < 2 * TILE:
                         values = values * inside(first_row + row)
                     elif step == GROUP - 1:
@@ -321,38 +349,43 @@
         lambda p, h, c: (device(p, h, 1, c), device(p, 1 - h, 1, c))
     )
 
-    def from_right(p, h, c):
-        half, coarse = beside(h, c, 1)
-        return device(p, half, 0, coarse), device(p, h, 1, c)
-
-    def from_left(p, h, c):
-        half, coarse = beside(h, c, 1)
-        return device(p, h, 1, c), device(p, half, 1, coarse)
-
-    far_south = lax.ppermute(kernel, AXES, within_plane(from_right))
-    far_north = lax.ppermute(kernel, AXES, within_plane(from_left))
+    def from_next_pair(p, h, c):
+        half, coarse = beside(h, c, 1 if h else -1)
+        return device(p, half, 1, coarse), device(p, h, 1, c)
+
+    unused = {device(0, 0, 0, c) for c in range(8)}
+    pairs = [pair for pair in to_other_north if pair[0] not in unused]
+    far_south = lax.ppermute(kernel, AXES, pairs)
+    far_north = lax.ppermute(kernel, AXES, within_plane(from_next_pair))
     near_south = lax.ppermute(kernel, AXES, to_north)
 
-    message = shape(SENT * COLS + EXTRA)
-    same, other, relaxed = call(
+    messages = [shape((SENT - 2 * k) * COLS + EXTRA) for k in (0, 0, 1, 2, 3)]
+    same, *others, relaxed = call(
         first_kernel,
         68,
         OWN + 2 * DEPTH,
-        (message, message, shape(OWN * COLS, F32)),
+        (*messages, shape(OWN * COLS, F32)),
         [SMEM] + [VMEM] * 5,
         (pltpu.VMEM((WIDE * COLS, C), F32),),
     )(step_sizes, above, initial, below, kernels, biases)
-    other_south = lax.ppermute(other, AXES, to_other_north)
-    other_north = lax.ppermute(other, AXES, north_to_north)
+    defects = []
+    for k in range(GROUP):
+        half, core = k // 2, k % 2
+        pairs = [
+            (device(p, half, core, c), device(p, 1 - half, 1, c))
+            for p in range(PLANES)
+            for c in range(8)
+        ]
+        defects.append(lax.ppermute(others[k], AXES, pairs))
     same_south = lax.ppermute(same, AXES, to_north)
-    defects = [same_south, same, other_south, other_north]
+    defects = [same_south, same, *defects]
     chain_kernels = jnp.stack([near_south, kernel, far_south, far_north])
 
     block = shape(TILE * COLS)
     entering, passed = [], []
     for turn in range(PLANES):
         last = turn == PLANES - 1
-        outs = (block,) * (GROUP if last else GROUP + 1)
+        outs = (shape(2 * TILE * COLS), block, block) if last else (block,) * (GROUP + 1)
         operands = [*entering, *passed, *defects, chain_kernels]
         results = call(
             functools.partial(chain_kernel, turn),
@@ -362,8 +395,8 @@
             [VMEM] * len(operands),
             (pltpu.VMEM((GROUP, TILE * COLS, C), BF16),),
         )(*operands)
-        passed = results[-GROUP:]
         if not last:
+            passed = results[-GROUP:]
             entering = []
             for by in (1, 0, -1):
                 pairs = [
@@ -373,34 +406,44 @@
                 ]
                 entering.append(lax.ppermute(results[0], AXES, pairs))
 
-    near_state, own_state, far_state, across_state = passed
-
-    def halos(to_same, to_other_core):
+    to_south, own_state, across_state = results
+    arrived = lax.ppermute(to_south, AXES, [(b, a) for a, b in to_north])
+    mine, theirs = pl.pallas_call(
+        pack_kernel,
+        name="pack",
+        out_shape=(block, block),
+        in_specs=[VMEM] * 3,
+        out_specs=(VMEM, VMEM),
+        compiler_params=pltpu.CompilerParams(vmem_limit_bytes=8 * 2**20),
+    )(own_state, across_state, arrived)
+
+    def halos(half_of_lower):
         pairs = []
         for plane in range(PLANES):
-            for coarse in range(8):
-                if coarse > 0:
-                    dest = device(plane, to_same, to_other_core, coarse)
-                    pairs.append((device(plane, 1, 1, coarse - 1), dest))
-                if coarse < 7:
-                    dest = device(plane, 1 - to_same, to_other_core, coarse)
-                    pairs.append((device(plane, 0, 1, coarse + 1), dest))
+            for core in range(2):
+                for coarse in range(8):
+                    if coarse > 0:
+                        dest = device(plane, half_of_lower, core, coarse)
+                        pairs.append((device(plane, 1, core, coarse - 1), dest))
+                    if coarse < 7:
+                        dest = device(plane, 1 - half_of_lower, core, coarse)
+                        pairs.append((device(plane, 0, core, coarse + 1), dest))
         return pairs
 
-    near = lax.ppermute(near_state, AXES, [(b, a) for a, b in to_north])
-    far = lax.ppermute(far_state, AXES, [(b, a) for a, b in to_other_north])
-    halo_c = lax.ppermute(near_state, AXES, halos(1, 0))
-    halo_d = lax.ppermute(far_state, AXES, halos(0, 0))
-    across = lax.ppermute(across_state, AXES, north_to_north)
-    halo_a = lax.ppermute(own_state, AXES, halos(1, 1))
-    halo_b = lax.ppermute(across_state, AXES, halos(0, 1))
+    halo_a = lax.ppermute(mine, AXES, halos(1))
+    halo_b = lax.ppermute(theirs, AXES, halos(0))
+    swap = [
+        (device(p, h, core, c), device(p, 1 - h, core, c))
+        for p in range(PLANES)
+        for h in range(2)
+        for core in range(2)
+        for c in range(8)
+    ]
+    across = lax.ppermute(theirs, AXES, swap)
     result = shape(OWN * COLS, F32)
     corrected, finished = call(
-        last_kernel, 44, OWN + 2 * LAYERS, (result, result), [SMEM] + [VMEM] * 12
-    )(
-        step_sizes, initial, relaxed, own_state, across, halo_a, halo_b,
-        near, far, halo_c, halo_d, kernels, biases,
-    )
+        last_kernel, 44, OWN + 2 * LAYERS, (result, result), [SMEM] + [VMEM] * 8
+    )(step_sizes, initial, relaxed, mine, across, halo_a, halo_b, kernels, biases)
     return (
         corrected.reshape(start_states.shape),
         finished.reshape(start_states.shape),

time: 153 us -> 144 us (0.941)
  the two profiles are of different devices: /device:TPU:232 before, /device:TPU:248 now
where the time goes in v3:
time: 144 us
  waiting for transfers between devices  81.5 us (57%)
  starting transfers between devices  45.5 us (32%)
  Pallas kernels  12.4 us (9%)
  local copies, waits for them, and re-layouts  2.35 us (2%)
    ppermute x1, waiting for transfers between devices, local(): arrived = lax.ppermute(to_south, AXES, [(b, a) for a, b in to_north])  60.2 us
    ppermute x21, starting transfers between devices, local(): entering.append(lax.ppermute(results[0], AXES, pairs))  14 us
    ppermute x1, waiting for transfers between devices, local(): above = lax.ppermute(to_below, 'coarse', downward)  13.6 us
    pallas_call x1, Pallas kernels, local(): call(first_kernel, 68, OWN + 2 * DEPTH, (*messages, shape(OWN * COLS, F32...  6.3 us
    ppermute x1, starting transfers between devices, local(): far_south = lax.ppermute(kernel, AXES, pairs)  5.42 us
    pallas_call x1, Pallas kernels, local(): call(last_kernel, 44, OWN + 2 * LAYERS, (result, result), [SMEM] + [VMEM]...  5.01 us
    ppermute x1, starting transfers between devices, local(): halo_b = lax.ppermute(theirs, AXES, halos(0))  4.87 us
    ppermute x1, starting transfers between devices, local(): below = lax.ppermute(to_above, 'coarse', upward)  4.72 us
  transfers between devices with their start and end apart: 35, of which 6 were waited for; matrix products, arithmetic and copies ran while one was open for 0% of the time, Pallas kernels for 4%

profile of v3, /device:TPU:248, one launch (start us, length us, event | category | flops | bytes accessed | tf_op | source)
XLA Modules:
  0.0 143.6 jit_solution(695389431358123551)
XLA Ops:
  0.7 2.3 %copy-done = bf16[4,9,256,256]{3,2,1,0:T(8,128)(2,1)S(1)} copy-done((bf16[4,9,256,256]{3,2,1,0:T(8,128)(2,1)S(1)}, bf16[4,9,256,256]{3,2,1,0:T(8,128)(2,1)}, u32[]{:S(2)}) %copy-start) | copy-done | bytes 4718616
  3.0 0.1 pick.1
  3.1 0.9 collective-permute-start.9
  3.9 5.4 %collective-permute-start.8 = (bf16[2304,256]{1,0:T(8,128)(2,1)S(1)}, bf16[2304,256]{1,0:T(8,128)(2,1)S(1)}, u32[]{:S(2)}, u32[]{:S(2)}) collective-permute-start(bf16[2304,256]{1,0:T(8,128)(2,1)S(1)} %pick.1), channel_id=1, source_target_pairs={{16,8},{17,9},{18,10},{19,11},{20,12},{21,13},{22,14},{23,15},{32,... | collective-permute-start | bytes 3538952 | tf_op jit(solution)/shard_map/ppermute | solution.py:358
  9.4 1.5 %collective-permute-start.7 = (bf16[2304,256]{1,0:T(8,128)(2,1)S(1)}, bf16[2304,256]{1,0:T(8,128)(2,1)S(1)}, u32[]{:S(2)}, u32[]{:S(2)}) collective-permute-start(bf16[2304,256]{1,0:T(8,128)(2,1)S(1)} %pick.1), channel_id=1, source_target_pairs={{0,8},{1,9},{2,10},{3,11},{4,12},{5,13},{6,14},{7,15},{16,24},{17,... | collective-permute-start | bytes 3538952 | tf_op jit(solution)/shard_map/ppermute | solution.py:360
  10.9 3.5 %collective-permute-start = (bf16[448,256]{1,0:T(8,128)(2,1)S(1)}, bf16[448,256]{1,0:T(8,128)(2,1)S(1)}, u32[]{:S(2)}, u32[]{:S(2)}) collective-permute-start(bf16[448,256]{1,0:T(8,128)(2,1)S(1)} %get-tuple-element.52), channel_id=1, source_target_pairs={{0,1},{1,2},{2,3},{3,4},{4,5},{5,6},{6,7},{8,9},{9,10},{10,11},{11... | collective-permute-start | bytes 688136 | tf_op jit(solution)/shard_map/ppermute | solution.py:333
  14.4 4.7 %collective-permute-start.1 = (bf16[448,256]{1,0:T(8,128)(2,1)S(1)}, bf16[448,256]{1,0:T(8,128)(2,1)S(1)}, u32[]{:S(2)}, u32[]{:S(2)}) collective-permute-start(bf16[448,256]{1,0:T(8,128)(2,1)S(1)} %get-tuple-element.53), channel_id=1, source_target_pairs={{1,0},{2,1},{3,2},{4,3},{5,4},{6,5},{7,6},{9,8},{10,9},{11,10},{12... | collective-permute-start | bytes 688136 | tf_op jit(solution)/shard_map/ppermute | solution.py:334
  19.2 13.6 %collective-permute-done.up = bf16[448,256]{1,0:T(8,128)(2,1)S(1)} collective-permute-done((bf16[448,256]{1,0:T(8,128)(2,1)S(1)}, bf16[448,256]{1,0:T(8,128)(2,1)S(1)}, u32[]{:S(2)}, u32[]{:S(2)}) %collective-permute-start) | collective-permute-done | bytes 229408 | tf_op jit(solution)/shard_map/ppermute | solution.py:333
  32.7 0.1 collective-permute-done.1.down
  32.8 6.3 %shard_map.59 = (bf16[656,256]{1,0:T(8,128)(2,1)S(1)}, bf16[656,256]{1,0:T(8,128)(2,1)S(1)}, bf16[528,256]{1,0:T(8,128)(2,1)S(1)}, bf16[400,256]{1,0:T(8,128)(2,...) custom-call(f32[4]{0:T(128)S(1)} %copy-done.4, bf16[448,256]{1,0:T(8,128)(2,1)S(1)} %collective-permute-done.up, ...), custom_call_target="tpu_custom_call" | custom-call | flops 5133828096 | bytes 10027008 | tf_op jit(solution)/shard_map/pallas_call | solution.py:363
  39.2 0.7 collective-permute-start.6
  39.8 0.7 collective-permute-start.5
  40.5 0.0 collective-permute-done.9
  40.5 0.7 collective-permute-start.4
  41.2 0.0 collective-permute-done.8
  41.2 1.3 collective-permute-start.3
  42.5 0.0 collective-permute-done.7
  42.5 1.3 collective-permute-start.2
  43.9 0.6 pad_maximum_fusion.refs_6_.refs_13_
  44.5 0.0 collective-permute-done.6.refs_5_.refs_12_
  44.5 2.6 %collective-permute-done.3.refs_2_.refs_9_ = bf16[656,256]{1,0:T(8,128)(2,1)S(1)} collective-permute-done((bf16[656,256]{1,0:T(8,128)(2,1)S(1)}, bf16[656,256]{1,0:T(8,128)(2,1)S(1)}, u32[]{:S(2)}, u32[]{:S(2)}) %collective-permute-start.3) | collective-permute-done | bytes 335904 | tf_op jit(solution)/shard_map/ppermute | solution.py:379
  47.2 0.0 collective-permute-done.2.refs_0_.refs_7_
  47.2 0.7 collective-permute-start.12
  47.9 0.7 collective-permute-start.11
  48.6 0.7 collective-permute-start.10
  49.3 0.0 collective-permute-done.12.refs_2_
  49.3 0.0 collective-permute-done.11.refs_1_
  49.3 0.1 shard_map.61
  49.4 0.7 collective-permute-start.15
  50.0 0.7 collective-permute-start.14
  50.7 0.7 collective-permute-start.13
  51.4 0.0 collective-permute-done.15.refs_2_
  51.4 0.3 shard_map.62
  51.7 0.7 collective-permute-start.18
  52.4 0.7 collective-permute-start.17
  53.0 0.7 collective-permute-start.16
  53.7 0.0 collective-permute-done.17.refs_1_
  53.7 0.0 collective-permute-done.16.refs_0_
  53.8 0.1 shard_map.63
  53.8 0.7 collective-permute-start.21
  54.5 0.7 collective-permute-start.20
  55.2 0.7 collective-permute-start.19
  55.9 0.0 collective-permute-done.21.refs_2_
  55.9 0.1 shard_map.64
  56.0 0.7 collective-permute-start.24
  56.7 0.7 collective-permute-start.23
  57.3 0.7 collective-permute-start.22
  58.0 0.1 shard_map.65
  58.1 0.7 collective-permute-start.27
  58.8 0.7 collective-permute-start.26
  59.5 0.7 collective-permute-start.25
  60.2 0.3 shard_map.66
  60.5 0.7 collective-permute-start.30
  61.2 0.7 collective-permute-start.29
  61.8 0.7 collective-permute-start.28
  62.5 0.1 shard_map.67
  62.6 1.3 collective-permute-start.31
  63.9 60.2 %collective-permute-done.31.arrived = bf16[512,256]{1,0:T(8,128)(2,1)S(1)} collective-permute-done((bf16[512,256]{1,0:T(8,128)(2,1)S(1)}, bf16[512,256]{1,0:T(8,128)(2,1)S(1)}, u32[]{:S(2)}, u32[]{:S(2)}) %collective-permute-start.31) | collective-permute-done | bytes 262176 | tf_op jit(solution)/shard_map/ppermute | solution.py:410
  124.1 4.6 %collective-permute-start.33 = (bf16[256,256]{1,0:T(8,128)(2,1)S(1)}, bf16[256,256]{1,0:T(8,128)(2,1)S(1)}, u32[]{:S(2)}, u32[]{:S(2)}) collective-permute-start(bf16[256,256]{1,0:T(8,128)(2,1)S(1)} %get-tuple-element.98.mine), channel_id=1, source_target_pairs={{1,0},{16,17},{2,1},{17,18},{3,2},{18,19},{4,3},{19,20},{5,4},{20,... | collective-permute-start | bytes 393224 | tf_op jit(solution)/shard_map/ppermute | solution.py:433
  128.7 4.9 %collective-permute-start.34 = (bf16[256,256]{1,0:T(8,128)(2,1)S(1)}, bf16[256,256]{1,0:T(8,128)(2,1)S(1)}, u32[]{:S(2)}, u32[]{:S(2)}) collective-permute-start(bf16[256,256]{1,0:T(8,128)(2,1)S(1)} %get-tuple-element.99), channel_id=1, source_target_pairs={{1,16},{16,1},{2,17},{17,2},{3,18},{18,3},{4,19},{19,4},{5,20},{20... | collective-permute-start | bytes 393224 | tf_op jit(solution)/shard_map/ppermute | solution.py:434
  133.5 0.1 collective-permute-start.32
  133.7 4.3 %collective-permute-done.34.halo_b = bf16[256,256]{1,0:T(8,128)(2,1)S(1)} collective-permute-done((bf16[256,256]{1,0:T(8,128)(2,1)S(1)}, bf16[256,256]{1,0:T(8,128)(2,1)S(1)}, u32[]{:S(2)}, u32[]{:S(2)}) %collective-permute-start.34) | collective-permute-done | bytes 131104 | tf_op jit(solution)/shard_map/ppermute | solution.py:434
  137.9 0.7 collective-permute-done.32.across
  138.6 5.0 %shard_map.68 = (f32[512,256]{1,0:T(8,128)}, f32[512,256]{1,0:T(8,128)}) custom-call(f32[4]{0:T(128)S(1)} %copy-done.4, f32[512,256]{1,0:T(8,128)S(1)} %bitcast.14, f32[512,256]{1,0:T(8,128)S(1)} %get-tuple-element.54.relaxed, bf16[256,256]{1,0:T(8,128)(2,1)S(1)} %get-tuple-element.98.mine, bf16[256,256]{1,0:T(8,128)(2,1)S(1)} %collective-permute-done.32.across, ...), custom_call_target="tpu_custom_call" | custom-call | flops 3321888768 | bytes 6488064 | tf_op jit(solution)/shard_map/pallas_call | solution.py:444
  (30 shorter events, 0.2 us)
Async XLA Ops:
  0.6 32.2 %copy-start.4 = (f32[4]{0:T(128)S(1)}, f32[4]{0:T(128)}, u32[]{:S(2)}) copy-start(f32[4]{0:T(128)} %steps.3) | copy-start | bytes 52
  0.6 2.3 %copy-start = (bf16[4,9,256,256]{3,2,1,0:T(8,128)(2,1)S(1)}, bf16[4,9,256,256]{3,2,1,0:T(8,128)(2,1)}, u32[]{:S(2)}) copy-start(bf16[4,9,256,256]{3,2,1,0:T(8,128)(2,1)} %param.5) | copy-start | bytes 14155780
  3.0 7.9 %copy-start.2 = (f32[1,1,8,64,256]{4,3,2,1,0:T(8,128)S(1)}, f32[1,1,8,64,256]{4,3,2,1,0:T(8,128)}, u32[]{:S(2)}) copy-start(f32[1,1,8,64,256]{4,3,2,1,0:T(8,128)} %param.4) | copy-start | bytes 1572868
  3.0 29.9 %copy-start.1 = (bf16[4,9,256,256]{3,2,1,0:T(8,128)(2,1)S(1)}, bf16[4,9,256,256]{3,2,1,0:T(8,128)(2,1)}, u32[]{:S(2)}) copy-start(bf16[4,9,256,256]{3,2,1,0:T(8,128)(2,1)} %param.5) | copy-start | bytes 14155780
  3.0 29.9 %copy-start.3 = (f32[4,256]{1,0:T(4,128)S(1)}, f32[4,256]{1,0:T(4,128)}, u32[]{:S(2)}) copy-start(f32[4,256]{1,0:T(4,128)} %biases.3) | copy-start | bytes 12292
  3.1 37.4 %collective-permute-start.9 = (bf16[2304,256]{1,0:T(8,128)(2,1)S(1)}, bf16[2304,256]{1,0:T(8,128)(2,1)S(1)}, u32[]{:S(2)}, u32[]{:S(2)}) collective-permute-start(bf16[2304,256]{1,0:T(8,128)(2,1)S(1)} %pick.1), channel_id=1, source_target_pairs={{25,8},{24,9},{27,10},{26,11},{29,12},{28,13},{31,14},{30,15},{9,2... | collective-permute-start | bytes 3538952 | tf_op jit(solution)/shard_map/ppermute | solution.py:359
  3.9 37.3 %collective-permute-start.8 = (bf16[2304,256]{1,0:T(8,128)(2,1)S(1)}, bf16[2304,256]{1,0:T(8,128)(2,1)S(1)}, u32[]{:S(2)}, u32[]{:S(2)}) collective-permute-start(bf16[2304,256]{1,0:T(8,128)(2,1)S(1)} %pick.1), channel_id=1, source_target_pairs={{16,8},{17,9},{18,10},{19,11},{20,12},{21,13},{22,14},{23,15},{32,... | collective-permute-start | bytes 3538952 | tf_op jit(solution)/shard_map/ppermute | solution.py:358
  9.4 33.2 %collective-permute-start.7 = (bf16[2304,256]{1,0:T(8,128)(2,1)S(1)}, bf16[2304,256]{1,0:T(8,128)(2,1)S(1)}, u32[]{:S(2)}, u32[]{:S(2)}) collective-permute-start(bf16[2304,256]{1,0:T(8,128)(2,1)S(1)} %pick.1), channel_id=1, source_target_pairs={{0,8},{1,9},{2,10},{3,11},{4,12},{5,13},{6,14},{7,15},{16,24},{17,... | collective-permute-start | bytes 3538952 | tf_op jit(solution)/shard_map/ppermute | solution.py:360
  10.9 21.8 %collective-permute-start = (bf16[448,256]{1,0:T(8,128)(2,1)S(1)}, bf16[448,256]{1,0:T(8,128)(2,1)S(1)}, u32[]{:S(2)}, u32[]{:S(2)}) collective-permute-start(bf16[448,256]{1,0:T(8,128)(2,1)S(1)} %get-tuple-element.52), channel_id=1, source_target_pairs={{0,1},{1,2},{2,3},{3,4},{4,5},{5,6},{6,7},{8,9},{9,10},{10,11},{11... | collective-permute-start | bytes 688136 | tf_op jit(solution)/shard_map/ppermute | solution.py:333
  14.4 18.4 %collective-permute-start.1 = (bf16[448,256]{1,0:T(8,128)(2,1)S(1)}, bf16[448,256]{1,0:T(8,128)(2,1)S(1)}, u32[]{:S(2)}, u32[]{:S(2)}) collective-permute-start(bf16[448,256]{1,0:T(8,128)(2,1)S(1)} %get-tuple-element.53), channel_id=1, source_target_pairs={{1,0},{2,1},{3,2},{4,3},{5,4},{6,5},{7,6},{9,8},{10,9},{11,10},{12... | collective-permute-start | bytes 688136 | tf_op jit(solution)/shard_map/ppermute | solution.py:334
  39.2 5.4 %collective-permute-start.6 = (bf16[272,256]{1,0:T(8,128)(2,1)S(1)}, bf16[272,256]{1,0:T(8,128)(2,1)S(1)}, u32[]{:S(2)}, u32[]{:S(2)}) collective-permute-start(bf16[272,256]{1,0:T(8,128)(2,1)S(1)} %get-tuple-element.59), channel_id=1, source_target_pairs={{24,8},{25,9},{26,10},{27,11},{28,12},{29,13},{30,14},{31,15},{56,... | collective-permute-start | bytes 417800 | tf_op jit(solution)/shard_map/ppermute | solution.py:379
  39.8 4.7 %collective-permute-start.5 = (bf16[400,256]{1,0:T(8,128)(2,1)S(1)}, bf16[400,256]{1,0:T(8,128)(2,1)S(1)}, u32[]{:S(2)}, u32[]{:S(2)}) collective-permute-start(bf16[400,256]{1,0:T(8,128)(2,1)S(1)} %get-tuple-element.58), channel_id=1, source_target_pairs={{16,8},{17,9},{18,10},{19,11},{20,12},{21,13},{22,14},{23,15},{48,... | collective-permute-start | bytes 614408 | tf_op jit(solution)/shard_map/ppermute | solution.py:379
  40.5 4.0 %collective-permute-start.4 = (bf16[528,256]{1,0:T(8,128)(2,1)S(1)}, bf16[528,256]{1,0:T(8,128)(2,1)S(1)}, u32[]{:S(2)}, u32[]{:S(2)}) collective-permute-start(bf16[528,256]{1,0:T(8,128)(2,1)S(1)} %get-tuple-element.57), channel_id=1, source_target_pairs={{8,24},{9,25},{10,26},{11,27},{12,28},{13,29},{14,30},{15,31},{40,... | collective-permute-start | bytes 811016 | tf_op jit(solution)/shard_map/ppermute | solution.py:379
  41.2 6.0 %collective-permute-start.3 = (bf16[656,256]{1,0:T(8,128)(2,1)S(1)}, bf16[656,256]{1,0:T(8,128)(2,1)S(1)}, u32[]{:S(2)}, u32[]{:S(2)}) collective-permute-start(bf16[656,256]{1,0:T(8,128)(2,1)S(1)} %get-tuple-element.56), channel_id=1, source_target_pairs={{0,24},{1,25},{2,26},{3,27},{4,28},{5,29},{6,30},{7,31},{32,56},{3... | collective-permute-start | bytes 1007624 | tf_op jit(solution)/shard_map/ppermute | solution.py:379
  42.5 4.6 %collective-permute-start.2 = (bf16[656,256]{1,0:T(8,128)(2,1)S(1)}, bf16[656,256]{1,0:T(8,128)(2,1)S(1)}, u32[]{:S(2)}, u32[]{:S(2)}) collective-permute-start(bf16[656,256]{1,0:T(8,128)(2,1)S(1)} %get-tuple-element.55.refs_1_.refs_8_), channel_id=1, source_target_pairs={{0,8},{1,9},{2,10},{3,11},{4,12},{5,13},{6,14},{7,15},{16,24},{17,... | collective-permute-start | bytes 1007624 | tf_op jit(solution)/shard_map/ppermute | solution.py:380
  47.2 2.0 %collective-permute-start.12 = (bf16[256,256]{1,0:T(8,128)(2,1)S(1)}, bf16[256,256]{1,0:T(8,128)(2,1)S(1)}, u32[]{:S(2)}, u32[]{:S(2)}) collective-permute-start(bf16[256,256]{1,0:T(8,128)(2,1)S(1)} %get-tuple-element.60), channel_id=1, source_target_pairs={{24,40},{9,56},{25,41},{10,57},{26,42},{11,58},{27,43},{12,59},{28... | collective-permute-start | bytes 393224 | tf_op jit(solution)/shard_map/ppermute | solution.py:407
  47.9 1.4 collective-permute-start.11
  48.6 0.7 collective-permute-start.10
  49.4 2.0 %collective-permute-start.15 = (bf16[256,256]{1,0:T(8,128)(2,1)S(1)}, bf16[256,256]{1,0:T(8,128)(2,1)S(1)}, u32[]{:S(2)}, u32[]{:S(2)}) collective-permute-start(bf16[256,256]{1,0:T(8,128)(2,1)S(1)} %get-tuple-element.65), channel_id=1, source_target_pairs={{56,72},{41,88},{57,73},{42,89},{58,74},{43,90},{59,75},{44,91},{6... | collective-permute-start | bytes 393224 | tf_op jit(solution)/shard_map/ppermute | solution.py:407
  50.0 1.4 collective-permute-start.14
  50.7 0.7 collective-permute-start.13
  51.7 2.0 %collective-permute-start.18 = (bf16[256,256]{1,0:T(8,128)(2,1)S(1)}, bf16[256,256]{1,0:T(8,128)(2,1)S(1)}, u32[]{:S(2)}, u32[]{:S(2)}) collective-permute-start(bf16[256,256]{1,0:T(8,128)(2,1)S(1)} %get-tuple-element.70), channel_id=1, source_target_pairs={{88,104},{73,120},{89,105},{74,121},{90,106},{75,122},{91,107},{76... | collective-permute-start | bytes 393224 | tf_op jit(solution)/shard_map/ppermute | solution.py:407
  52.4 1.4 collective-permute-start.17
  53.0 0.7 collective-permute-start.16
  53.8 2.0 %collective-permute-start.21 = (bf16[256,256]{1,0:T(8,128)(2,1)S(1)}, bf16[256,256]{1,0:T(8,128)(2,1)S(1)}, u32[]{:S(2)}, u32[]{:S(2)}) collective-permute-start(bf16[256,256]{1,0:T(8,128)(2,1)S(1)} %get-tuple-element.75), channel_id=1, source_target_pairs={{120,136},{105,152},{121,137},{106,153},{122,138},{107,154},{123,1... | collective-permute-start | bytes 393224 | tf_op jit(solution)/shard_map/ppermute | solution.py:407
  54.5 1.4 collective-permute-start.20
  55.2 0.7 collective-permute-start.19
  56.0 2.0 %collective-permute-start.24 = (bf16[256,256]{1,0:T(8,128)(2,1)S(1)}, bf16[256,256]{1,0:T(8,128)(2,1)S(1)}, u32[]{:S(2)}, u32[]{:S(2)}) collective-permute-start(bf16[256,256]{1,0:T(8,128)(2,1)S(1)} %get-tuple-element.80), channel_id=1, source_target_pairs={{152,168},{137,184},{153,169},{138,185},{154,170},{139,186},{155,1... | collective-permute-start | bytes 393224 | tf_op jit(solution)/shard_map/ppermute | solution.py:407
  56.7 1.4 collective-permute-start.23
  57.3 0.7 collective-permute-start.22
  58.1 2.0 %collective-permute-start.27 = (bf16[256,256]{1,0:T(8,128)(2,1)S(1)}, bf16[256,256]{1,0:T(8,128)(2,1)S(1)}, u32[]{:S(2)}, u32[]{:S(2)}) collective-permute-start(bf16[256,256]{1,0:T(8,128)(2,1)S(1)} %get-tuple-element.85), channel_id=1, source_target_pairs={{184,200},{169,216},{185,201},{170,217},{186,202},{171,218},{187,2... | collective-permute-start | bytes 393224 | tf_op jit(solution)/shard_map/ppermute | solution.py:407
  58.8 1.4 collective-permute-start.26
  59.5 0.7 collective-permute-start.25
  60.5 2.0 %collective-permute-start.30 = (bf16[256,256]{1,0:T(8,128)(2,1)S(1)}, bf16[256,256]{1,0:T(8,128)(2,1)S(1)}, u32[]{:S(2)}, u32[]{:S(2)}) collective-permute-start(bf16[256,256]{1,0:T(8,128)(2,1)S(1)} %get-tuple-element.90), channel_id=1, source_target_pairs={{216,232},{201,248},{217,233},{202,249},{218,234},{203,250},{219,2... | collective-permute-start | bytes 393224 | tf_op jit(solution)/shard_map/ppermute | solution.py:407
  61.2 1.4 collective-permute-start.29
  61.8 0.7 collective-permute-start.28
  62.6 61.5 %collective-permute-start.31 = (bf16[512,256]{1,0:T(8,128)(2,1)S(1)}, bf16[512,256]{1,0:T(8,128)(2,1)S(1)}, u32[]{:S(2)}, u32[]{:S(2)}) collective-permute-start(bf16[512,256]{1,0:T(8,128)(2,1)S(1)} %get-tuple-element.97), channel_id=1, source_target_pairs={{8,0},{9,1},{10,2},{11,3},{12,4},{13,5},{14,6},{15,7},{24,16},{25,... | collective-permute-start | bytes 786440 | tf_op jit(solution)/shard_map/ppermute | solution.py:410
  124.1 9.6 %collective-permute-start.33 = (bf16[256,256]{1,0:T(8,128)(2,1)S(1)}, bf16[256,256]{1,0:T(8,128)(2,1)S(1)}, u32[]{:S(2)}, u32[]{:S(2)}) collective-permute-start(bf16[256,256]{1,0:T(8,128)(2,1)S(1)} %get-tuple-element.98.mine), channel_id=1, source_target_pairs={{1,0},{16,17},{2,1},{17,18},{3,2},{18,19},{4,3},{19,20},{5,4},{20,... | collective-permute-start | bytes 393224 | tf_op jit(solution)/shard_map/ppermute | solution.py:433
  128.7 9.3 %collective-permute-start.34 = (bf16[256,256]{1,0:T(8,128)(2,1)S(1)}, bf16[256,256]{1,0:T(8,128)(2,1)S(1)}, u32[]{:S(2)}, u32[]{:S(2)}) collective-permute-start(bf16[256,256]{1,0:T(8,128)(2,1)S(1)} %get-tuple-element.99), channel_id=1, source_target_pairs={{1,16},{16,1},{2,17},{17,2},{3,18},{18,3},{4,19},{19,4},{5,20},{20... | collective-permute-start | bytes 393224 | tf_op jit(solution)/shard_map/ppermute | solution.py:434
  133.5 5.1 %collective-permute-start.32 = (bf16[256,256]{1,0:T(8,128)(2,1)S(1)}, bf16[256,256]{1,0:T(8,128)(2,1)S(1)}, u32[]{:S(2)}, u32[]{:S(2)}) collective-permute-start(bf16[256,256]{1,0:T(8,128)(2,1)S(1)} %get-tuple-element.99), channel_id=1, source_target_pairs={{0,16},{1,17},{2,18},{3,19},{4,20},{5,21},{6,22},{7,23},{8,24},{9,... | collective-permute-start | bytes 393224 | tf_op jit(solution)/shard_map/ppermute | solution.py:442

commit v4 on v3

--- a/solution.py
+++ b/solution.py
@@ -31,14 +31,17 @@
     return pl.ds(row * COLS, rows * COLS)
 
 
-def spread(wide, slot, row, values):
+def spread_at(wide, slot, at, values):
     col = lax.broadcasted_iota(jnp.int32, values.shape, 0)
     left = jnp.where(col == 0, 0.0, pltpu.roll(values, 1, 0))
     right = jnp.where(col == COLS - 1, 0.0, pltpu.roll(values, COLS - 1, 0))
-    at = cells(row, 1)
     wide[slot, at, 0:C] = left.astype(BF16)
     wide[slot, at, C : 2 * C] = values.astype(BF16)
     wide[slot, at, 2 * C : 3 * C] = right.astype(BF16)
+
+
+def spread(wide, slot, row, values):
+    spread_at(wide, slot, cells(row, 1), values)
 
 
 def convolve(wide, slot, kernel, row, rows):
@@ -95,13 +98,15 @@
     to_above[...] = initial[: DEPTH * COLS, :].astype(BF16)
 
 
-def pick_kernel(weights, kernel):
-    kernel[...] = weights[0]
+def pick_kernel(weights, kernel, sem):
+    copy = pltpu.make_async_copy(weights.at[0], kernel, sem)
+    copy.start()
+    copy.wait()
 
 
 def first_kernel(
     steps, up, own, down, weights, biases,
-    same, other0, other1, other2, other3, relaxed, state, wide, gain,
+    same, other0, other1, relaxed, state, wide, gain,
 ):
     plane, half, core, coarse = place()
     is_first = (plane == 0) & (half == 0) & (core == 0)
@@ -134,7 +139,7 @@
     pieces.append(jnp.zeros((EXTRA - len(pieces), C), F32))
     extra = jnp.concatenate(pieces, axis=0).astype(BF16)
     sides = [(same, half, 0)]
-    sides += [(ref, 1 - half, k) for k, ref in enumerate((other0, other1, other2, other3))]
+    sides += [(ref, 1 - half, k) for k, ref in enumerate((other0, other1))]
     for ref, side, skip in sides:
         rows = SENT - 2 * skip
         base = pl.multiple_of(side * (TILE * COLS) + skip * COLS, COLS)
@@ -156,41 +161,86 @@
         theirs[...] = arrived[TILE * COLS :, :]
 
 
-def last_kernel(
-    steps, initial, relaxed, mine, across, halo_a, halo_b, weights, biases,
-    corrected, finished, state, wide,
+FRAME = OWN + 2 * LAYERS
+
+
+class Frame:
+    def __init__(self, state, wide, steps, weights, biases):
+        self.half, self.coarse = place()[1], place()[3]
+        self.state, self.wide = state, wide
+        self.steps, self.weights, self.biases = steps, weights, biases
+
+    def start(self, row, rows):
+        return jnp.where(self.half == 1, row, FRAME - row - rows)
+
+    def span(self, row, rows, shift=0):
+        first = (self.start(row, rows) + shift) * COLS
+        return pl.ds(pl.multiple_of(first, COLS), rows * COLS)
+
+    def put(self, slot, row, rows, values):
+        for i in range(rows):
+            piece = values[i * COLS : (i + 1) * COLS, :]
+            at = self.start(row, rows) + i
+            to = pl.ds(pl.multiple_of(at * COLS, COLS), COLS)
+            self.state[to, :] = piece
+            if slot is not None:
+                spread_at(self.wide, slot, to, piece)
+
+    def layer(self, layer, row, rows, outside):
+        taps = [self.wide[layer % 2, self.span(row, rows, a - 1), :] for a in range(3)]
+        product = jnp.dot(
+            jnp.concatenate(taps, axis=1), self.weights[layer], preferred_element_type=F32
+        )
+        slope = jnp.tanh(product + self.biases[layer : layer + 1, :])
+        values = self.state[self.span(row, rows), :] + self.steps[layer] * slope
+        if outside:
+            masked = []
+            for i in range(rows):
+                at = self.coarse * OWN + self.start(row, rows) + i - LAYERS
+                masked.append(values[i * COLS : (i + 1) * COLS, :] * inside(at))
+            values = jnp.concatenate(masked, axis=0)
+        self.put((layer + 1) % 2 if layer < LAYERS - 1 else None, row, rows, values)
+
+
+def early_kernel(
+    steps, initial, halo, across, mine, weights, biases, corrected, part, edge, state, wide
 ):
-    plane, half, core, coarse = place()
+    plane, half, core, _ = place()
     is_first = (plane == 0) & (half == 0) & (core == 0)
-
-    def read(row):
-        at = cells(row % TILE, 1)
-        lower, upper = (
-            (halo_a, halo_b),
-            (across, mine),
-            (mine, across),
-            (halo_b, halo_a),
-        )[row // TILE]
-        values = jnp.where(half == 1, lower[at, :].astype(F32), upper[at, :].astype(F32))
-        if TILE <= row < TILE + OWN:
-            to = cells(row - TILE, 1)
+    frame = Frame(state, wide, steps, weights, biases)
+    for block, ref in enumerate((halo, across, mine)):
+        values = ref[...].astype(F32)
+        frame.put(0, block * TILE, TILE, values)
+        if block > 0:
+            to = frame.span(block * TILE, TILE, -LAYERS)
             corrected[to, :] = jnp.where(is_first, initial[to, :], values)
-        return values
-
-    def visit(layer, row, slope, values):
-        if layer == LAYERS - 1:
-            to = cells(row - LAYERS, 1)
-            finished[to, :] = jnp.where(is_first, relaxed[to, :], values)
-
-    relax_rows(LAYERS, coarse * OWN, read, weights, biases, steps, state, wide, visit)
+    for layer in range(LAYERS):
+        edge[cells(2 * layer, 2), :] = state[frame.span(10 - layer, 2), :]
+        for start, rows in chunks(10 - 2 * layer, 4):
+            row = layer + 1 + start
+            frame.layer(layer, row, rows, row < TILE)
+    part[...] = state[frame.span(TILE, TILE), :]
+
+
+def late_kernel(steps, relaxed, halo, edge, part, weights, biases, finished, state, wide):
+    plane, half, core, _ = place()
+    is_first = (plane == 0) & (half == 0) & (core == 0)
+    frame = Frame(state, wide, steps, weights, biases)
+    frame.put(0, 3 * TILE, TILE, halo[...].astype(F32))
+    for layer in range(LAYERS):
+        frame.put(layer % 2, 10 - layer, 2, edge[cells(2 * layer, 2), :])
+        frame.layer(layer, 11 - layer, TILE, layer < LAYERS - 1)
+    for row, values in ((TILE, part[...]), (2 * TILE, state[frame.span(2 * TILE, TILE), :])):
+        to = frame.span(row, TILE, -LAYERS)
+        finished[to, :] = jnp.where(is_first, relaxed[to, :], values)
 
 
 def chain_kernel(turn, *refs):
     refs = list(refs)
     entering = None if turn == 0 else [refs.pop(0) for _ in range(3)]
     before = None if turn == 0 else [refs.pop(0) for _ in range(GROUP)]
-    near, own_defect, *others = [refs.pop(0) for _ in range(2 + GROUP)]
-    sources = [(near, others[0]), (own_defect, others[1]), (others[2], near), (others[3], own_defect)]
+    near, mine, south, north = [refs.pop(0) for _ in range(4)]
+    sources = [(near, south), (mine, north), (south, near), (north, mine)]
     weights = refs.pop(0)
     following = None if turn == PLANES - 1 else refs.pop(0)
     if turn == PLANES - 1:
@@ -209,7 +259,7 @@
         picked = []
         for at_half in range(2):
             ref = sources[step][at_half]
-            skip = step if any(ref is other for other in others) else 0
+            skip = 1 if ref is north else 0
             start = (row - skip) * COLS if cut else (SENT - 2 * skip) * COLS
             picked.append(ref[pl.ds(start, rows), :].astype(F32))
         return jnp.where(half == 0, picked[0], picked[1])
@@ -336,9 +386,10 @@
         pick_kernel,
         name="pick",
         out_shape=shape(9 * C),
-        in_specs=[VMEM],
+        in_specs=[pl.BlockSpec(memory_space=pltpu.HBM)],
         out_specs=VMEM,
-        compiler_params=pltpu.CompilerParams(vmem_limit_bytes=8 * 2**20),
+        scratch_shapes=[pltpu.SemaphoreType.DMA(())],
+        compiler_params=pltpu.CompilerParams(vmem_limit_bytes=50 * 2**20),
     )(kernels)
 
     to_north = within_plane(lambda p, h, c: (device(p, h, 0, c), device(p, h, 1, c)))
@@ -359,7 +410,7 @@
     far_north = lax.ppermute(kernel, AXES, within_plane(from_next_pair))
     near_south = lax.ppermute(kernel, AXES, to_north)
 
-    messages = [shape((SENT - 2 * k) * COLS + EXTRA) for k in (0, 0, 1, 2, 3)]
+    messages = [shape((SENT - 2 * k) * COLS + EXTRA) for k in (0, 0, 1)]
     same, *others, relaxed = call(
         first_kernel,
         68,
@@ -368,17 +419,18 @@
         [SMEM] + [VMEM] * 5,
         (pltpu.VMEM((WIDE * COLS, C), F32),),
     )(step_sizes, above, initial, below, kernels, biases)
-    defects = []
-    for k in range(GROUP):
-        half, core = k // 2, k % 2
-        pairs = [
-            (device(p, half, core, c), device(p, 1 - half, 1, c))
-            for p in range(PLANES)
-            for c in range(8)
-        ]
-        defects.append(lax.ppermute(others[k], AXES, pairs))
-    same_south = lax.ppermute(same, AXES, to_north)
-    defects = [same_south, same, *defects]
+
+    def exchange(planes):
+        def send(message, link):
+            chosen = [pair for pair in link if pair[0] // device(1, 0, 0, 0) in planes]
+            return lax.ppermute(message, AXES, chosen)
+
+        other_south = send(others[0], to_other_north)
+        other_north = send(others[1], north_to_north)
+        return [send(same, to_north), same, other_south, other_north]
+
+    early = exchange(range(1))
+    late = exchange(range(1, PLANES))
     chain_kernels = jnp.stack([near_south, kernel, far_south, far_north])
 
     block = shape(TILE * COLS)
@@ -386,6 +438,7 @@
     for turn in range(PLANES):
         last = turn == PLANES - 1
         outs = (shape(2 * TILE * COLS), block, block) if last else (block,) * (GROUP + 1)
+        defects = late if turn else early
         operands = [*entering, *passed, *defects, chain_kernels]
         results = call(
             functools.partial(chain_kernel, turn),
@@ -441,9 +494,16 @@
     ]
     across = lax.ppermute(theirs, AXES, swap)
     result = shape(OWN * COLS, F32)
-    corrected, finished = call(
-        last_kernel, 44, OWN + 2 * LAYERS, (result, result), [SMEM] + [VMEM] * 8
-    )(step_sizes, initial, relaxed, mine, across, halo_a, halo_b, kernels, biases)
+    corrected, part, edge = call(
+        early_kernel,
+        28,
+        FRAME,
+        (result, shape(TILE * COLS, F32), shape(2 * LAYERS * COLS, F32)),
+        [SMEM] + [VMEM] * 6,
+    )(step_sizes, initial, halo_a, across, mine, kernels, biases)
+    finished = call(late_kernel, 16, FRAME, result, [SMEM] + [VMEM] * 6)(
+        step_sizes, relaxed, halo_b, edge, part, kernels, biases
+    )
     return (
         corrected.reshape(start_states.shape),
         finished.reshape(start_states.shape),

time: 144 us -> 144 us (level)
  the two profiles are of different devices: /device:TPU:248 before, /device:TPU:234 now
where the time goes in v4:
time: 144 us; the launch traced here: 143 us
  waiting for transfers between devices  81.2 us (56%)
  starting transfers between devices  42 us (29%)
  Pallas kernels  18.2 us (13%)
    ppermute x1, waiting for transfers between devices, local(): arrived = lax.ppermute(to_south, AXES, [(b, a) for a, b in to_north])  58.4 us
    ppermute x1, waiting for transfers between devices, local(): above = lax.ppermute(to_below, 'coarse', downward)  14.7 us
    ppermute x21, starting transfers between devices, local(): entering.append(lax.ppermute(results[0], AXES, pairs))  14 us
    pallas_call x1, Pallas kernels, local(): call(first_kernel, 68, OWN + 2 * DEPTH, (*messages, shape(OWN * COLS, F32...  6.24 us
    ppermute x6, starting transfers between devices, send(): return lax.ppermute(message, AXES, chosen)  5.34 us
    pallas_call x1, Pallas kernels, local(): call(early_kernel, 28, FRAME, (result, shape(TILE * COLS, F32), shape(2 *...  4.95 us
    pallas_call x1, Pallas kernels, local(): call(late_kernel, 16, FRAME, result, [SMEM] + [VMEM] * 6)  4.55 us
    ppermute x1, starting transfers between devices, local(): across = lax.ppermute(theirs, AXES, swap)  4.37 us
  transfers between devices with their start and end apart: 36, of which 6 were waited for; matrix products, arithmetic and copies ran while one was open for 0% of the time, Pallas kernels for 8%

profile of v4, /device:TPU:234, one launch (start us, length us, event | category | flops | bytes accessed | tf_op | source)
XLA Modules:
  0.0 143.4 jit_solution(751215621775180148)
XLA Ops:
  0.7 1.4 %pick.1 = bf16[2304,256]{1,0:T(8,128)(2,1)S(1)} custom-call(bf16[4,2304,256]{2,1,0:T(8,128)(2,1)} %bitcast.8), custom_call_target="tpu_custom_call" | custom-call | tf_op jit(solution)/shard_map/pick/pallas_call | solution.py:385
  2.1 1.9 %collective-permute-start.5 = (bf16[2304,256]{1,0:T(8,128)(2,1)S(1)}, bf16[2304,256]{1,0:T(8,128)(2,1)S(1)}, u32[]{:S(2)}, u32[]{:S(2)}) collective-permute-start(bf16[2304,256]{1,0:T(8,128)(2,1)S(1)} %pick.1), channel_id=1, source_target_pairs={{0,8},{1,9},{2,10},{3,11},{4,12},{5,13},{6,14},{7,15},{16,24},{17,... | collective-permute-start | bytes 3538952 | tf_op jit(solution)/shard_map/ppermute | solution.py:411
  4.1 1.4 collective-permute-start.6
  5.5 0.7 collective-permute-start.7
  6.3 4.3 %collective-permute-start = (bf16[448,256]{1,0:T(8,128)(2,1)S(1)}, bf16[448,256]{1,0:T(8,128)(2,1)S(1)}, u32[]{:S(2)}, u32[]{:S(2)}) collective-permute-start(bf16[448,256]{1,0:T(8,128)(2,1)S(1)} %get-tuple-element.51), channel_id=1, source_target_pairs={{0,1},{1,2},{2,3},{3,4},{4,5},{5,6},{6,7},{8,9},{9,10},{10,11},{11... | collective-permute-start | bytes 688136 | tf_op jit(solution)/shard_map/ppermute | solution.py:383
  10.7 3.9 %collective-permute-start.1 = (bf16[448,256]{1,0:T(8,128)(2,1)S(1)}, bf16[448,256]{1,0:T(8,128)(2,1)S(1)}, u32[]{:S(2)}, u32[]{:S(2)}) collective-permute-start(bf16[448,256]{1,0:T(8,128)(2,1)S(1)} %get-tuple-element.52), channel_id=1, source_target_pairs={{1,0},{2,1},{3,2},{4,3},{5,4},{6,5},{7,6},{9,8},{10,9},{11,10},{12... | collective-permute-start | bytes 688136 | tf_op jit(solution)/shard_map/ppermute | solution.py:384
  14.6 14.7 %collective-permute-done.up = bf16[448,256]{1,0:T(8,128)(2,1)S(1)} collective-permute-done((bf16[448,256]{1,0:T(8,128)(2,1)S(1)}, bf16[448,256]{1,0:T(8,128)(2,1)S(1)}, u32[]{:S(2)}, u32[]{:S(2)}) %collective-permute-start) | collective-permute-done | bytes 229408 | tf_op jit(solution)/shard_map/ppermute | solution.py:383
  29.3 2.6 %collective-permute-done.1.down = bf16[448,256]{1,0:T(8,128)(2,1)S(1)} collective-permute-done((bf16[448,256]{1,0:T(8,128)(2,1)S(1)}, bf16[448,256]{1,0:T(8,128)(2,1)S(1)}, u32[]{:S(2)}, u32[]{:S(2)}) %collective-permute-start.1) | collective-permute-done | bytes 229408 | tf_op jit(solution)/shard_map/ppermute | solution.py:384
  31.9 6.2 %shard_map.59 = (bf16[656,256]{1,0:T(8,128)(2,1)S(1)}, bf16[656,256]{1,0:T(8,128)(2,1)S(1)}, bf16[528,256]{1,0:T(8,128)(2,1)S(1)}, f32[512,256]{1,0:T(8,128)S(1)}) custom-call(f32[4]{0:T(128)S(1)} %copy-done.3, bf16[448,256]{1,0:T(8,128)(2,1)S(1)} %collective-permute-done.up, f32[512,256]{1,0:T(8,128)S(1)} %bitcast.14, ...), custom_call_target="tpu_custom_call" | custom-call | flops 5133828096 | bytes 10027008 | tf_op jit(solution)/shard_map/pallas_call | solution.py:414
  38.1 0.7 collective-permute-start.4
  38.8 0.7 collective-permute-start.2
  39.5 0.0 collective-permute-done.4.refs_3_
  39.5 1.3 collective-permute-start.11
  40.8 0.7 collective-permute-start.3
  41.5 0.0 collective-permute-done.6
  41.5 1.3 collective-permute-start.12
  42.8 0.0 collective-permute-done.7
  42.9 0.7 collective-permute-start.13
  43.5 0.6 pad_maximum_fusion.refs_4_.refs_11_
  44.2 0.0 collective-permute-done.3.refs_2_
  44.2 0.1 shard_map.60
  44.3 0.7 collective-permute-start.10
  45.0 0.7 collective-permute-start.8
  45.7 0.7 collective-permute-start.9
  46.3 0.0 collective-permute-done.11.refs_7_
  46.3 1.1 collective-permute-done.12.refs_9_
  47.5 0.0 collective-permute-done.10.refs_2_
  47.5 0.1 shard_map.61
  47.6 0.7 collective-permute-start.14
  48.3 0.7 collective-permute-start.15
  48.9 0.7 collective-permute-start.16
  49.6 0.0 collective-permute-done.14.refs_0_
  49.6 0.3 shard_map.62
  49.9 0.7 collective-permute-start.17
  50.6 0.7 collective-permute-start.18
  51.3 0.7 collective-permute-start.19
  52.0 0.0 collective-permute-done.19.refs_2_
  52.0 0.1 shard_map.63
  52.0 0.7 collective-permute-start.20
  52.7 0.7 collective-permute-start.21
  53.4 0.7 collective-permute-start.22
  54.1 0.0 collective-permute-done.20.refs_0_
  54.1 0.1 shard_map.64
  54.2 0.7 collective-permute-start.23
  54.9 0.7 collective-permute-start.24
  55.5 0.7 collective-permute-start.25
  56.3 0.1 shard_map.65
  56.3 0.7 collective-permute-start.26
  57.0 0.7 collective-permute-start.27
  57.7 0.7 collective-permute-start.28
  58.4 0.3 shard_map.66
  58.7 0.7 collective-permute-start.29
  59.4 0.7 collective-permute-start.30
  60.0 0.7 collective-permute-start.31
  60.8 0.1 shard_map.67
  60.8 1.3 collective-permute-start.32
  62.1 58.4 %collective-permute-done.32.arrived = bf16[512,256]{1,0:T(8,128)(2,1)S(1)} collective-permute-done((bf16[512,256]{1,0:T(8,128)(2,1)S(1)}, bf16[512,256]{1,0:T(8,128)(2,1)S(1)}, u32[]{:S(2)}, u32[]{:S(2)}) %collective-permute-start.32) | collective-permute-done | bytes 262176 | tf_op jit(solution)/shard_map/ppermute | solution.py:463
  120.6 2.7 %collective-permute-start.33 = (bf16[256,256]{1,0:T(8,128)(2,1)S(1)}, bf16[256,256]{1,0:T(8,128)(2,1)S(1)}, u32[]{:S(2)}, u32[]{:S(2)}) collective-permute-start(bf16[256,256]{1,0:T(8,128)(2,1)S(1)} %get-tuple-element.94.mine), channel_id=1, source_target_pairs={{1,0},{16,17},{2,1},{17,18},{3,2},{18,19},{4,3},{19,20},{5,4},{20,... | collective-permute-start | bytes 393224 | tf_op jit(solution)/shard_map/ppermute | solution.py:486
  123.3 4.4 %collective-permute-start.34 = (bf16[256,256]{1,0:T(8,128)(2,1)S(1)}, bf16[256,256]{1,0:T(8,128)(2,1)S(1)}, u32[]{:S(2)}, u32[]{:S(2)}) collective-permute-start(bf16[256,256]{1,0:T(8,128)(2,1)S(1)} %get-tuple-element.95), channel_id=1, source_target_pairs={{0,16},{1,17},{2,18},{3,19},{4,20},{5,21},{6,22},{7,23},{8,24},{9,... | collective-permute-start | bytes 393224 | tf_op jit(solution)/shard_map/ppermute | solution.py:495
  127.6 1.9 %collective-permute-start.35 = (bf16[256,256]{1,0:T(8,128)(2,1)S(1)}, bf16[256,256]{1,0:T(8,128)(2,1)S(1)}, u32[]{:S(2)}, u32[]{:S(2)}) collective-permute-start(bf16[256,256]{1,0:T(8,128)(2,1)S(1)} %get-tuple-element.95), channel_id=1, source_target_pairs={{1,16},{16,1},{2,17},{17,2},{3,18},{18,3},{4,19},{19,4},{5,20},{20... | collective-permute-start | bytes 393224 | tf_op jit(solution)/shard_map/ppermute | solution.py:487
  129.6 1.7 %collective-permute-done.33.halo = bf16[256,256]{1,0:T(8,128)(2,1)S(1)} collective-permute-done((bf16[256,256]{1,0:T(8,128)(2,1)S(1)}, bf16[256,256]{1,0:T(8,128)(2,1)S(1)}, u32[]{:S(2)}, u32[]{:S(2)}) %collective-permute-start.33) | collective-permute-done | bytes 131104 | tf_op jit(solution)/shard_map/ppermute | solution.py:486
  131.3 2.6 %collective-permute-done.34.across = bf16[256,256]{1,0:T(8,128)(2,1)S(1)} collective-permute-done((bf16[256,256]{1,0:T(8,128)(2,1)S(1)}, bf16[256,256]{1,0:T(8,128)(2,1)S(1)}, u32[]{:S(2)}, u32[]{:S(2)}) %collective-permute-start.34) | collective-permute-done | bytes 131104 | tf_op jit(solution)/shard_map/ppermute | solution.py:495
  133.9 4.9 %shard_map.68 = (f32[512,256]{1,0:T(8,128)}, f32[256,256]{1,0:T(8,128)S(1)}, f32[512,256]{1,0:T(8,128)S(1)}) custom-call(f32[4]{0:T(128)S(1)} %copy-done.3, f32[512,256]{1,0:T(8,128)S(1)} %bitcast.15, bf16[256,256]{1,0:T(8,128)(2,1)S(1)} %collective-permute-done.33.halo, bf16[256,256]{1,0:T(8,128)(2,1)S(1)} %collective-permute-done.34.across, ...), custom_call_target="tpu_custom_call" | custom-call | flops 2113929216 | bytes 4128768 | tf_op jit(solution)/shard_map/pallas_call | solution.py:497
  138.8 4.5 %shard_map.69 = f32[512,256]{1,0:T(8,128)} custom-call(f32[4]{0:T(128)S(1)} %copy-done.3, f32[512,256]{1,0:T(8,128)S(1)} %get-tuple-element.97.relaxed, bf16[256,256]{1,0:T(8,128)(2,1)S(1)} %collective-permute-done.35.halo, f32[512,256]{1,0:T(8,128)S(1)} %get-tuple-element.98.edge, f32[256,256]{1,0:T(8,128)S(1)} %get-tuple-element.99.part, ...), custom_call_target="tpu_custom_call" | custom-call | flops 1207959552 | bytes 2359296 | tf_op jit(solution)/shard_map/pallas_call | solution.py:504
  (31 shorter events, 0.1 us)
Async XLA Ops:
  0.6 31.2 %copy-start = (bf16[4,9,256,256]{3,2,1,0:T(8,128)(2,1)S(1)}, bf16[4,9,256,256]{3,2,1,0:T(8,128)(2,1)}, u32[]{:S(2)}) copy-start(bf16[4,9,256,256]{3,2,1,0:T(8,128)(2,1)} %param.5) | copy-start | bytes 14155780
  0.6 5.6 %copy-start.1 = (f32[1,1,8,64,256]{4,3,2,1,0:T(8,128)S(1)}, f32[1,1,8,64,256]{4,3,2,1,0:T(8,128)}, u32[]{:S(2)}) copy-start(f32[1,1,8,64,256]{4,3,2,1,0:T(8,128)} %param.4) | copy-start | bytes 1572868
  0.7 31.2 %copy-start.2 = (f32[4,256]{1,0:T(4,128)S(1)}, f32[4,256]{1,0:T(4,128)}, u32[]{:S(2)}) copy-start(f32[4,256]{1,0:T(4,128)} %biases.5) | copy-start | bytes 12292
  0.7 31.2 %copy-start.3 = (f32[4]{0:T(128)S(1)}, f32[4]{0:T(128)}, u32[]{:S(2)}) copy-start(f32[4]{0:T(128)} %steps.5) | copy-start | bytes 52
  2.1 38.7 %collective-permute-start.5 = (bf16[2304,256]{1,0:T(8,128)(2,1)S(1)}, bf16[2304,256]{1,0:T(8,128)(2,1)S(1)}, u32[]{:S(2)}, u32[]{:S(2)}) collective-permute-start(bf16[2304,256]{1,0:T(8,128)(2,1)S(1)} %pick.1), channel_id=1, source_target_pairs={{0,8},{1,9},{2,10},{3,11},{4,12},{5,13},{6,14},{7,15},{16,24},{17,... | collective-permute-start | bytes 3538952 | tf_op jit(solution)/shard_map/ppermute | solution.py:411
  4.1 37.4 %collective-permute-start.6 = (bf16[2304,256]{1,0:T(8,128)(2,1)S(1)}, bf16[2304,256]{1,0:T(8,128)(2,1)S(1)}, u32[]{:S(2)}, u32[]{:S(2)}) collective-permute-start(bf16[2304,256]{1,0:T(8,128)(2,1)S(1)} %pick.1), channel_id=1, source_target_pairs={{16,8},{17,9},{18,10},{19,11},{20,12},{21,13},{22,14},{23,15},{32,... | collective-permute-start | bytes 3538952 | tf_op jit(solution)/shard_map/ppermute | solution.py:409
  5.5 37.3 %collective-permute-start.7 = (bf16[2304,256]{1,0:T(8,128)(2,1)S(1)}, bf16[2304,256]{1,0:T(8,128)(2,1)S(1)}, u32[]{:S(2)}, u32[]{:S(2)}) collective-permute-start(bf16[2304,256]{1,0:T(8,128)(2,1)S(1)} %pick.1), channel_id=1, source_target_pairs={{25,8},{24,9},{27,10},{26,11},{29,12},{28,13},{31,14},{30,15},{9,2... | collective-permute-start | bytes 3538952 | tf_op jit(solution)/shard_map/ppermute | solution.py:410
  6.3 23.0 %collective-permute-start = (bf16[448,256]{1,0:T(8,128)(2,1)S(1)}, bf16[448,256]{1,0:T(8,128)(2,1)S(1)}, u32[]{:S(2)}, u32[]{:S(2)}) collective-permute-start(bf16[448,256]{1,0:T(8,128)(2,1)S(1)} %get-tuple-element.51), channel_id=1, source_target_pairs={{0,1},{1,2},{2,3},{3,4},{4,5},{5,6},{6,7},{8,9},{9,10},{10,11},{11... | collective-permute-start | bytes 688136 | tf_op jit(solution)/shard_map/ppermute | solution.py:383
  10.7 21.2 %collective-permute-start.1 = (bf16[448,256]{1,0:T(8,128)(2,1)S(1)}, bf16[448,256]{1,0:T(8,128)(2,1)S(1)}, u32[]{:S(2)}, u32[]{:S(2)}) collective-permute-start(bf16[448,256]{1,0:T(8,128)(2,1)S(1)} %get-tuple-element.52), channel_id=1, source_target_pairs={{1,0},{2,1},{3,2},{4,3},{5,4},{6,5},{7,6},{9,8},{10,9},{11,10},{12... | collective-permute-start | bytes 688136 | tf_op jit(solution)/shard_map/ppermute | solution.py:384
  38.1 1.4 collective-permute-start.4
  38.8 5.4 %collective-permute-start.2 = (bf16[656,256]{1,0:T(8,128)(2,1)S(1)}, bf16[656,256]{1,0:T(8,128)(2,1)S(1)}, u32[]{:S(2)}, u32[]{:S(2)}) collective-permute-start(bf16[656,256]{1,0:T(8,128)(2,1)S(1)} %get-tuple-element.53.refs_1_.refs_8_), channel_id=1, source_target_pairs={{0,8},{1,9},{2,10},{3,11},{4,12},{5,13},{6,14},{7,15},{16,24},{17,... | collective-permute-start | bytes 1007624 | tf_op jit(solution)/shard_map/ppermute | solution.py:426
  39.5 6.8 %collective-permute-start.11 = (bf16[656,256]{1,0:T(8,128)(2,1)S(1)}, bf16[656,256]{1,0:T(8,128)(2,1)S(1)}, u32[]{:S(2)}, u32[]{:S(2)}) collective-permute-start(bf16[656,256]{1,0:T(8,128)(2,1)S(1)} %get-tuple-element.53.refs_1_.refs_8_), channel_id=1, source_target_pairs={{32,40},{33,41},{34,42},{35,43},{36,44},{37,45},{38,46},{39,47},{4... | collective-permute-start | bytes 1007624 | tf_op jit(solution)/shard_map/ppermute | solution.py:426
  40.8 3.4 %collective-permute-start.3 = (bf16[656,256]{1,0:T(8,128)(2,1)S(1)}, bf16[656,256]{1,0:T(8,128)(2,1)S(1)}, u32[]{:S(2)}, u32[]{:S(2)}) collective-permute-start(bf16[656,256]{1,0:T(8,128)(2,1)S(1)} %get-tuple-element.54), channel_id=1, source_target_pairs={{0,24},{1,25},{2,26},{3,27},{4,28},{5,29},{6,30},{7,31},{16,8},{17... | collective-permute-start | bytes 1007624 | tf_op jit(solution)/shard_map/ppermute | solution.py:426
  41.5 6.0 %collective-permute-start.12 = (bf16[656,256]{1,0:T(8,128)(2,1)S(1)}, bf16[656,256]{1,0:T(8,128)(2,1)S(1)}, u32[]{:S(2)}, u32[]{:S(2)}) collective-permute-start(bf16[656,256]{1,0:T(8,128)(2,1)S(1)} %get-tuple-element.54), channel_id=1, source_target_pairs={{32,56},{33,57},{34,58},{35,59},{36,60},{37,61},{38,62},{39,63},{4... | collective-permute-start | bytes 1007624 | tf_op jit(solution)/shard_map/ppermute | solution.py:426
  42.9 2.8 %collective-permute-start.13 = (bf16[528,256]{1,0:T(8,128)(2,1)S(1)}, bf16[528,256]{1,0:T(8,128)(2,1)S(1)}, u32[]{:S(2)}, u32[]{:S(2)}) collective-permute-start(bf16[528,256]{1,0:T(8,128)(2,1)S(1)} %get-tuple-element.55), channel_id=1, source_target_pairs={{40,56},{41,57},{42,58},{43,59},{44,60},{45,61},{46,62},{47,63},{5... | collective-permute-start | bytes 811016 | tf_op jit(solution)/shard_map/ppermute | solution.py:426
  44.3 3.2 %collective-permute-start.10 = (bf16[256,256]{1,0:T(8,128)(2,1)S(1)}, bf16[256,256]{1,0:T(8,128)(2,1)S(1)}, u32[]{:S(2)}, u32[]{:S(2)}) collective-permute-start(bf16[256,256]{1,0:T(8,128)(2,1)S(1)} %get-tuple-element.56), channel_id=1, source_target_pairs={{24,40},{9,56},{25,41},{10,57},{26,42},{11,58},{27,43},{12,59},{28... | collective-permute-start | bytes 393224 | tf_op jit(solution)/shard_map/ppermute | solution.py:460
  45.0 2.5 %collective-permute-start.8 = (bf16[256,256]{1,0:T(8,128)(2,1)S(1)}, bf16[256,256]{1,0:T(8,128)(2,1)S(1)}, u32[]{:S(2)}, u32[]{:S(2)}) collective-permute-start(bf16[256,256]{1,0:T(8,128)(2,1)S(1)} %get-tuple-element.56), channel_id=1, source_target_pairs={{8,56},{24,41},{9,57},{25,42},{10,58},{26,43},{11,59},{27,44},{12,... | collective-permute-start | bytes 393224 | tf_op jit(solution)/shard_map/ppermute | solution.py:460
  45.7 1.8 %collective-permute-start.9 = (bf16[256,256]{1,0:T(8,128)(2,1)S(1)}, bf16[256,256]{1,0:T(8,128)(2,1)S(1)}, u32[]{:S(2)}, u32[]{:S(2)}) collective-permute-start(bf16[256,256]{1,0:T(8,128)(2,1)S(1)} %get-tuple-element.56), channel_id=1, source_target_pairs={{8,40},{24,56},{9,41},{25,57},{10,42},{26,58},{11,43},{27,59},{12,... | collective-permute-start | bytes 393224 | tf_op jit(solution)/shard_map/ppermute | solution.py:460
  47.6 2.0 %collective-permute-start.14 = (bf16[256,256]{1,0:T(8,128)(2,1)S(1)}, bf16[256,256]{1,0:T(8,128)(2,1)S(1)}, u32[]{:S(2)}, u32[]{:S(2)}) collective-permute-start(bf16[256,256]{1,0:T(8,128)(2,1)S(1)} %get-tuple-element.61), channel_id=1, source_target_pairs={{40,88},{56,73},{41,89},{57,74},{42,90},{58,75},{43,91},{59,76},{4... | collective-permute-start | bytes 393224 | tf_op jit(solution)/shard_map/ppermute | solution.py:460
  48.3 1.4 collective-permute-start.15
  48.9 0.7 collective-permute-start.16
  49.9 2.0 %collective-permute-start.17 = (bf16[256,256]{1,0:T(8,128)(2,1)S(1)}, bf16[256,256]{1,0:T(8,128)(2,1)S(1)}, u32[]{:S(2)}, u32[]{:S(2)}) collective-permute-start(bf16[256,256]{1,0:T(8,128)(2,1)S(1)} %get-tuple-element.66), channel_id=1, source_target_pairs={{72,120},{88,105},{73,121},{89,106},{74,122},{90,107},{75,123},{91... | collective-permute-start | bytes 393224 | tf_op jit(solution)/shard_map/ppermute | solution.py:460
  50.6 1.4 collective-permute-start.18
  51.3 0.7 collective-permute-start.19
  52.0 2.0 %collective-permute-start.20 = (bf16[256,256]{1,0:T(8,128)(2,1)S(1)}, bf16[256,256]{1,0:T(8,128)(2,1)S(1)}, u32[]{:S(2)}, u32[]{:S(2)}) collective-permute-start(bf16[256,256]{1,0:T(8,128)(2,1)S(1)} %get-tuple-element.71), channel_id=1, source_target_pairs={{104,152},{120,137},{105,153},{121,138},{106,154},{122,139},{107,1... | collective-permute-start | bytes 393224 | tf_op jit(solution)/shard_map/ppermute | solution.py:460
  52.7 1.4 collective-permute-start.21
  53.4 0.7 collective-permute-start.22
  54.2 2.0 %collective-permute-start.23 = (bf16[256,256]{1,0:T(8,128)(2,1)S(1)}, bf16[256,256]{1,0:T(8,128)(2,1)S(1)}, u32[]{:S(2)}, u32[]{:S(2)}) collective-permute-start(bf16[256,256]{1,0:T(8,128)(2,1)S(1)} %get-tuple-element.76), channel_id=1, source_target_pairs={{136,184},{152,169},{137,185},{153,170},{138,186},{154,171},{139,1... | collective-permute-start | bytes 393224 | tf_op jit(solution)/shard_map/ppermute | solution.py:460
  54.9 1.4 collective-permute-start.24
  55.5 0.7 collective-permute-start.25
  56.3 2.0 %collective-permute-start.26 = (bf16[256,256]{1,0:T(8,128)(2,1)S(1)}, bf16[256,256]{1,0:T(8,128)(2,1)S(1)}, u32[]{:S(2)}, u32[]{:S(2)}) collective-permute-start(bf16[256,256]{1,0:T(8,128)(2,1)S(1)} %get-tuple-element.81), channel_id=1, source_target_pairs={{168,216},{184,201},{169,217},{185,202},{170,218},{186,203},{171,2... | collective-permute-start | bytes 393224 | tf_op jit(solution)/shard_map/ppermute | solution.py:460
  57.0 1.4 collective-permute-start.27
  57.7 0.7 collective-permute-start.28
  58.7 2.0 %collective-permute-start.29 = (bf16[256,256]{1,0:T(8,128)(2,1)S(1)}, bf16[256,256]{1,0:T(8,128)(2,1)S(1)}, u32[]{:S(2)}, u32[]{:S(2)}) collective-permute-start(bf16[256,256]{1,0:T(8,128)(2,1)S(1)} %get-tuple-element.86), channel_id=1, source_target_pairs={{200,248},{216,233},{201,249},{217,234},{202,250},{218,235},{203,2... | collective-permute-start | bytes 393224 | tf_op jit(solution)/shard_map/ppermute | solution.py:460
  59.4 1.4 collective-permute-start.30
  60.0 0.7 collective-permute-start.31
  60.8 59.7 %collective-permute-start.32 = (bf16[512,256]{1,0:T(8,128)(2,1)S(1)}, bf16[512,256]{1,0:T(8,128)(2,1)S(1)}, u32[]{:S(2)}, u32[]{:S(2)}) collective-permute-start(bf16[512,256]{1,0:T(8,128)(2,1)S(1)} %get-tuple-element.93), channel_id=1, source_target_pairs={{8,0},{9,1},{10,2},{11,3},{12,4},{13,5},{14,6},{15,7},{24,16},{25,... | collective-permute-start | bytes 786440 | tf_op jit(solution)/shard_map/ppermute | solution.py:463
  120.6 10.7 %collective-permute-start.33 = (bf16[256,256]{1,0:T(8,128)(2,1)S(1)}, bf16[256,256]{1,0:T(8,128)(2,1)S(1)}, u32[]{:S(2)}, u32[]{:S(2)}) collective-permute-start(bf16[256,256]{1,0:T(8,128)(2,1)S(1)} %get-tuple-element.94.mine), channel_id=1, source_target_pairs={{1,0},{16,17},{2,1},{17,18},{3,2},{18,19},{4,3},{19,20},{5,4},{20,... | collective-permute-start | bytes 393224 | tf_op jit(solution)/shard_map/ppermute | solution.py:486
  123.3 10.6 %collective-permute-start.34 = (bf16[256,256]{1,0:T(8,128)(2,1)S(1)}, bf16[256,256]{1,0:T(8,128)(2,1)S(1)}, u32[]{:S(2)}, u32[]{:S(2)}) collective-permute-start(bf16[256,256]{1,0:T(8,128)(2,1)S(1)} %get-tuple-element.95), channel_id=1, source_target_pairs={{0,16},{1,17},{2,18},{3,19},{4,20},{5,21},{6,22},{7,23},{8,24},{9,... | collective-permute-start | bytes 393224 | tf_op jit(solution)/shard_map/ppermute | solution.py:495
  127.6 11.2 %collective-permute-start.35 = (bf16[256,256]{1,0:T(8,128)(2,1)S(1)}, bf16[256,256]{1,0:T(8,128)(2,1)S(1)}, u32[]{:S(2)}, u32[]{:S(2)}) collective-permute-start(bf16[256,256]{1,0:T(8,128)(2,1)S(1)} %get-tuple-element.95), channel_id=1, source_target_pairs={{1,16},{16,1},{2,17},{17,2},{3,18},{18,3},{4,19},{19,4},{5,20},{20... | collective-permute-start | bytes 393224 | tf_op jit(solution)/shard_map/ppermute | solution.py:487

commit v5 on v3

--- a/solution.py
+++ b/solution.py
@@ -95,13 +95,15 @@
     to_above[...] = initial[: DEPTH * COLS, :].astype(BF16)
 
 
-def pick_kernel(weights, kernel):
-    kernel[...] = weights[0]
+def pick_kernel(weights, kernel, sem):
+    copy = pltpu.make_async_copy(weights.at[0], kernel, sem)
+    copy.start()
+    copy.wait()
 
 
 def first_kernel(
     steps, up, own, down, weights, biases,
-    same, other0, other1, other2, other3, relaxed, state, wide, gain,
+    same, other0, other1, relaxed, state, wide, gain,
 ):
     plane, half, core, coarse = place()
     is_first = (plane == 0) & (half == 0) & (core == 0)
@@ -134,7 +136,7 @@
     pieces.append(jnp.zeros((EXTRA - len(pieces), C), F32))
     extra = jnp.concatenate(pieces, axis=0).astype(BF16)
     sides = [(same, half, 0)]
-    sides += [(ref, 1 - half, k) for k, ref in enumerate((other0, other1, other2, other3))]
+    sides += [(ref, 1 - half, k) for k, ref in enumerate((other0, other1))]
     for ref, side, skip in sides:
         rows = SENT - 2 * skip
         base = pl.multiple_of(side * (TILE * COLS) + skip * COLS, COLS)
@@ -189,8 +191,8 @@
     refs = list(refs)
     entering = None if turn == 0 else [refs.pop(0) for _ in range(3)]
     before = None if turn == 0 else [refs.pop(0) for _ in range(GROUP)]
-    near, own_defect, *others = [refs.pop(0) for _ in range(2 + GROUP)]
-    sources = [(near, others[0]), (own_defect, others[1]), (others[2], near), (others[3], own_defect)]
+    near, mine, south, north = [refs.pop(0) for _ in range(4)]
+    sources = [(near, south), (mine, north), (south, near), (north, mine)]
     weights = refs.pop(0)
     following = None if turn == PLANES - 1 else refs.pop(0)
     if turn == PLANES - 1:
@@ -209,7 +211,7 @@
         picked = []
         for at_half in range(2):
             ref = sources[step][at_half]
-            skip = step if any(ref is other for other in others) else 0
+            skip = 1 if ref is north else 0
             start = (row - skip) * COLS if cut else (SENT - 2 * skip) * COLS
             picked.append(ref[pl.ds(start, rows), :].astype(F32))
         return jnp.where(half == 0, picked[0], picked[1])
@@ -249,7 +251,9 @@
             bias = extra[0:1, :] + extra[1:2, :] + extra[2:3, :]
             scale = extra[3:4, :] + extra[4:5, :] + extra[5:6, :]
             kernel = weights[jnp.bitwise_xor(step, 2 * half)]
-            for start, rows in chunks(3 * TILE - 2 * (step + 1), 2):
+            spare = 1 if turn == PLANES - 1 else 0
+            for start, rows in chunks(3 * TILE - 2 * (step + 1 + spare), 2):
+                start += spare
                 slope = jnp.tanh(convolve(wide, step % 2, kernel, start, rows) + bias)
                 for i in range(rows):
                     row = start + i + step + 1
@@ -336,9 +340,10 @@
         pick_kernel,
         name="pick",
         out_shape=shape(9 * C),
-        in_specs=[VMEM],
+        in_specs=[pl.BlockSpec(memory_space=pltpu.HBM)],
         out_specs=VMEM,
-        compiler_params=pltpu.CompilerParams(vmem_limit_bytes=8 * 2**20),
+        scratch_shapes=[pltpu.SemaphoreType.DMA(())],
+        compiler_params=pltpu.CompilerParams(vmem_limit_bytes=50 * 2**20),
     )(kernels)
 
     to_north = within_plane(lambda p, h, c: (device(p, h, 0, c), device(p, h, 1, c)))
@@ -359,7 +364,7 @@
     far_north = lax.ppermute(kernel, AXES, within_plane(from_next_pair))
     near_south = lax.ppermute(kernel, AXES, to_north)
 
-    messages = [shape((SENT - 2 * k) * COLS + EXTRA) for k in (0, 0, 1, 2, 3)]
+    messages = [shape((SENT - 2 * k) * COLS + EXTRA) for k in (0, 0, 1)]
     same, *others, relaxed = call(
         first_kernel,
         68,
@@ -368,17 +373,18 @@
         [SMEM] + [VMEM] * 5,
         (pltpu.VMEM((WIDE * COLS, C), F32),),
     )(step_sizes, above, initial, below, kernels, biases)
-    defects = []
-    for k in range(GROUP):
-        half, core = k // 2, k % 2
-        pairs = [
-            (device(p, half, core, c), device(p, 1 - half, 1, c))
-            for p in range(PLANES)
-            for c in range(8)
-        ]
-        defects.append(lax.ppermute(others[k], AXES, pairs))
-    same_south = lax.ppermute(same, AXES, to_north)
-    defects = [same_south, same, *defects]
+
+    def exchange(planes):
+        def send(message, link):
+            chosen = [pair for pair in link if pair[0] // device(1, 0, 0, 0) in planes]
+            return lax.ppermute(message, AXES, chosen)
+
+        other_south = send(others[0], to_other_north)
+        other_north = send(others[1], north_to_north)
+        return [send(same, to_north), same, other_south, other_north]
+
+    early = exchange(range(1))
+    late = exchange(range(1, PLANES))
     chain_kernels = jnp.stack([near_south, kernel, far_south, far_north])
 
     block = shape(TILE * COLS)
@@ -386,6 +392,7 @@
     for turn in range(PLANES):
         last = turn == PLANES - 1
         outs = (shape(2 * TILE * COLS), block, block) if last else (block,) * (GROUP + 1)
+        defects = late if turn else early
         operands = [*entering, *passed, *defects, chain_kernels]
         results = call(
             functools.partial(chain_kernel, turn),

time: 144 us -> 142 us (0.986)
  the two profiles are of different devices: /device:TPU:248 before, /device:TPU:232 now
where the time goes in v5:
time: 142 us; the launch traced here: 141 us
  waiting for transfers between devices  81.9 us (58%)
  starting transfers between devices  43.5 us (31%)
  Pallas kernels  13.7 us (10%)
    ppermute x1, waiting for transfers between devices, local(): arrived = lax.ppermute(to_south, AXES, [(b, a) for a, b in to_north])  58.2 us
    ppermute x1, waiting for transfers between devices, local(): above = lax.ppermute(to_below, 'coarse', downward)  15 us
    ppermute x21, starting transfers between devices, local(): entering.append(lax.ppermute(results[0], AXES, pairs))  14 us
    pallas_call x1, Pallas kernels, local(): call(first_kernel, 68, OWN + 2 * DEPTH, (*messages, shape(OWN * COLS, F32...  6.25 us
    ppermute x6, starting transfers between devices, send(): return lax.ppermute(message, AXES, chosen)  5.34 us
    pallas_call x1, Pallas kernels, local(): call(last_kernel, 44, OWN + 2 * LAYERS, (result, result), [SMEM] + [VMEM]...  5.01 us
    ppermute x1, starting transfers between devices, local(): halo_a = lax.ppermute(mine, AXES, halos(1))  5 us
    ppermute x1, waiting for transfers between devices, local(): halo_b = lax.ppermute(theirs, AXES, halos(0))  4.87 us
  transfers between devices with their start and end apart: 36, of which 5 were waited for; matrix products, arithmetic and copies ran while one was open for 0% of the time, Pallas kernels for 5%

profile of v5, /device:TPU:232, one launch (start us, length us, event | category | flops | bytes accessed | tf_op | source)
XLA Modules:
  0.0 141.0 jit_solution(432975551323240097)
XLA Ops:
  0.7 1.4 %pick.1 = bf16[2304,256]{1,0:T(8,128)(2,1)S(1)} custom-call(bf16[4,2304,256]{2,1,0:T(8,128)(2,1)} %bitcast.9), custom_call_target="tpu_custom_call" | custom-call | tf_op jit(solution)/shard_map/pick/pallas_call | solution.py:339
  2.1 1.9 %collective-permute-start.5 = (bf16[2304,256]{1,0:T(8,128)(2,1)S(1)}, bf16[2304,256]{1,0:T(8,128)(2,1)S(1)}, u32[]{:S(2)}, u32[]{:S(2)}) collective-permute-start(bf16[2304,256]{1,0:T(8,128)(2,1)S(1)} %pick.1), channel_id=1, source_target_pairs={{0,8},{1,9},{2,10},{3,11},{4,12},{5,13},{6,14},{7,15},{16,24},{17,... | collective-permute-start | bytes 3538952 | tf_op jit(solution)/shard_map/ppermute | solution.py:365
  4.1 2.4 %collective-permute-start.6 = (bf16[2304,256]{1,0:T(8,128)(2,1)S(1)}, bf16[2304,256]{1,0:T(8,128)(2,1)S(1)}, u32[]{:S(2)}, u32[]{:S(2)}) collective-permute-start(bf16[2304,256]{1,0:T(8,128)(2,1)S(1)} %pick.1), channel_id=1, source_target_pairs={{16,8},{17,9},{18,10},{19,11},{20,12},{21,13},{22,14},{23,15},{32,... | collective-permute-start | bytes 3538952 | tf_op jit(solution)/shard_map/ppermute | solution.py:363
  6.5 0.7 collective-permute-start.7
  7.3 4.6 %collective-permute-start = (bf16[448,256]{1,0:T(8,128)(2,1)S(1)}, bf16[448,256]{1,0:T(8,128)(2,1)S(1)}, u32[]{:S(2)}, u32[]{:S(2)}) collective-permute-start(bf16[448,256]{1,0:T(8,128)(2,1)S(1)} %get-tuple-element.50), channel_id=1, source_target_pairs={{0,1},{1,2},{2,3},{3,4},{4,5},{5,6},{6,7},{8,9},{9,10},{10,11},{11... | collective-permute-start | bytes 688136 | tf_op jit(solution)/shard_map/ppermute | solution.py:337
  11.9 3.6 %collective-permute-start.1 = (bf16[448,256]{1,0:T(8,128)(2,1)S(1)}, bf16[448,256]{1,0:T(8,128)(2,1)S(1)}, u32[]{:S(2)}, u32[]{:S(2)}) collective-permute-start(bf16[448,256]{1,0:T(8,128)(2,1)S(1)} %get-tuple-element.51), channel_id=1, source_target_pairs={{1,0},{2,1},{3,2},{4,3},{5,4},{6,5},{7,6},{9,8},{10,9},{11,10},{12... | collective-permute-start | bytes 688136 | tf_op jit(solution)/shard_map/ppermute | solution.py:338
  15.5 15.0 %collective-permute-done.up = bf16[448,256]{1,0:T(8,128)(2,1)S(1)} collective-permute-done((bf16[448,256]{1,0:T(8,128)(2,1)S(1)}, bf16[448,256]{1,0:T(8,128)(2,1)S(1)}, u32[]{:S(2)}, u32[]{:S(2)}) %collective-permute-start) | collective-permute-done | bytes 229408 | tf_op jit(solution)/shard_map/ppermute | solution.py:337
  30.5 2.6 %collective-permute-done.1.down = bf16[448,256]{1,0:T(8,128)(2,1)S(1)} collective-permute-done((bf16[448,256]{1,0:T(8,128)(2,1)S(1)}, bf16[448,256]{1,0:T(8,128)(2,1)S(1)}, u32[]{:S(2)}, u32[]{:S(2)}) %collective-permute-start.1) | collective-permute-done | bytes 229408 | tf_op jit(solution)/shard_map/ppermute | solution.py:338
  33.1 6.3 %shard_map.59 = (bf16[656,256]{1,0:T(8,128)(2,1)S(1)}, bf16[656,256]{1,0:T(8,128)(2,1)S(1)}, bf16[528,256]{1,0:T(8,128)(2,1)S(1)}, f32[512,256]{1,0:T(8,128)S(1)}) custom-call(f32[4]{0:T(128)S(1)} %copy-done.3, bf16[448,256]{1,0:T(8,128)(2,1)S(1)} %collective-permute-done.up, f32[512,256]{1,0:T(8,128)S(1)} %bitcast.13, ...), custom_call_target="tpu_custom_call" | custom-call | flops 5133828096 | bytes 10027008 | tf_op jit(solution)/shard_map/pallas_call | solution.py:368
  39.4 0.7 collective-permute-start.4
  40.1 0.7 collective-permute-start.2
  40.8 0.0 collective-permute-done.4.refs_3_
  40.8 1.3 collective-permute-start.11
  42.1 0.0 collective-permute-done.5
  42.1 0.7 collective-permute-start.3
  42.8 1.3 collective-permute-start.12
  44.1 0.0 collective-permute-done.7
  44.1 0.7 collective-permute-start.13
  44.8 0.6 pad_maximum_fusion.refs_4_.refs_11_
  45.5 0.0 collective-permute-done.2.refs_0_
  45.5 0.1 shard_map.60
  45.6 0.7 collective-permute-start.10
  46.2 0.7 collective-permute-start.8
  46.9 0.7 collective-permute-start.9
  47.6 0.0 collective-permute-done.11.refs_7_
  47.6 1.1 collective-permute-done.12.refs_9_
  48.8 0.0 collective-permute-done.9.refs_1_
  48.8 0.1 shard_map.61
  48.9 0.7 collective-permute-start.14
  49.5 0.7 collective-permute-start.15
  50.2 0.7 collective-permute-start.16
  50.9 0.0 collective-permute-done.14.refs_0_
  50.9 0.0 collective-permute-done.15.refs_1_
  50.9 0.3 shard_map.62
  51.2 0.7 collective-permute-start.17
  51.9 0.7 collective-permute-start.18
  52.5 0.7 collective-permute-start.19
  53.2 0.0 collective-permute-done.17.refs_0_
  53.2 0.1 shard_map.63
  53.3 0.7 collective-permute-start.20
  54.0 0.7 collective-permute-start.21
  54.7 0.7 collective-permute-start.22
  55.4 0.0 collective-permute-done.20.refs_0_
  55.4 0.0 collective-permute-done.21.refs_1_
  55.4 0.1 shard_map.64
  55.5 0.7 collective-permute-start.23
  56.1 0.7 collective-permute-start.24
  56.8 0.7 collective-permute-start.25
  57.5 0.1 shard_map.65
  57.6 0.7 collective-permute-start.26
  58.3 0.7 collective-permute-start.27
  59.0 0.7 collective-permute-start.28
  59.7 0.3 shard_map.66
  60.0 0.7 collective-permute-start.29
  60.6 0.7 collective-permute-start.30
  61.3 0.7 collective-permute-start.31
  62.0 0.1 shard_map.67
  62.1 1.3 collective-permute-start.32
  63.4 58.2 %collective-permute-done.32.arrived = bf16[512,256]{1,0:T(8,128)(2,1)S(1)} collective-permute-done((bf16[512,256]{1,0:T(8,128)(2,1)S(1)}, bf16[512,256]{1,0:T(8,128)(2,1)S(1)}, u32[]{:S(2)}, u32[]{:S(2)}) %collective-permute-start.32) | collective-permute-done | bytes 262176 | tf_op jit(solution)/shard_map/ppermute | solution.py:417
  121.6 0.2 collective-permute-start.33
  121.8 5.0 %collective-permute-start.34 = (bf16[256,256]{1,0:T(8,128)(2,1)S(1)}, bf16[256,256]{1,0:T(8,128)(2,1)S(1)}, u32[]{:S(2)}, u32[]{:S(2)}) collective-permute-start(bf16[256,256]{1,0:T(8,128)(2,1)S(1)} %get-tuple-element.94.mine), channel_id=1, source_target_pairs={{1,0},{16,17},{2,1},{17,18},{3,2},{18,19},{4,3},{19,20},{5,4},{20,... | collective-permute-start | bytes 393224 | tf_op jit(solution)/shard_map/ppermute | solution.py:440
  126.8 4.3 %collective-permute-start.35 = (bf16[256,256]{1,0:T(8,128)(2,1)S(1)}, bf16[256,256]{1,0:T(8,128)(2,1)S(1)}, u32[]{:S(2)}, u32[]{:S(2)}) collective-permute-start(bf16[256,256]{1,0:T(8,128)(2,1)S(1)} %get-tuple-element.95), channel_id=1, source_target_pairs={{1,16},{16,1},{2,17},{17,2},{3,18},{18,3},{4,19},{19,4},{5,20},{20... | collective-permute-start | bytes 393224 | tf_op jit(solution)/shard_map/ppermute | solution.py:441
  131.1 4.9 %collective-permute-done.35.halo_b = bf16[256,256]{1,0:T(8,128)(2,1)S(1)} collective-permute-done((bf16[256,256]{1,0:T(8,128)(2,1)S(1)}, bf16[256,256]{1,0:T(8,128)(2,1)S(1)}, u32[]{:S(2)}, u32[]{:S(2)}) %collective-permute-start.35) | collective-permute-done | bytes 131104 | tf_op jit(solution)/shard_map/ppermute | solution.py:441
  136.0 5.0 %shard_map.68 = (f32[512,256]{1,0:T(8,128)}, f32[512,256]{1,0:T(8,128)}) custom-call(f32[4]{0:T(128)S(1)} %copy-done.3, f32[512,256]{1,0:T(8,128)S(1)} %bitcast.14, f32[512,256]{1,0:T(8,128)S(1)} %get-tuple-element.52.relaxed, bf16[256,256]{1,0:T(8,128)(2,1)S(1)} %get-tuple-element.94.mine, bf16[256,256]{1,0:T(8,128)(2,1)S(1)} %collective-permute-done.33.across, ...), custom_call_target="tpu_custom_call" | custom-call | flops 3321888768 | bytes 6488064 | tf_op jit(solution)/shard_map/pallas_call | solution.py:451
  (30 shorter events, 0.1 us)
Async XLA Ops:
  0.6 32.5 %copy-start = (bf16[4,9,256,256]{3,2,1,0:T(8,128)(2,1)S(1)}, bf16[4,9,256,256]{3,2,1,0:T(8,128)(2,1)}, u32[]{:S(2)}) copy-start(bf16[4,9,256,256]{3,2,1,0:T(8,128)(2,1)} %param.5) | copy-start | bytes 14155780
  0.6 6.6 %copy-start.1 = (f32[1,1,8,64,256]{4,3,2,1,0:T(8,128)S(1)}, f32[1,1,8,64,256]{4,3,2,1,0:T(8,128)}, u32[]{:S(2)}) copy-start(f32[1,1,8,64,256]{4,3,2,1,0:T(8,128)} %param.4) | copy-start | bytes 1572868
  0.7 32.5 %copy-start.2 = (f32[4,256]{1,0:T(4,128)S(1)}, f32[4,256]{1,0:T(4,128)}, u32[]{:S(2)}) copy-start(f32[4,256]{1,0:T(4,128)} %biases.3) | copy-start | bytes 12292
  0.7 32.5 %copy-start.3 = (f32[4]{0:T(128)S(1)}, f32[4]{0:T(128)}, u32[]{:S(2)}) copy-start(f32[4]{0:T(128)} %steps.3) | copy-start | bytes 52
  2.1 40.0 %collective-permute-start.5 = (bf16[2304,256]{1,0:T(8,128)(2,1)S(1)}, bf16[2304,256]{1,0:T(8,128)(2,1)S(1)}, u32[]{:S(2)}, u32[]{:S(2)}) collective-permute-start(bf16[2304,256]{1,0:T(8,128)(2,1)S(1)} %pick.1), channel_id=1, source_target_pairs={{0,8},{1,9},{2,10},{3,11},{4,12},{5,13},{6,14},{7,15},{16,24},{17,... | collective-permute-start | bytes 3538952 | tf_op jit(solution)/shard_map/ppermute | solution.py:365
  4.1 38.7 %collective-permute-start.6 = (bf16[2304,256]{1,0:T(8,128)(2,1)S(1)}, bf16[2304,256]{1,0:T(8,128)(2,1)S(1)}, u32[]{:S(2)}, u32[]{:S(2)}) collective-permute-start(bf16[2304,256]{1,0:T(8,128)(2,1)S(1)} %pick.1), channel_id=1, source_target_pairs={{16,8},{17,9},{18,10},{19,11},{20,12},{21,13},{22,14},{23,15},{32,... | collective-permute-start | bytes 3538952 | tf_op jit(solution)/shard_map/ppermute | solution.py:363
  6.5 37.7 %collective-permute-start.7 = (bf16[2304,256]{1,0:T(8,128)(2,1)S(1)}, bf16[2304,256]{1,0:T(8,128)(2,1)S(1)}, u32[]{:S(2)}, u32[]{:S(2)}) collective-permute-start(bf16[2304,256]{1,0:T(8,128)(2,1)S(1)} %pick.1), channel_id=1, source_target_pairs={{25,8},{24,9},{27,10},{26,11},{29,12},{28,13},{31,14},{30,15},{9,2... | collective-permute-start | bytes 3538952 | tf_op jit(solution)/shard_map/ppermute | solution.py:364
  7.3 23.3 %collective-permute-start = (bf16[448,256]{1,0:T(8,128)(2,1)S(1)}, bf16[448,256]{1,0:T(8,128)(2,1)S(1)}, u32[]{:S(2)}, u32[]{:S(2)}) collective-permute-start(bf16[448,256]{1,0:T(8,128)(2,1)S(1)} %get-tuple-element.50), channel_id=1, source_target_pairs={{0,1},{1,2},{2,3},{3,4},{4,5},{5,6},{6,7},{8,9},{9,10},{10,11},{11... | collective-permute-start | bytes 688136 | tf_op jit(solution)/shard_map/ppermute | solution.py:337
  11.9 21.2 %collective-permute-start.1 = (bf16[448,256]{1,0:T(8,128)(2,1)S(1)}, bf16[448,256]{1,0:T(8,128)(2,1)S(1)}, u32[]{:S(2)}, u32[]{:S(2)}) collective-permute-start(bf16[448,256]{1,0:T(8,128)(2,1)S(1)} %get-tuple-element.51), channel_id=1, source_target_pairs={{1,0},{2,1},{3,2},{4,3},{5,4},{6,5},{7,6},{9,8},{10,9},{11,10},{12... | collective-permute-start | bytes 688136 | tf_op jit(solution)/shard_map/ppermute | solution.py:338
  39.4 1.4 collective-permute-start.4
  40.1 5.4 %collective-permute-start.2 = (bf16[656,256]{1,0:T(8,128)(2,1)S(1)}, bf16[656,256]{1,0:T(8,128)(2,1)S(1)}, u32[]{:S(2)}, u32[]{:S(2)}) collective-permute-start(bf16[656,256]{1,0:T(8,128)(2,1)S(1)} %get-tuple-element.53.refs_1_.refs_8_), channel_id=1, source_target_pairs={{0,8},{1,9},{2,10},{3,11},{4,12},{5,13},{6,14},{7,15},{16,24},{17,... | collective-permute-start | bytes 1007624 | tf_op jit(solution)/shard_map/ppermute | solution.py:380
  40.8 6.8 %collective-permute-start.11 = (bf16[656,256]{1,0:T(8,128)(2,1)S(1)}, bf16[656,256]{1,0:T(8,128)(2,1)S(1)}, u32[]{:S(2)}, u32[]{:S(2)}) collective-permute-start(bf16[656,256]{1,0:T(8,128)(2,1)S(1)} %get-tuple-element.53.refs_1_.refs_8_), channel_id=1, source_target_pairs={{32,40},{33,41},{34,42},{35,43},{36,44},{37,45},{38,46},{39,47},{4... | collective-permute-start | bytes 1007624 | tf_op jit(solution)/shard_map/ppermute | solution.py:380
  42.1 3.4 %collective-permute-start.3 = (bf16[656,256]{1,0:T(8,128)(2,1)S(1)}, bf16[656,256]{1,0:T(8,128)(2,1)S(1)}, u32[]{:S(2)}, u32[]{:S(2)}) collective-permute-start(bf16[656,256]{1,0:T(8,128)(2,1)S(1)} %get-tuple-element.54), channel_id=1, source_target_pairs={{0,24},{1,25},{2,26},{3,27},{4,28},{5,29},{6,30},{7,31},{16,8},{17... | collective-permute-start | bytes 1007624 | tf_op jit(solution)/shard_map/ppermute | solution.py:380
  42.8 6.0 %collective-permute-start.12 = (bf16[656,256]{1,0:T(8,128)(2,1)S(1)}, bf16[656,256]{1,0:T(8,128)(2,1)S(1)}, u32[]{:S(2)}, u32[]{:S(2)}) collective-permute-start(bf16[656,256]{1,0:T(8,128)(2,1)S(1)} %get-tuple-element.54), channel_id=1, source_target_pairs={{32,56},{33,57},{34,58},{35,59},{36,60},{37,61},{38,62},{39,63},{4... | collective-permute-start | bytes 1007624 | tf_op jit(solution)/shard_map/ppermute | solution.py:380
  44.1 2.8 %collective-permute-start.13 = (bf16[528,256]{1,0:T(8,128)(2,1)S(1)}, bf16[528,256]{1,0:T(8,128)(2,1)S(1)}, u32[]{:S(2)}, u32[]{:S(2)}) collective-permute-start(bf16[528,256]{1,0:T(8,128)(2,1)S(1)} %get-tuple-element.55), channel_id=1, source_target_pairs={{40,56},{41,57},{42,58},{43,59},{44,60},{45,61},{46,62},{47,63},{5... | collective-permute-start | bytes 811016 | tf_op jit(solution)/shard_map/ppermute | solution.py:380
  45.6 3.2 %collective-permute-start.10 = (bf16[256,256]{1,0:T(8,128)(2,1)S(1)}, bf16[256,256]{1,0:T(8,128)(2,1)S(1)}, u32[]{:S(2)}, u32[]{:S(2)}) collective-permute-start(bf16[256,256]{1,0:T(8,128)(2,1)S(1)} %get-tuple-element.56), channel_id=1, source_target_pairs={{24,40},{9,56},{25,41},{10,57},{26,42},{11,58},{27,43},{12,59},{28... | collective-permute-start | bytes 393224 | tf_op jit(solution)/shard_map/ppermute | solution.py:414
  46.2 2.5 %collective-permute-start.8 = (bf16[256,256]{1,0:T(8,128)(2,1)S(1)}, bf16[256,256]{1,0:T(8,128)(2,1)S(1)}, u32[]{:S(2)}, u32[]{:S(2)}) collective-permute-start(bf16[256,256]{1,0:T(8,128)(2,1)S(1)} %get-tuple-element.56), channel_id=1, source_target_pairs={{8,56},{24,41},{9,57},{25,42},{10,58},{26,43},{11,59},{27,44},{12,... | collective-permute-start | bytes 393224 | tf_op jit(solution)/shard_map/ppermute | solution.py:414
  46.9 1.8 %collective-permute-start.9 = (bf16[256,256]{1,0:T(8,128)(2,1)S(1)}, bf16[256,256]{1,0:T(8,128)(2,1)S(1)}, u32[]{:S(2)}, u32[]{:S(2)}) collective-permute-start(bf16[256,256]{1,0:T(8,128)(2,1)S(1)} %get-tuple-element.56), channel_id=1, source_target_pairs={{8,40},{24,56},{9,41},{25,57},{10,42},{26,58},{11,43},{27,59},{12,... | collective-permute-start | bytes 393224 | tf_op jit(solution)/shard_map/ppermute | solution.py:414
  48.9 2.0 %collective-permute-start.14 = (bf16[256,256]{1,0:T(8,128)(2,1)S(1)}, bf16[256,256]{1,0:T(8,128)(2,1)S(1)}, u32[]{:S(2)}, u32[]{:S(2)}) collective-permute-start(bf16[256,256]{1,0:T(8,128)(2,1)S(1)} %get-tuple-element.61), channel_id=1, source_target_pairs={{40,88},{56,73},{41,89},{57,74},{42,90},{58,75},{43,91},{59,76},{4... | collective-permute-start | bytes 393224 | tf_op jit(solution)/shard_map/ppermute | solution.py:414
  49.5 1.4 collective-permute-start.15
  50.2 0.7 collective-permute-start.16
  51.2 2.0 %collective-permute-start.17 = (bf16[256,256]{1,0:T(8,128)(2,1)S(1)}, bf16[256,256]{1,0:T(8,128)(2,1)S(1)}, u32[]{:S(2)}, u32[]{:S(2)}) collective-permute-start(bf16[256,256]{1,0:T(8,128)(2,1)S(1)} %get-tuple-element.66), channel_id=1, source_target_pairs={{72,120},{88,105},{73,121},{89,106},{74,122},{90,107},{75,123},{91... | collective-permute-start | bytes 393224 | tf_op jit(solution)/shard_map/ppermute | solution.py:414
  51.9 1.4 collective-permute-start.18
  52.5 0.7 collective-permute-start.19
  53.3 2.0 %collective-permute-start.20 = (bf16[256,256]{1,0:T(8,128)(2,1)S(1)}, bf16[256,256]{1,0:T(8,128)(2,1)S(1)}, u32[]{:S(2)}, u32[]{:S(2)}) collective-permute-start(bf16[256,256]{1,0:T(8,128)(2,1)S(1)} %get-tuple-element.71), channel_id=1, source_target_pairs={{104,152},{120,137},{105,153},{121,138},{106,154},{122,139},{107,1... | collective-permute-start | bytes 393224 | tf_op jit(solution)/shard_map/ppermute | solution.py:414
  54.0 1.4 collective-permute-start.21
  54.7 0.7 collective-permute-start.22
  55.5 2.0 %collective-permute-start.23 = (bf16[256,256]{1,0:T(8,128)(2,1)S(1)}, bf16[256,256]{1,0:T(8,128)(2,1)S(1)}, u32[]{:S(2)}, u32[]{:S(2)}) collective-permute-start(bf16[256,256]{1,0:T(8,128)(2,1)S(1)} %get-tuple-element.76), channel_id=1, source_target_pairs={{136,184},{152,169},{137,185},{153,170},{138,186},{154,171},{139,1... | collective-permute-start | bytes 393224 | tf_op jit(solution)/shard_map/ppermute | solution.py:414
  56.1 1.4 collective-permute-start.24
  56.8 0.7 collective-permute-start.25
  57.6 2.0 %collective-permute-start.26 = (bf16[256,256]{1,0:T(8,128)(2,1)S(1)}, bf16[256,256]{1,0:T(8,128)(2,1)S(1)}, u32[]{:S(2)}, u32[]{:S(2)}) collective-permute-start(bf16[256,256]{1,0:T(8,128)(2,1)S(1)} %get-tuple-element.81), channel_id=1, source_target_pairs={{168,216},{184,201},{169,217},{185,202},{170,218},{186,203},{171,2... | collective-permute-start | bytes 393224 | tf_op jit(solution)/shard_map/ppermute | solution.py:414
  58.3 1.4 collective-permute-start.27
  59.0 0.7 collective-permute-start.28
  60.0 2.0 %collective-permute-start.29 = (bf16[256,256]{1,0:T(8,128)(2,1)S(1)}, bf16[256,256]{1,0:T(8,128)(2,1)S(1)}, u32[]{:S(2)}, u32[]{:S(2)}) collective-permute-start(bf16[256,256]{1,0:T(8,128)(2,1)S(1)} %get-tuple-element.86), channel_id=1, source_target_pairs={{200,248},{216,233},{201,249},{217,234},{202,250},{218,235},{203,2... | collective-permute-start | bytes 393224 | tf_op jit(solution)/shard_map/ppermute | solution.py:414
  60.6 1.4 collective-permute-start.30
  61.3 0.7 collective-permute-start.31
  62.1 59.5 %collective-permute-start.32 = (bf16[512,256]{1,0:T(8,128)(2,1)S(1)}, bf16[512,256]{1,0:T(8,128)(2,1)S(1)}, u32[]{:S(2)}, u32[]{:S(2)}) collective-permute-start(bf16[512,256]{1,0:T(8,128)(2,1)S(1)} %get-tuple-element.93), channel_id=1, source_target_pairs={{8,0},{9,1},{10,2},{11,3},{12,4},{13,5},{14,6},{15,7},{24,16},{25,... | collective-permute-start | bytes 786440 | tf_op jit(solution)/shard_map/ppermute | solution.py:417
  121.6 9.5 %collective-permute-start.33 = (bf16[256,256]{1,0:T(8,128)(2,1)S(1)}, bf16[256,256]{1,0:T(8,128)(2,1)S(1)}, u32[]{:S(2)}, u32[]{:S(2)}) collective-permute-start(bf16[256,256]{1,0:T(8,128)(2,1)S(1)} %get-tuple-element.95), channel_id=1, source_target_pairs={{0,16},{1,17},{2,18},{3,19},{4,20},{5,21},{6,22},{7,23},{8,24},{9,... | collective-permute-start | bytes 393224 | tf_op jit(solution)/shard_map/ppermute | solution.py:449
  121.8 9.3 %collective-permute-start.34 = (bf16[256,256]{1,0:T(8,128)(2,1)S(1)}, bf16[256,256]{1,0:T(8,128)(2,1)S(1)}, u32[]{:S(2)}, u32[]{:S(2)}) collective-permute-start(bf16[256,256]{1,0:T(8,128)(2,1)S(1)} %get-tuple-element.94.mine), channel_id=1, source_target_pairs={{1,0},{16,17},{2,1},{17,18},{3,2},{18,19},{4,3},{19,20},{5,4},{20,... | collective-permute-start | bytes 393224 | tf_op jit(solution)/shard_map/ppermute | solution.py:440
  126.8 9.2 %collective-permute-start.35 = (bf16[256,256]{1,0:T(8,128)(2,1)S(1)}, bf16[256,256]{1,0:T(8,128)(2,1)S(1)}, u32[]{:S(2)}, u32[]{:S(2)}) collective-permute-start(bf16[256,256]{1,0:T(8,128)(2,1)S(1)} %get-tuple-element.95), channel_id=1, source_target_pairs={{1,16},{16,1},{2,17},{17,2},{3,18},{18,3},{4,19},{19,4},{5,20},{20... | collective-permute-start | bytes 393224 | tf_op jit(solution)/shard_map/ppermute | solution.py:441
